TPU v7x, 32 devices: a whole 2x2x4 slice. The times are simulated.
32 devices in a mesh: groups: 2 (over y), row: 4 (over z), col: 4 (over x, core).
Axes of the slice: x: 2, y: 2, z: 4, core: 2. Of those that a mesh axis runs over, the one named last changes fastest.
Arguments:
- positions: float32 [2, 8, 4, 512], P(None, ('groups', 'row'), 'col'), parts along dimension 1, may hold values from 0 to 1
- genes: int32 [8, 4, 512], P(('groups', 'row'), 'col'), parts along dimension 0, may hold values from 0 to 479
- candidates: int32 [8, 4, 512, 128], P(('groups', 'row'), 'col'), parts along dimension 0, may hold values from 0 to 1151, as said below
- block_counts: int32 [8, 4, 2], P(('groups', 'row'), 'col'), parts along dimension 0, may hold values from 0 to 256, as said below
- profile_weights: float32 [480, 8, 4, 128], P(None, ('groups', 'row'), 'col'), parts along dimension 1, may hold values from 0.05 to 5
- centroids: float32 [2, 8, 4, 128], P(None, ('groups', 'row'), 'col'), parts along dimension 1, may hold values from 0 to 1
- spreads: float32 [2, 8, 4, 128], P(None, ('groups', 'row'), 'col'), parts along dimension 1, may hold values from 0.05 to 0.4
- correlation: float32 [8, 4, 128], P(('groups', 'row'), 'col'), parts along dimension 0, may hold values from -0.6 to 0.6
Outputs:
- final_profile: float32 [480, 8, 4, 128], P(None, ('groups', 'row'), 'col'), parts along dimension 1
- final_cells: float32 [6, 8, 4, 128], P(None, ('groups', 'row'), 'col'), parts along dimension 1
There are 2 independent parts, one for each index of `groups`. A program takes and returns all parts, laid end to end along the dimension named above; each array names one. Nothing has to cross between parts.
Inputs may be any that keep to these rules, and one draw needn't show every extreme that they name: `candidates`: every candidate names a cell of the transcript's own tile or of one of the eight tiles around it that lie in the slab; an id may appear more than once in one list. `block_counts`: in each tile the blocks with a nonzero count come first, and the first block of every tile is full.
All inputs are finite; a program needn't handle non-finite values.
Results may differ from a plain program's by a relative error of at most 0.0003.
Values sent between devices are 32-bit elements; how exact they have to be, the bound alone decides.
No kernel may reach another device: no remote copies, remote signals or barrier semaphores. Data moves between devices by JAX's collectives and lax.ppermute only.
A program may use at most 64 MiB of HBM per device.

v0:
```python
import jax
import jax.numpy as jnp
from jax import lax
from jax.sharding import PartitionSpec as P

BLOCK = 256
ITERS = 2


pseudo_count = 0.05
prior_weight = 1.0


def shifted(x, axis, by):
    count = lax.axis_size(axis)
    pairs = [(i, i + by) for i in range(count) if 0 <= i + by < count]
    return lax.ppermute(x, axis, pairs)


def padded(x, sides, width):
    for axis, dim in sides:
        count, length = (lax.axis_size(axis), x.shape[dim])
        up = [(i, (i + 1) % count) for i in range(count - 1)]
        down = [(j, i) for i, j in up]
        last = lax.slice_in_dim(x, length - width, length, axis=dim)
        first = lax.slice_in_dim(x, 0, width, axis=dim)
        before = lax.ppermute(last, axis, up)
        after = lax.ppermute(first, axis, down)
        x = jnp.concatenate([before, x, after], axis=dim)
    return x


def update_cells(gene_counts, moments, centre_row, centre_col, cov_rr, cov_rc, cov_cc):
    weight_sum, sum_row, sum_col, sum_rr, sum_rc, sum_cc = moments
    gene_total = gene_counts.shape[0]
    profile = (gene_counts + pseudo_count) / (
        jnp.sum(gene_counts, axis=0) + gene_total * pseudo_count
    )
    new_row = (sum_row + prior_weight * centre_row) / (weight_sum + prior_weight)
    new_col = (sum_col + prior_weight * centre_col) / (weight_sum + prior_weight)
    scatter_rr = sum_rr - 2.0 * new_row * sum_row + weight_sum * new_row * new_row
    scatter_rc = sum_rc - new_row * sum_col - new_col * sum_row + weight_sum * new_row * new_col
    scatter_cc = sum_cc - 2.0 * new_col * sum_col + weight_sum * new_col * new_col
    denominator = weight_sum + prior_weight
    return (
        profile,
        new_row,
        new_col,
        (scatter_rr + prior_weight * cov_rr) / denominator,
        (scatter_rc + prior_weight * cov_rc) / denominator,
        (scatter_cc + prior_weight * cov_cc) / denominator,
        jnp.log(weight_sum + 1.0),
    )


def return_sums(partial_value):
    column_sums = partial_value[:, :, 1]
    for across in (0, 2):
        column_sums = column_sums + shifted(partial_value[:, :, across], "col", across - 1)
    owned_sums = column_sums[:, 1]
    for across in (0, 2):
        owned_sums = owned_sums + shifted(column_sums[:, across], "row", across - 1)
    return owned_sums


def body(
    positions, genes, candidates, block_counts, profile_weights, centroids, spreads, correlation
):
    gene_total = profile_weights.shape[0]
    tile_cells = profile_weights.shape[3]
    near_width = 9 * tile_cells
    pos_row = positions[0, 0, 0]
    pos_col = positions[1, 0, 0]
    gene_ids = genes[0, 0]
    neighbour_ids = candidates[0, 0]
    live_counts = block_counts[0, 0]
    slot_of = jnp.arange(near_width, dtype=jnp.int32) // tile_cells
    offset_row = (slot_of // 3 - 1).astype(jnp.float32)
    offset_col = (slot_of % 3 - 1).astype(jnp.float32)
    profile = (profile_weights / jnp.sum(profile_weights, axis=0, keepdims=True))[:, 0, 0]
    centre_row = centroids[0, 0, 0]
    centre_col = centroids[1, 0, 0]
    spread_row = spreads[0, 0, 0]
    spread_col = spreads[1, 0, 0]
    cov_rr = spread_row * spread_row
    cov_cc = spread_col * spread_col
    cov_rc = correlation[0, 0] * spread_row * spread_col
    log_weight = jnp.zeros((tile_cells,), jnp.float32)
    block_rows = jnp.arange(BLOCK, dtype=jnp.int32)
    gene_axis = jnp.arange(gene_total, dtype=jnp.int32)
    slot_range = jnp.arange(9, dtype=jnp.int32)
    cell_range = jnp.arange(tile_cells, dtype=jnp.int32)
    for iteration in range(ITERS):
        determinant = cov_rr * cov_cc - cov_rc * cov_rc
        cell_state = jnp.concatenate(
            [
                jnp.log(profile),
                jnp.stack(
                    [
                        centre_row,
                        centre_col,
                        cov_cc / determinant,
                        -cov_rc / determinant,
                        cov_rr / determinant,
                        log_weight - 0.5 * jnp.log(determinant),
                    ]
                ),
            ],
            axis=0,
        )
        nearby = padded(cell_state[:, None, None, :], (("row", 1), ("col", 2)), 1).reshape(
            gene_total + 6, near_width
        )
        log_table = nearby[:gene_total]
        near_row = nearby[gene_total] + offset_row
        near_col = nearby[gene_total + 1] + offset_col
        near_rr = nearby[gene_total + 2]
        near_rc = nearby[gene_total + 3]
        near_cc = nearby[gene_total + 4]
        near_bias = nearby[gene_total + 5]

        def one_block(block_index, accum):
            count_acc, moment_acc = accum
            row_start = block_index * BLOCK
            block_genes = lax.dynamic_slice_in_dim(gene_ids, row_start, BLOCK)
            block_row = lax.dynamic_slice_in_dim(pos_row, row_start, BLOCK)
            block_col = lax.dynamic_slice_in_dim(pos_col, row_start, BLOCK)
            block_cand = lax.dynamic_slice_in_dim(neighbour_ids, row_start, BLOCK, 0)
            valid_rows = (block_rows < live_counts[block_index]).astype(jnp.float32)
            gene_hot = (block_genes[:, None] == gene_axis[None, :]).astype(jnp.float32)
            gene_logs = jnp.dot(gene_hot, log_table, precision=lax.Precision.HIGHEST)
            delta_row = block_row[:, None] - near_row[None, :]
            delta_col = block_col[:, None] - near_col[None, :]
            score = (
                gene_logs
                + near_bias
                - 0.5
                * (
                    near_rr * delta_row * delta_row
                    + 2.0 * near_rc * delta_row * delta_col
                    + near_cc * delta_col * delta_col
                )
            )
            cand_slot = block_cand // tile_cells
            cand_within = block_cand % tile_cells
            slot_hot = (cand_slot[:, None, :] == slot_range[None, :, None]).astype(jnp.bfloat16)
            cell_hot = (cand_within[:, :, None] == cell_range[None, None, :]).astype(jnp.bfloat16)
            multiple = jnp.einsum(
                "tas,tsk->tak", slot_hot, cell_hot, preferred_element_type=jnp.float32
            ).reshape(BLOCK, near_width)
            picked = multiple > 0
            row_max = jnp.max(jnp.where(picked, score, -jnp.inf), axis=1, keepdims=True)
            exp_terms = multiple * jnp.exp(jnp.where(picked, score - row_max, -jnp.inf))
            posterior = exp_terms / jnp.sum(exp_terms, axis=1, keepdims=True) * valid_rows[:, None]
            onehot = gene_hot.astype(jnp.bfloat16)
            count_acc = count_acc + lax.dot_general(
                onehot,
                posterior.astype(jnp.bfloat16),
                (((0,), (0,)), ((), ())),
                preferred_element_type=jnp.float32,
            )
            features = jnp.stack(
                [
                    jnp.ones_like(block_row),
                    block_row,
                    block_col,
                    block_row * block_row,
                    block_row * block_col,
                    block_col * block_col,
                ]
            )
            moment_acc = moment_acc + jnp.dot(features, posterior, precision=lax.Precision.HIGHEST)
            return (count_acc, moment_acc)

        turns = live_counts.shape[0]
        start_acc = (
            jnp.zeros((gene_total, near_width), jnp.float32),
            jnp.zeros((6, near_width), jnp.float32),
        )
        count_acc, moment_acc = lax.fori_loop(0, turns, one_block, start_acc)
        weight_sum = moment_acc[0]
        sum_row = moment_acc[1] - offset_row * weight_sum
        sum_col = moment_acc[2] - offset_col * weight_sum
        sum_rr = (
            moment_acc[3] - 2.0 * offset_row * moment_acc[1] + offset_row * offset_row * weight_sum
        )
        sum_rc = (
            moment_acc[4]
            - offset_row * moment_acc[2]
            - offset_col * moment_acc[1]
            + offset_row * offset_col * weight_sum
        )
        sum_cc = (
            moment_acc[5] - 2.0 * offset_col * moment_acc[2] + offset_col * offset_col * weight_sum
        )
        partial_value = jnp.concatenate(
            [count_acc, jnp.stack([weight_sum, sum_row, sum_col, sum_rr, sum_rc, sum_cc])], axis=0
        ).reshape(gene_total + 6, 3, 3, tile_cells)
        owned_sums = return_sums(partial_value)
        moments = tuple((owned_sums[gene_total + member] for member in range(6)))
        profile, centre_row, centre_col, cov_rr, cov_rc, cov_cc, log_weight = update_cells(
            owned_sums[:gene_total], moments, centre_row, centre_col, cov_rr, cov_rc, cov_cc
        )
    final_cells = jnp.stack(
        [
            centre_row,
            centre_col,
            0.5 * jnp.log(cov_rr),
            0.5 * jnp.log(cov_cc),
            cov_rc / jnp.sqrt(cov_rr * cov_cc),
            log_weight,
        ]
    )
    return (jnp.log(profile)[:, None, None, :], final_cells[:, None, None, :])


def solution(mesh):
    return jax.shard_map(
        body,
        mesh=mesh,
        in_specs=(
            P(None, ("groups", "row"), "col", None),
            P(("groups", "row"), "col", None),
            P(("groups", "row"), "col", None, None),
            P(("groups", "row"), "col", None),
            P(None, ("groups", "row"), "col", None),
            P(None, ("groups", "row"), "col", None),
            P(None, ("groups", "row"), "col", None),
            P(("groups", "row"), "col", None),
        ),
        out_specs=(
            P(None, ("groups", "row"), "col", None),
            P(None, ("groups", "row"), "col", None),
        ),
        check_vma=False,
    )
```

profile of v0, /device:TPU:14, one launch (start us, length us, event | category | flops | bytes accessed | tf_op | source)
XLA Modules:
  0.0 232.1 jit_solution(2639746537659281810)
XLA Ops:
  5.4 3.5 %collective-permute-start = (f32[486,1,1,128]{3,2,1,0:T(1,128)S(1)}, f32[486,1,1,128]{3,2,1,0:T(1,128)S(1)}, u32[]{:S(2)}, u32[]{:S(2)}) collective-permute-start(f32[486,1,1,128]{3,2,1,0:T(1,128)S(1)} %broadcast_in_dim.126), channel_id=1, source_target_pairs={{0,4},{4,8},{8,12},{1,5},{5,9},{9,13},{2,6},{6,10},{10,14},{3,7},{... | collective-permute-start | bytes 746504 | tf_op jit(solution)/shard_map/ppermute | solution.py:27
  8.9 2.4 %collective-permute-start.1 = (f32[486,1,1,128]{3,2,1,0:T(1,128)S(1)}, f32[486,1,1,128]{3,2,1,0:T(1,128)S(1)}, u32[]{:S(2)}, u32[]{:S(2)}) collective-permute-start(f32[486,1,1,128]{3,2,1,0:T(1,128)S(1)} %broadcast_in_dim.126), channel_id=1, source_target_pairs={{4,0},{8,4},{12,8},{5,1},{9,5},{13,9},{6,2},{10,6},{14,10},{7,3},{... | collective-permute-start | bytes 746504 | tf_op jit(solution)/shard_map/ppermute | solution.py:28
  11.3 3.8 %collective-permute-done = f32[486,1,1,128]{3,2,1,0:T(1,128)S(1)} collective-permute-done((f32[486,1,1,128]{3,2,1,0:T(1,128)S(1)}, f32[486,1,1,128]{3,2,1,0:T(1,128)S(1)}, u32[]{:S(2)}, u32[]{:S(2)}) %collective-permute-start) | collective-permute-done | bytes 248864 | tf_op jit(solution)/shard_map/ppermute | solution.py:27
  15.6 2.7 %collective-permute-done.1 = f32[486,1,1,128]{3,2,1,0:T(1,128)S(1)} collective-permute-done((f32[486,1,1,128]{3,2,1,0:T(1,128)S(1)}, f32[486,1,1,128]{3,2,1,0:T(1,128)S(1)}, u32[]{:S(2)}, u32[]{:S(2)}) %collective-permute-start.1) | collective-permute-done | bytes 248864 | tf_op jit(solution)/shard_map/ppermute | solution.py:28
  20.4 3.6 %collective-permute-start.3 = (f32[486,3,1,128]{3,2,1,0:T(1,128)S(1)}, f32[486,3,1,128]{3,2,1,0:T(1,128)S(1)}, u32[]{:S(2)}, u32[]{:S(2)}) collective-permute-start(f32[486,3,1,128]{3,2,1,0:T(1,128)S(1)} %constant_dynamic-update-slice_fusion), channel_id=1, source_target_pairs={{1,0},{2,1},{3,2},{5,4},{6,5},{7,6},{9,8},{10,9},{11,10},{13,12},{... | collective-permute-start | bytes 2239496 | tf_op jit(solution)/shard_map/ppermute | solution.py:28
  24.1 7.3 %collective-permute-done.2 = f32[486,3,1,128]{3,2,1,0:T(1,128)S(1)} collective-permute-done((f32[486,3,1,128]{3,2,1,0:T(1,128)S(1)}, f32[486,3,1,128]{3,2,1,0:T(1,128)S(1)}, u32[]{:S(2)}, u32[]{:S(2)}) %collective-permute-start.2) | collective-permute-done | bytes 746528 | tf_op jit(solution)/shard_map/ppermute | solution.py:27
  35.6 2.7 %copy.81 = f32[480,3,3,128]{0,3,2,1:T(8,128)} copy(f32[480,3,3,128]{3,2,1,0:T(4,128)S(1)} %slice.278) | data formatting | bytes 4423680 | tf_op jit(solution)/shard_map/slice | solution.py:114
  38.3 3.0 %copy.82 = f32[480,1152]{1,0:T(8,128)} copy(f32[480,1152]{0,1:T(8,128)} %bitcast.165) | data formatting | bytes 4423680
  41.4 39.9 %while.36 = (s32[]{:T(128)}, f32[480,1152]{1,0:T(8,128)}, f32[6,1152]{1,0:T(8,128)S(1)}, s32[512]{0:T(512)S(1)}, s32[512,128]{1,0:T(8,128)S(1)}, /*index=5*/f32[...) while((s32[]{:T(128)}, f32[480,1152]{1,0:T(8,128)}, ...), condition=%wide.region_4.5_spmd.clone, body=%wide.region_1.4_spmd.clone.sunk | while | flops 2093718912 | bytes 24165672 | solution.py:180
  41.6 8.1 %fusion.139 = f32[256,9,128]{2,1,0:T(8,128)} fusion(s32[256,128]{1,0:T(8,128)S(1)} %add_select_fusion.12, s32[256,128]{1,0:T(8,128)S(1)} %get-tuple-element.1426), kind=kOutput, calls=%fused_computation.9.clone.1 | convolution fusion | flops 79986688 | bytes 1441792 | tf_op jit(solution)/shard_map/while/body/eval_jaxpr/tas,tsk->tak/dot_general | solution.py:148
  52.2 3.5 %select_reduce_fusion.4 = (f32[256]{0:T(256)S(1)}, f32[256,1152]{1,0:T(8,128)S(1)}) fusion(f32[256,1152]{1,0:T(8,128)S(1)} %copy.112, f32[1152]{0:T(1024)S(1)} %reduce.43, f32[1152]{0:T(1024)S(1)} %get-tuple-element.1510, f32[256]{0:T(256)S(1)} %get-tuple-element.1427, f32[1152]{0:T(1024)S(1)} %broadcast_multiply_fusion.4, ...), kind=kOutput, calls=%fused_computation.27.clone.1 | convolution fusion | flops 1703534336 | bytes 4602880 | tf_op jit(solution)/shard_map/while/body/eval_jaxpr/dot_general | solution.py:131
  57.8 2.0 convolution_add_fusion.10
  60.7 8.1 %fusion.139 = f32[256,9,128]{2,1,0:T(8,128)} fusion(s32[256,128]{1,0:T(8,128)S(1)} %add_select_fusion.12, s32[256,128]{1,0:T(8,128)S(1)} %get-tuple-element.1426), kind=kOutput, calls=%fused_computation.9.clone.1 | convolution fusion | flops 79986688 | bytes 1441792 | tf_op jit(solution)/shard_map/while/body/eval_jaxpr/tas,tsk->tak/dot_general | solution.py:148
  71.3 3.5 %select_reduce_fusion.4 = (f32[256]{0:T(256)S(1)}, f32[256,1152]{1,0:T(8,128)S(1)}) fusion(f32[256,1152]{1,0:T(8,128)S(1)} %copy.112, f32[1152]{0:T(1024)S(1)} %reduce.43, f32[1152]{0:T(1024)S(1)} %get-tuple-element.1510, f32[256]{0:T(256)S(1)} %get-tuple-element.1427, f32[1152]{0:T(1024)S(1)} %broadcast_multiply_fusion.4, ...), kind=kOutput, calls=%fused_computation.27.clone.1 | convolution fusion | flops 1703534336 | bytes 4602880 | tf_op jit(solution)/shard_map/while/body/eval_jaxpr/dot_general | solution.py:131
  76.9 3.7 %convolution_add_fusion.10 = f32[480,1152]{1,0:T(8,128)} fusion(f32[480,1152]{1,0:T(8,128)} %get-tuple-element.1478, pred[]{:T(512)S(6)} %compare.50, f32[256,1152]{1,0:T(8,128)S(1)} %divide_multiply_fusion.4, s32[256]{0:T(256)S(1)} %dynamic_slice.163), kind=kOutput, calls=%fused_computation.11.clone.1 | convolution fusion | flops 284884992 | bytes 5604353 | tf_op jit(solution)/shard_map/while/body/eval_jaxpr/dot_general | solution.py:156
  81.3 2.0 copy.83
  85.5 5.0 %concatenate.64 = f32[486,3,3,128]{3,0,1,2:T(8,128)S(1)} concatenate(f32[480,3,3,128]{3,0,1,2:T(8,128)} %copy.84, f32[1,3,3,128]{3,0,1,2:T(1,128)S(1)} %copy.85, f32[1,3,3,128]{3,0,1,2:T(1,128)S(1)} %copy.86, f32[1,3,3,128]{3,0,1,2:T(1,128)S(1)} %copy.87, f32[1,3,3,128]{3,0,1,2:T(1,128)S(1)} %copy.88, f32[1,3,3,128]{3,0,1,2:T(1,128)S(1)} %copy.89, f32[1,3,3,128]{3,0,1,2:T(1,128)S(1)} %copy.90), dimensions={0} | concatenate | bytes 4478976 | tf_op jit(solution)/shard_map/concatenate | solution.py:196
  90.7 3.8 %collective-permute-start.4 = (f32[486,3,128]{2,0,1:T(8,128)S(1)}, f32[486,3,128]{2,0,1:T(8,128)S(1)}, u32[]{:S(2)}, u32[]{:S(2)}) collective-permute-start(f32[486,3,128]{2,0,1:T(8,128)S(1)} %get-tuple-element.1217), channel_id=1, source_target_pairs={{1,0},{2,1},{3,2},{5,4},{6,5},{7,6},{9,8},{10,9},{11,10},{13,12},{... | collective-permute-start | bytes 2239496 | tf_op jit(solution)/shard_map/ppermute | solution.py:17
  96.4 7.2 %collective-permute-done.4 = f32[486,3,128]{2,0,1:T(8,128)S(1)} collective-permute-done((f32[486,3,128]{2,0,1:T(8,128)S(1)}, f32[486,3,128]{2,0,1:T(8,128)S(1)}, u32[]{:S(2)}, u32[]{:S(2)}) %collective-permute-start.4) | collective-permute-done | bytes 746528 | tf_op jit(solution)/shard_map/ppermute | solution.py:17
  103.6 3.8 %collective-permute-done.5 = f32[486,3,128]{2,0,1:T(8,128)S(1)} collective-permute-done((f32[486,3,128]{2,0,1:T(8,128)S(1)}, f32[486,3,128]{2,0,1:T(8,128)S(1)}, u32[]{:S(2)}, u32[]{:S(2)}) %collective-permute-start.5) | collective-permute-done | bytes 746528 | tf_op jit(solution)/shard_map/ppermute | solution.py:17
  107.6 2.5 %collective-permute-start.6 = (f32[486,128]{1,0:T(8,128)S(1)}, f32[486,128]{1,0:T(8,128)S(1)}, u32[]{:S(2)}, u32[]{:S(2)}) collective-permute-start(f32[486,128]{1,0:T(8,128)S(1)} %get-tuple-element.1227), channel_id=1, source_target_pairs={{4,0},{8,4},{12,8},{5,1},{9,5},{13,9},{6,2},{10,6},{14,10},{7,3},{... | collective-permute-start | bytes 746504 | tf_op jit(solution)/shard_map/ppermute | solution.py:17
  110.2 3.5 %collective-permute-start.7 = (f32[486,128]{1,0:T(8,128)S(1)}, f32[486,128]{1,0:T(8,128)S(1)}, u32[]{:S(2)}, u32[]{:S(2)}) collective-permute-start(f32[486,128]{1,0:T(8,128)S(1)} %get-tuple-element.1228), channel_id=1, source_target_pairs={{0,4},{4,8},{8,12},{1,5},{5,9},{9,13},{2,6},{6,10},{10,14},{3,7},{... | collective-permute-start | bytes 746504 | tf_op jit(solution)/shard_map/ppermute | solution.py:17
  113.7 2.1 collective-permute-done.6
  115.8 2.6 %collective-permute-done.7 = f32[486,128]{1,0:T(8,128)S(1)} collective-permute-done((f32[486,128]{1,0:T(8,128)S(1)}, f32[486,128]{1,0:T(8,128)S(1)}, u32[]{:S(2)}, u32[]{:S(2)}) %collective-permute-start.7) | collective-permute-done | bytes 248864 | tf_op jit(solution)/shard_map/ppermute | solution.py:17
  118.7 3.5 %collective-permute-start.8 = (f32[486,1,1,128]{3,0,2,1:T(8,128)S(1)}, f32[486,1,1,128]{3,0,2,1:T(8,128)S(1)}, u32[]{:S(2)}, u32[]{:S(2)}) collective-permute-start(f32[486,1,1,128]{3,0,2,1:T(8,128)S(1)} %bitcast.166), channel_id=1, source_target_pairs={{0,4},{4,8},{8,12},{1,5},{5,9},{9,13},{2,6},{6,10},{10,14},{3,7},{... | collective-permute-start | bytes 746504 | tf_op jit(solution)/shard_map/ppermute | solution.py:27
  122.1 2.4 %collective-permute-start.9 = (f32[486,1,1,128]{3,0,2,1:T(8,128)S(1)}, f32[486,1,1,128]{3,0,2,1:T(8,128)S(1)}, u32[]{:S(2)}, u32[]{:S(2)}) collective-permute-start(f32[486,1,1,128]{3,0,2,1:T(8,128)S(1)} %bitcast.167), channel_id=1, source_target_pairs={{4,0},{8,4},{12,8},{5,1},{9,5},{13,9},{6,2},{10,6},{14,10},{7,3},{... | collective-permute-start | bytes 746504 | tf_op jit(solution)/shard_map/ppermute | solution.py:28
  124.5 2.3 collective-permute-done.8
  126.8 3.5 %collective-permute-done.9 = f32[486,1,1,128]{3,0,2,1:T(8,128)S(1)} collective-permute-done((f32[486,1,1,128]{3,0,2,1:T(8,128)S(1)}, f32[486,1,1,128]{3,0,2,1:T(8,128)S(1)}, u32[]{:S(2)}, u32[]{:S(2)}) %collective-permute-start.9) | collective-permute-done | bytes 248864 | tf_op jit(solution)/shard_map/ppermute | solution.py:28
  133.1 3.6 %collective-permute-start.11 = (f32[486,3,1,128]{3,2,1,0:T(1,128)S(1)}, f32[486,3,1,128]{3,2,1,0:T(1,128)S(1)}, u32[]{:S(2)}, u32[]{:S(2)}) collective-permute-start(f32[486,3,1,128]{3,2,1,0:T(1,128)S(1)} %copy.91), channel_id=1, source_target_pairs={{1,0},{2,1},{3,2},{5,4},{6,5},{7,6},{9,8},{10,9},{11,10},{13,12},{... | collective-permute-start | bytes 2239496 | tf_op jit(solution)/shard_map/ppermute | solution.py:28
  136.7 7.4 %collective-permute-done.10 = f32[486,3,1,128]{3,2,1,0:T(1,128)} collective-permute-done((f32[486,3,1,128]{3,2,1,0:T(1,128)S(1)}, f32[486,3,1,128]{3,2,1,0:T(1,128)}, u32[]{:S(2)}, u32[]{:S(2)}) %collective-permute-start.10) | collective-permute-done | bytes 746528 | tf_op jit(solution)/shard_map/ppermute | solution.py:27
  147.6 3.1 %copy.95 = f32[480,3,3,128]{0,3,2,1:T(8,128)} copy(f32[480,3,3,128]{3,0,2,1:T(8,128)} %slice.292) | data formatting | bytes 4423680 | tf_op jit(solution)/shard_map/slice | solution.py:114
  150.8 3.0 %copy.96 = f32[480,1152]{1,0:T(8,128)} copy(f32[480,1152]{0,1:T(8,128)} %bitcast.163) | data formatting | bytes 4423680
  153.8 39.9 %while.37 = (s32[]{:T(128)}, f32[480,1152]{1,0:T(8,128)}, f32[6,1152]{1,0:T(8,128)S(1)}, s32[512]{0:T(512)S(1)}, s32[512,128]{1,0:T(8,128)S(1)}, /*index=5*/f32[...) while((s32[]{:T(128)}, f32[480,1152]{1,0:T(8,128)}, ...), condition=%wide.region_9.10_spmd.clone, body=%wide.region_6.9_spmd.clone.sunk | while | flops 2093718912 | bytes 24165672 | solution.py:180
  154.0 8.1 %fusion.148 = f32[256,9,128]{2,1,0:T(8,128)} fusion(s32[256,128]{1,0:T(8,128)S(1)} %add_select_fusion.14, s32[256,128]{1,0:T(8,128)S(1)} %get-tuple-element.1449), kind=kOutput, calls=%fused_computation.49.clone.1 | convolution fusion | flops 79986688 | bytes 1441792 | tf_op jit(solution)/shard_map/while/body/eval_jaxpr/tas,tsk->tak/dot_general | solution.py:148
  164.5 3.5 %select_reduce_fusion.5 = (f32[256]{0:T(256)S(1)}, f32[256,1152]{1,0:T(8,128)S(1)}) fusion(f32[256,1152]{1,0:T(8,128)S(1)} %copy.114, f32[1152]{0:T(1024)S(1)} %reduce.46, f32[1152]{0:T(1024)S(1)} %get-tuple-element.1573, f32[256]{0:T(256)S(1)} %get-tuple-element.1450, f32[1152]{0:T(1024)S(1)} %broadcast_multiply_fusion.5, ...), kind=kOutput, calls=%fused_computation.67.clone.1 | convolution fusion | flops 1703534336 | bytes 4602880 | tf_op jit(solution)/shard_map/while/body/eval_jaxpr/dot_general | solution.py:131
  170.2 2.0 convolution_add_fusion.12
  173.1 8.1 %fusion.148 = f32[256,9,128]{2,1,0:T(8,128)} fusion(s32[256,128]{1,0:T(8,128)S(1)} %add_select_fusion.14, s32[256,128]{1,0:T(8,128)S(1)} %get-tuple-element.1449), kind=kOutput, calls=%fused_computation.49.clone.1 | convolution fusion | flops 79986688 | bytes 1441792 | tf_op jit(solution)/shard_map/while/body/eval_jaxpr/tas,tsk->tak/dot_general | solution.py:148
  183.7 3.5 %select_reduce_fusion.5 = (f32[256]{0:T(256)S(1)}, f32[256,1152]{1,0:T(8,128)S(1)}) fusion(f32[256,1152]{1,0:T(8,128)S(1)} %copy.114, f32[1152]{0:T(1024)S(1)} %reduce.46, f32[1152]{0:T(1024)S(1)} %get-tuple-element.1573, f32[256]{0:T(256)S(1)} %get-tuple-element.1450, f32[1152]{0:T(1024)S(1)} %broadcast_multiply_fusion.5, ...), kind=kOutput, calls=%fused_computation.67.clone.1 | convolution fusion | flops 1703534336 | bytes 4602880 | tf_op jit(solution)/shard_map/while/body/eval_jaxpr/dot_general | solution.py:131
  189.3 3.7 %convolution_add_fusion.12 = f32[480,1152]{1,0:T(8,128)} fusion(f32[480,1152]{1,0:T(8,128)} %get-tuple-element.1541, pred[]{:T(512)S(6)} %compare.51, f32[256,1152]{1,0:T(8,128)S(1)} %divide_multiply_fusion.5, s32[256]{0:T(256)S(1)} %dynamic_slice.169), kind=kOutput, calls=%fused_computation.51.clone.1 | convolution fusion | flops 284884992 | bytes 5604353 | tf_op jit(solution)/shard_map/while/body/eval_jaxpr/dot_general | solution.py:156
  193.7 2.0 copy.97
  197.9 5.0 %concatenate.75 = f32[486,3,3,128]{3,0,1,2:T(8,128)S(1)} concatenate(f32[480,3,3,128]{3,0,1,2:T(8,128)} %copy.98, f32[1,3,3,128]{3,0,1,2:T(1,128)S(1)} %copy.99, f32[1,3,3,128]{3,0,1,2:T(1,128)S(1)} %copy.100, f32[1,3,3,128]{3,0,1,2:T(1,128)S(1)} %copy.101, f32[1,3,3,128]{3,0,1,2:T(1,128)S(1)} %copy.102, f32[1,3,3,128]{3,0,1,2:T(1,128)S(1)} %copy.103, f32[1,3,3,128]{3,0,1,2:T(1,128)S(1)} %copy.104), dimensions={0} | concatenate | bytes 4478976 | tf_op jit(solution)/shard_map/concatenate | solution.py:196
  203.1 3.8 %collective-permute-start.12 = (f32[486,3,128]{2,0,1:T(8,128)S(1)}, f32[486,3,128]{2,0,1:T(8,128)S(1)}, u32[]{:S(2)}, u32[]{:S(2)}) collective-permute-start(f32[486,3,128]{2,0,1:T(8,128)S(1)} %get-tuple-element.1212), channel_id=1, source_target_pairs={{1,0},{2,1},{3,2},{5,4},{6,5},{7,6},{9,8},{10,9},{11,10},{13,12},{... | collective-permute-start | bytes 2239496 | tf_op jit(solution)/shard_map/ppermute | solution.py:17
  208.8 7.2 %collective-permute-done.12 = f32[486,3,128]{2,0,1:T(8,128)S(1)} collective-permute-done((f32[486,3,128]{2,0,1:T(8,128)S(1)}, f32[486,3,128]{2,0,1:T(8,128)S(1)}, u32[]{:S(2)}, u32[]{:S(2)}) %collective-permute-start.12) | collective-permute-done | bytes 746528 | tf_op jit(solution)/shard_map/ppermute | solution.py:17
  216.0 3.8 %collective-permute-done.13 = f32[486,3,128]{2,0,1:T(8,128)S(1)} collective-permute-done((f32[486,3,128]{2,0,1:T(8,128)S(1)}, f32[486,3,128]{2,0,1:T(8,128)S(1)}, u32[]{:S(2)}, u32[]{:S(2)}) %collective-permute-start.13) | collective-permute-done | bytes 746528 | tf_op jit(solution)/shard_map/ppermute | solution.py:17
  220.0 2.4 %collective-permute-start.14 = (f32[486,128]{1,0:T(8,128)S(1)}, f32[486,128]{1,0:T(8,128)S(1)}, u32[]{:S(2)}, u32[]{:S(2)}) collective-permute-start(f32[486,128]{1,0:T(8,128)S(1)} %get-tuple-element.1225), channel_id=1, source_target_pairs={{4,0},{8,4},{12,8},{5,1},{9,5},{13,9},{6,2},{10,6},{14,10},{7,3},{... | collective-permute-start | bytes 746504 | tf_op jit(solution)/shard_map/ppermute | solution.py:17
  222.4 3.5 %collective-permute-start.15 = (f32[486,128]{1,0:T(8,128)S(1)}, f32[486,128]{1,0:T(8,128)S(1)}, u32[]{:S(2)}, u32[]{:S(2)}) collective-permute-start(f32[486,128]{1,0:T(8,128)S(1)} %get-tuple-element.1226), channel_id=1, source_target_pairs={{0,4},{4,8},{8,12},{1,5},{5,9},{9,13},{2,6},{6,10},{10,14},{3,7},{... | collective-permute-start | bytes 746504 | tf_op jit(solution)/shard_map/ppermute | solution.py:17
  225.9 2.3 collective-permute-done.14
  228.1 2.4 %collective-permute-done.15 = f32[486,128]{1,0:T(8,128)S(1)} collective-permute-done((f32[486,128]{1,0:T(8,128)S(1)}, f32[486,128]{1,0:T(8,128)S(1)}, u32[]{:S(2)}, u32[]{:S(2)}) %collective-permute-start.15) | collective-permute-done | bytes 248864 | tf_op jit(solution)/shard_map/ppermute | solution.py:17
  (182 shorter events, 50.0 us)
Async XLA Ops:
  5.1 18.9 %copy-start.4 = (f32[2,1,1,512]{3,2,1,0:T(1,128)S(1)}, f32[2,1,1,512]{3,2,1,0:T(1,128)}, u32[]{:S(2)}) copy-start(f32[2,1,1,512]{3,2,1,0:T(1,128)} %param.12) | copy-start | bytes 12292
  5.4 9.7 %collective-permute-start = (f32[486,1,1,128]{3,2,1,0:T(1,128)S(1)}, f32[486,1,1,128]{3,2,1,0:T(1,128)S(1)}, u32[]{:S(2)}, u32[]{:S(2)}) collective-permute-start(f32[486,1,1,128]{3,2,1,0:T(1,128)S(1)} %broadcast_in_dim.126), channel_id=1, source_target_pairs={{0,4},{4,8},{8,12},{1,5},{5,9},{9,13},{2,6},{6,10},{10,14},{3,7},{... | collective-permute-start | bytes 746504 | tf_op jit(solution)/shard_map/ppermute | solution.py:27
  8.9 9.4 %collective-permute-start.1 = (f32[486,1,1,128]{3,2,1,0:T(1,128)S(1)}, f32[486,1,1,128]{3,2,1,0:T(1,128)S(1)}, u32[]{:S(2)}, u32[]{:S(2)}) collective-permute-start(f32[486,1,1,128]{3,2,1,0:T(1,128)S(1)} %broadcast_in_dim.126), channel_id=1, source_target_pairs={{4,0},{8,4},{12,8},{5,1},{9,5},{13,9},{6,2},{10,6},{14,10},{7,3},{... | collective-permute-start | bytes 746504 | tf_op jit(solution)/shard_map/ppermute | solution.py:28
  18.4 12.9 %collective-permute-start.2 = (f32[486,3,1,128]{3,2,1,0:T(1,128)S(1)}, f32[486,3,1,128]{3,2,1,0:T(1,128)S(1)}, u32[]{:S(2)}, u32[]{:S(2)}) collective-permute-start(f32[486,3,1,128]{3,2,1,0:T(1,128)S(1)} %constant_dynamic-update-slice_fusion), channel_id=1, source_target_pairs={{0,1},{1,2},{2,3},{4,5},{5,6},{6,7},{8,9},{9,10},{10,11},{12,13},{... | collective-permute-start | bytes 2239496 | tf_op jit(solution)/shard_map/ppermute | solution.py:27
  20.4 12.7 %collective-permute-start.3 = (f32[486,3,1,128]{3,2,1,0:T(1,128)S(1)}, f32[486,3,1,128]{3,2,1,0:T(1,128)S(1)}, u32[]{:S(2)}, u32[]{:S(2)}) collective-permute-start(f32[486,3,1,128]{3,2,1,0:T(1,128)S(1)} %constant_dynamic-update-slice_fusion), channel_id=1, source_target_pairs={{1,0},{2,1},{3,2},{5,4},{6,5},{7,6},{9,8},{10,9},{11,10},{13,12},{... | collective-permute-start | bytes 2239496 | tf_op jit(solution)/shard_map/ppermute | solution.py:28
  38.2 3.1 %copy-start = (s32[1,1,512,128]{3,2,1,0:T(8,128)S(1)}, s32[1,1,512,128]{3,2,1,0:T(8,128)}, u32[]{:S(2)}) copy-start(s32[1,1,512,128]{3,2,1,0:T(8,128)} %param.14) | copy-start | bytes 786436
  38.3 3.1 %copy-start.1 = (s32[1,1,512]{2,1,0:T(1,128)S(1)}, s32[1,1,512]{2,1,0:T(1,128)}, u32[]{:S(2)}) copy-start(s32[1,1,512]{2,1,0:T(1,128)} %param.13) | copy-start | bytes 6148
  38.3 3.1 %copy-start.5 = (s32[1,1,2]{2,1,0:T(1,128)S(1)}, s32[1,1,2]{2,1,0:T(1,128)}, u32[]{:S(2)}) copy-start(s32[1,1,2]{2,1,0:T(1,128)} %param.15) | copy-start | bytes 28
  90.7 12.9 %collective-permute-start.4 = (f32[486,3,128]{2,0,1:T(8,128)S(1)}, f32[486,3,128]{2,0,1:T(8,128)S(1)}, u32[]{:S(2)}, u32[]{:S(2)}) collective-permute-start(f32[486,3,128]{2,0,1:T(8,128)S(1)} %get-tuple-element.1217), channel_id=1, source_target_pairs={{1,0},{2,1},{3,2},{5,4},{6,5},{7,6},{9,8},{10,9},{11,10},{13,12},{... | collective-permute-start | bytes 2239496 | tf_op jit(solution)/shard_map/ppermute | solution.py:17
  94.5 12.9 %collective-permute-start.5 = (f32[486,3,128]{2,0,1:T(8,128)S(1)}, f32[486,3,128]{2,0,1:T(8,128)S(1)}, u32[]{:S(2)}, u32[]{:S(2)}) collective-permute-start(f32[486,3,128]{2,0,1:T(8,128)S(1)} %get-tuple-element.1218), channel_id=1, source_target_pairs={{0,1},{1,2},{2,3},{4,5},{5,6},{6,7},{8,9},{9,10},{10,11},{12,13},{... | collective-permute-start | bytes 2239496 | tf_op jit(solution)/shard_map/ppermute | solution.py:17
  107.6 10.9 %copy-start.2 = (f32[2,1,1,128]{3,2,1,0:T(1,128)S(1)}, f32[2,1,1,128]{3,2,1,0:T(1,128)}, u32[]{:S(2)}) copy-start(f32[2,1,1,128]{3,2,1,0:T(1,128)} %param.18) | copy-start | bytes 3076
  107.6 10.8 %copy-start.3 = (f32[2,1,1,128]{3,2,1,0:T(1,128)S(1)}, f32[2,1,1,128]{3,2,1,0:T(1,128)}, u32[]{:S(2)}) copy-start(f32[2,1,1,128]{3,2,1,0:T(1,128)} %param.17) | copy-start | bytes 3076
  107.6 8.1 %collective-permute-start.6 = (f32[486,128]{1,0:T(8,128)S(1)}, f32[486,128]{1,0:T(8,128)S(1)}, u32[]{:S(2)}, u32[]{:S(2)}) collective-permute-start(f32[486,128]{1,0:T(8,128)S(1)} %get-tuple-element.1227), channel_id=1, source_target_pairs={{4,0},{8,4},{12,8},{5,1},{9,5},{13,9},{6,2},{10,6},{14,10},{7,3},{... | collective-permute-start | bytes 746504 | tf_op jit(solution)/shard_map/ppermute | solution.py:17
  110.2 8.1 %collective-permute-start.7 = (f32[486,128]{1,0:T(8,128)S(1)}, f32[486,128]{1,0:T(8,128)S(1)}, u32[]{:S(2)}, u32[]{:S(2)}) collective-permute-start(f32[486,128]{1,0:T(8,128)S(1)} %get-tuple-element.1228), channel_id=1, source_target_pairs={{0,4},{4,8},{8,12},{1,5},{5,9},{9,13},{2,6},{6,10},{10,14},{3,7},{... | collective-permute-start | bytes 746504 | tf_op jit(solution)/shard_map/ppermute | solution.py:17
  118.7 8.1 %collective-permute-start.8 = (f32[486,1,1,128]{3,0,2,1:T(8,128)S(1)}, f32[486,1,1,128]{3,0,2,1:T(8,128)S(1)}, u32[]{:S(2)}, u32[]{:S(2)}) collective-permute-start(f32[486,1,1,128]{3,0,2,1:T(8,128)S(1)} %bitcast.166), channel_id=1, source_target_pairs={{0,4},{4,8},{8,12},{1,5},{5,9},{9,13},{2,6},{6,10},{10,14},{3,7},{... | collective-permute-start | bytes 746504 | tf_op jit(solution)/shard_map/ppermute | solution.py:27
  122.1 8.1 %collective-permute-start.9 = (f32[486,1,1,128]{3,0,2,1:T(8,128)S(1)}, f32[486,1,1,128]{3,0,2,1:T(8,128)S(1)}, u32[]{:S(2)}, u32[]{:S(2)}) collective-permute-start(f32[486,1,1,128]{3,0,2,1:T(8,128)S(1)} %bitcast.167), channel_id=1, source_target_pairs={{4,0},{8,4},{12,8},{5,1},{9,5},{13,9},{6,2},{10,6},{14,10},{7,3},{... | collective-permute-start | bytes 746504 | tf_op jit(solution)/shard_map/ppermute | solution.py:28
  131.1 13.0 %collective-permute-start.10 = (f32[486,3,1,128]{3,2,1,0:T(1,128)S(1)}, f32[486,3,1,128]{3,2,1,0:T(1,128)}, u32[]{:S(2)}, u32[]{:S(2)}) collective-permute-start(f32[486,3,1,128]{3,2,1,0:T(1,128)S(1)} %copy.91), channel_id=1, source_target_pairs={{0,1},{1,2},{2,3},{4,5},{5,6},{6,7},{8,9},{9,10},{10,11},{12,13},{... | collective-permute-start | bytes 2239496 | tf_op jit(solution)/shard_map/ppermute | solution.py:27
  133.1 12.7 %collective-permute-start.11 = (f32[486,3,1,128]{3,2,1,0:T(1,128)S(1)}, f32[486,3,1,128]{3,2,1,0:T(1,128)S(1)}, u32[]{:S(2)}, u32[]{:S(2)}) collective-permute-start(f32[486,3,1,128]{3,2,1,0:T(1,128)S(1)} %copy.91), channel_id=1, source_target_pairs={{1,0},{2,1},{3,2},{5,4},{6,5},{7,6},{9,8},{10,9},{11,10},{13,12},{... | collective-permute-start | bytes 2239496 | tf_op jit(solution)/shard_map/ppermute | solution.py:28
  203.1 12.9 %collective-permute-start.12 = (f32[486,3,128]{2,0,1:T(8,128)S(1)}, f32[486,3,128]{2,0,1:T(8,128)S(1)}, u32[]{:S(2)}, u32[]{:S(2)}) collective-permute-start(f32[486,3,128]{2,0,1:T(8,128)S(1)} %get-tuple-element.1212), channel_id=1, source_target_pairs={{1,0},{2,1},{3,2},{5,4},{6,5},{7,6},{9,8},{10,9},{11,10},{13,12},{... | collective-permute-start | bytes 2239496 | tf_op jit(solution)/shard_map/ppermute | solution.py:17
  206.9 12.9 %collective-permute-start.13 = (f32[486,3,128]{2,0,1:T(8,128)S(1)}, f32[486,3,128]{2,0,1:T(8,128)S(1)}, u32[]{:S(2)}, u32[]{:S(2)}) collective-permute-start(f32[486,3,128]{2,0,1:T(8,128)S(1)} %get-tuple-element.1213), channel_id=1, source_target_pairs={{0,1},{1,2},{2,3},{4,5},{5,6},{6,7},{8,9},{9,10},{10,11},{12,13},{... | collective-permute-start | bytes 2239496 | tf_op jit(solution)/shard_map/ppermute | solution.py:17
  220.0 8.1 %collective-permute-start.14 = (f32[486,128]{1,0:T(8,128)S(1)}, f32[486,128]{1,0:T(8,128)S(1)}, u32[]{:S(2)}, u32[]{:S(2)}) collective-permute-start(f32[486,128]{1,0:T(8,128)S(1)} %get-tuple-element.1225), channel_id=1, source_target_pairs={{4,0},{8,4},{12,8},{5,1},{9,5},{13,9},{6,2},{10,6},{14,10},{7,3},{... | collective-permute-start | bytes 746504 | tf_op jit(solution)/shard_map/ppermute | solution.py:17
  222.4 8.1 %collective-permute-start.15 = (f32[486,128]{1,0:T(8,128)S(1)}, f32[486,128]{1,0:T(8,128)S(1)}, u32[]{:S(2)}, u32[]{:S(2)}) collective-permute-start(f32[486,128]{1,0:T(8,128)S(1)} %get-tuple-element.1226), channel_id=1, source_target_pairs={{0,4},{4,8},{8,12},{1,5},{5,9},{9,13},{2,6},{6,10},{10,14},{3,7},{... | collective-permute-start | bytes 746504 | tf_op jit(solution)/shard_map/ppermute | solution.py:17
where the time goes:
time: 233 us; the launch traced here: 232 us
  matrix products  60.5 us (26%)
  waiting for transfers between devices  60.4 us (26%)
  local copies, waits for them, and re-layouts  48 us (21%)
  starting transfers between devices  46.2 us (20%)
  other arithmetic  15.4 us (7%)
    dot_general x4, matrix products, one_block(): jnp.einsum('tas,tsk->tak', slot_hot, cell_hot, preferred_element_type=jnp...  32.4 us
    ppermute x8, waiting for transfers between devices, shifted(): return lax.ppermute(x, axis, pairs)  31.3 us
    ppermute x8, starting transfers between devices, shifted(): return lax.ppermute(x, axis, pairs)  23.3 us
    ppermute x4, waiting for transfers between devices, padded(): before = lax.ppermute(last, axis, up)  20.7 us
    dot_general x4, matrix products, one_block(): gene_logs = jnp.dot(gene_hot, log_table, precision=lax.Precision.HIGHEST)  14.1 us
    concatenate x28, local copies, waits for them, and re-layouts, body(): jnp.concatenate([count_acc, jnp.stack([weight_sum, sum_row, sum_col, sum_...  14.1 us
    ppermute x4, starting transfers between devices, padded(): after = lax.ppermute(first, axis, down)  12 us
    dot_general x4, matrix products, one_block(): lax.dot_general(onehot, posterior.astype(jnp.bfloat16), (((0,), (0,)), ((...  11.4 us
  transfers between devices with their start and end apart: 16, of which 16 were waited for; matrix products, arithmetic and copies ran while one was open for 1% of the time, Pallas kernels for 0%

commit v1 on v0

v1 whole, which is shorter than its diff:
```python
import functools

import jax
import jax.numpy as jnp
from jax import lax
from jax.experimental import pallas as pl
from jax.experimental.pallas import tpu as pltpu
from jax.sharding import PartitionSpec as P

BLOCK = 256
ITERS = 2
LANES = 128
FEATURES = 8
PARTS = 3
NEVER = -1e30

pseudo_count = 0.05
prior_weight = 1.0

f32 = jnp.float32
bf16 = jnp.bfloat16
i32 = jnp.int32


def shifted(x, axis, by):
    count = lax.axis_size(axis)
    pairs = [(i, i + by) for i in range(count) if 0 <= i + by < count]
    return lax.ppermute(x, axis, pairs)


def params(mib=40):
    return pltpu.CompilerParams(vmem_limit_bytes=mib << 20)


def cost(flops, size):
    return pl.CostEstimate(flops=flops, bytes_accessed=size, transcendentals=0)


def call(kernel, name, outs, in_specs, scratch, flops, args):
    shapes = [jax.ShapeDtypeStruct(s, d) for s, d in outs]
    return pl.pallas_call(
        kernel,
        name=name,
        out_shape=shapes,
        in_specs=in_specs,
        out_specs=[pl.BlockSpec(memory_space=pltpu.VMEM)] * len(shapes),
        scratch_shapes=scratch,
        compiler_params=params(),
        cost_estimate=cost(flops, 1 << 20),
    )(*args)


VMEM = pl.BlockSpec(memory_space=pltpu.VMEM)
SMEM = pl.BlockSpec(memory_space=pltpu.SMEM)


def lane_tile(k):
    return pl.ds(k * LANES, LANES)


def pack_kernel(count_ref, cand_ref, pos_ref, gene_ref, out_ref):
    tokens, slots = cand_ref.shape
    tiles = tokens // LANES
    out_ref[0:slots, :] = cand_ref[...].astype(f32).T
    lane = lax.broadcasted_iota(i32, (1, LANES), 1)
    for k in range(tiles):
        start = k * LANES
        live = (start % BLOCK + lane) < count_ref[start // BLOCK]
        rows = [
            pos_ref[k : k + 1, :],
            pos_ref[tiles + k : tiles + k + 1, :],
            gene_ref[k : k + 1, :].astype(f32),
            live.astype(f32),
            jnp.zeros((FEATURES - 4, LANES), f32),
        ]
        out_ref[slots : slots + FEATURES, lane_tile(k)] = jnp.concatenate(rows, axis=0)


def multiple_kernel(tile_cells, up_ref, own_ref, down_ref, left_ref, mid_ref, right_ref, word_s, unit_s):
    rows, tokens = own_ref.shape
    slots = rows - FEATURES
    words = tile_cells // 8
    shift = tile_cells.bit_length() - 1
    word_shift = words.bit_length() - 1
    held = 3 * words // 8
    per_tile = words // 8
    sub = lax.broadcasted_iota(i32, (8, LANES), 0)
    outs = (left_ref, mid_ref, right_ref)
    nibbles = jnp.full((8, LANES), 0x0F0F0F0F, i32)
    for source, z_ref in enumerate((up_ref, own_ref, down_ref)):
        for k in range(tokens // LANES):
            local = z_ref[0:slots, lane_tile(k)].astype(i32) - (2 - source) * 3 * tile_cells
            word_s[k] = (local >> shift) * words + (local & (words - 1))
            unit_s[k] = 1 << (((local & (tile_cells - 1)) >> word_shift) * 4)
        for k in range(tokens // LANES):

            def group(g, carry):
                low, high = carry
                word = [jnp.zeros((8, LANES), i32) for _ in range(held)]
                for j in range(8):
                    which = word_s[k, pl.ds(g * 8 + j, 8, stride=0), :]
                    unit = unit_s[k, pl.ds(g * 8 + j, 8, stride=0), :]
                    for n in range(held):
                        word[n] = word[n] + jnp.where(which == sub + 8 * n, unit, 0)
                low = [a + (w & nibbles) for a, w in zip(low, word)]
                high = [a + ((w >> 4) & nibbles) for a, w in zip(high, word)]
                return low, high

            zero = [jnp.zeros((8, LANES), i32) for _ in range(held)]
            low, high = lax.fori_loop(0, slots // 8, group, (zero, list(zero)))
            live = z_ref[slots + 3 : slots + 4, lane_tile(k)]
            for n in range(held):
                for field in range(8):
                    part = low[n] if field % 2 == 0 else high[n]
                    value = ((part >> (8 * (field // 2))) & 255).astype(f32) * live
                    row = field * words + (n % per_tile) * 8
                    outs[n // per_tile][source, row : row + 8, lane_tile(k)] = value
        for out in outs:
            out[source, tile_cells : tile_cells + FEATURES, :] = z_ref[slots : slots + FEATURES, :]


def set_tables(log_rows, state, log_weight, log_s, ltp_s, par_s):
    genes, cells = log_rows.shape
    padded = log_s.shape[0]
    log_s[0:genes, :] = log_rows
    if padded > genes:
        log_s[genes:padded, :] = jnp.zeros((padded - genes, cells), f32)
    rest = log_s[...].T
    for part in range(PARTS):
        piece = rest.astype(bf16)
        ltp_s[part * cells : (part + 1) * cells, :] = piece
        if part + 1 < PARTS:
            rest = rest - piece.astype(f32)
    mu_row, mu_col, rr, rc, cc = state
    det = rr * cc - rc * rc
    rows = [
        mu_row,
        mu_col,
        -0.5 * (cc / det),
        rc / det,
        -0.5 * (rr / det),
        log_weight - 0.5 * jnp.log(det),
        jnp.zeros((LANES - 6, cells), f32),
    ]
    columns = jnp.concatenate(rows, axis=0).T
    for n in range(6):
        par_s[n] = jnp.broadcast_to(columns[:, n : n + 1], (cells, LANES))


def gene_hot(x_ref, source, cells, padded):
    tokens = x_ref.shape[2]
    gene = x_ref[source, cells + 2 : cells + 3, :].astype(i32)
    axis = lax.broadcasted_iota(i32, (padded, tokens), 0)
    return jnp.where(axis == gene, 1.0, 0.0).astype(bf16)


def neighbour(source, side):
    rows, cols = lax.axis_size("row"), lax.axis_size("col")
    row = lax.axis_index("row") + source - 1
    col = lax.axis_index("col") + side - 1
    inside = (row >= 0) & (row < rows) & (col >= 0) & (col < cols)
    at = jnp.clip(row, 0, rows - 1) * cols + jnp.clip(col, 0, cols - 1)
    return inside, at


def score_block(x_ref, source, side, hot, ltp_s, par_s, gl_s, sc_s, e_ref, m_ref, out_ref):
    cells = sc_s.shape[0]
    tokens = sc_s.shape[1]
    tiles = tokens // LANES
    gl_s[...] = jnp.dot(ltp_s[...], hot, preferred_element_type=f32)
    step_row = (source - 1).astype(f32) if hasattr(source, "astype") else float(source - 1)
    y0 = [x_ref[source, cells : cells + 1, lane_tile(k)] + step_row for k in range(tiles)]
    y1 = [x_ref[source, cells + 1 : cells + 2, lane_tile(k)] + float(side - 1) for k in range(tiles)]
    block = source * 3 + side

    def first(c, top):
        at = pl.multiple_of(c * 8, 8)
        p = [par_s[n, pl.ds(at, 8), :] for n in range(6)]
        out = []
        for k in range(tiles):
            d0 = y0[k] - p[0]
            d1 = y1[k] - p[1]
            logs = gl_s[pl.ds(at, 8), lane_tile(k)]
            for part in range(1, PARTS):
                logs = logs + gl_s[pl.ds(part * cells + at, 8), lane_tile(k)]
            score = logs + p[5] + (d0 * (p[2] * d0 + p[3] * d1) + p[4] * d1 * d1)
            count = x_ref[source, pl.ds(at, 8), lane_tile(k)]
            score = jnp.where(count > 0.0, score, NEVER)
            sc_s[pl.ds(at, 8), lane_tile(k)] = score
            out.append(jnp.maximum(top[k], score))
        return out

    top = lax.fori_loop(0, cells // 8, first, [jnp.full((8, LANES), NEVER, f32)] * tiles, unroll=2)
    top = [jnp.max(a, axis=0, keepdims=True) for a in top]

    def second(c, total):
        at = pl.multiple_of(c * 8, 8)
        out = []
        for k in range(tiles):
            e = x_ref[source, pl.ds(at, 8), lane_tile(k)] * jnp.exp(
                sc_s[pl.ds(at, 8), lane_tile(k)] - top[k]
            )
            e_ref[block, pl.ds(at, 8), lane_tile(k)] = e
            out.append(total[k] + e)
        return out

    total = lax.fori_loop(0, cells // 8, second, [jnp.zeros((8, LANES), f32)] * tiles, unroll=2)
    total = [jnp.sum(a, axis=0, keepdims=True) for a in total]
    both = jnp.concatenate(top + total, axis=0)
    m_ref[block] = both
    inside, at = neighbour(source, side)

    @pl.when(inside)
    def _():
        out_ref[at] = both


def first_kernel(
    w_ref, centre_ref, spread_ref, corr_ref, left_ref, mid_ref, right_ref,
    e_ref, m_ref, out_ref, state_ref,
    log_s, ltp_s, par_s, gl_s, sc_s,
):
    weights = w_ref[...]
    profile = weights / jnp.sum(weights, axis=0, keepdims=True)
    spread_row, spread_col = spread_ref[0:1, :], spread_ref[1:2, :]
    state = (
        centre_ref[0:1, :],
        centre_ref[1:2, :],
        spread_row * spread_row,
        corr_ref[0:1, :] * spread_row * spread_col,
        spread_col * spread_col,
    )
    cells = weights.shape[1]
    state_ref[...] = jnp.concatenate(list(state) + [jnp.zeros((3, cells), f32)], axis=0)
    set_tables(jnp.log(profile), state, jnp.zeros((1, cells), f32), log_s, ltp_s, par_s)
    out_ref[...] = jnp.zeros(out_ref.shape, f32)
    for side, x_ref in enumerate((left_ref, mid_ref, right_ref)):

        @pl.loop(0, 3)
        def _(source):
            hot = gene_hot(x_ref, source, cells, log_s.shape[0])
            score_block(x_ref, source, side, hot, ltp_s, par_s, gl_s, sc_s, e_ref, m_ref, out_ref)


def join_kernel(in_ref, out_ref):
    half = in_ref.shape[1] // 2
    parts = []
    for source in range(3):
        for side in range(3):
            inside, at = neighbour(source, side)
            part = in_ref[at]
            parts.append((jnp.where(inside, part[0:half], NEVER), jnp.where(inside, part[half:], 0.0)))
    top = functools.reduce(jnp.maximum, [m for m, _ in parts])
    total = sum(s * jnp.exp(m - top) for m, s in parts)
    factor = jnp.where(total > 0.0, 1.0 / total, 0.0)
    both = jnp.concatenate([top, factor], axis=0)
    for at in range(out_ref.shape[0]):
        out_ref[at] = both


def posterior_sums(x_refs, e_ref, m_ref, q_ref, hot_s, sh_s, mom_s, cnt_s, keep):
    cells, tokens = sh_s.shape
    tiles = tokens // LANES
    mom_s[...] = jnp.zeros(mom_s.shape, f32)
    cnt_s[...] = jnp.zeros(cnt_s.shape, f32)
    for side, x_ref in enumerate(x_refs):

        @pl.loop(0, 3)
        def _(source):
            block = source * 3 + side
            slot = block if keep else 0
            hot_s[slot] = gene_hot(x_ref, source, cells, cnt_s.shape[0])
            inside, at = neighbour(source, side)
            step_row = (source - 1).astype(f32)
            factor, features = [], []
            for k in range(tiles):
                m = m_ref[block, k : k + 1, :]
                f = jnp.exp(m - q_ref[at, k : k + 1, :]) * q_ref[at, tiles + k : tiles + k + 1, :]
                factor.append(jnp.where(inside, f, 0.0))
                y0 = x_ref[source, cells : cells + 1, lane_tile(k)] + step_row
                y1 = x_ref[source, cells + 1 : cells + 2, lane_tile(k)] + float(side - 1)
                features.append((y0, y1, y0 * y0, y0 * y1, y1 * y1))

            def group(c, carry):
                rows = pl.ds(pl.multiple_of(c * 16, 16), 16)
                sums = [mom_s[n, rows, :] for n in range(6)]
                for k in range(tiles):
                    p = e_ref[block, rows, lane_tile(k)] * factor[k]
                    sh_s[rows, lane_tile(k)] = p.astype(bf16)
                    sums[0] = sums[0] + p
                    for n in range(5):
                        sums[n + 1] = sums[n + 1] + p * features[k][n]
                for n in range(6):
                    mom_s[n, rows, :] = sums[n]
                return carry

            lax.fori_loop(0, cells // 16, group, 0)
            cnt_s[...] += lax.dot_general(
                hot_s[slot], sh_s[...], (((1,), (1,)), ((), ())), preferred_element_type=f32
            )


def new_cells(genes, mom_s, cnt_s, state_ref):
    weight, s0, s1, s00, s01, s11 = [jnp.sum(mom_s[n].T, axis=0, keepdims=True) for n in range(6)]
    mu_row, mu_col, rr, rc, cc = [state_ref[n : n + 1, :] for n in range(5)]
    counts = cnt_s[0:genes, :]
    profile = (counts + pseudo_count) / (
        jnp.sum(counts, axis=0, keepdims=True) + genes * pseudo_count
    )
    denominator = weight + prior_weight
    new_row = (s0 + prior_weight * mu_row) / denominator
    new_col = (s1 + prior_weight * mu_col) / denominator
    q_rr = s00 - 2.0 * new_row * s0 + weight * new_row * new_row
    q_rc = s01 - new_row * s1 - new_col * s0 + weight * new_row * new_col
    q_cc = s11 - 2.0 * new_col * s1 + weight * new_col * new_col
    state = (
        new_row,
        new_col,
        (q_rr + prior_weight * rr) / denominator,
        (q_rc + prior_weight * rc) / denominator,
        (q_cc + prior_weight * cc) / denominator,
    )
    return jnp.log(profile), state, jnp.log(weight + 1.0)


def middle_kernel(
    genes,
    left_ref, mid_ref, right_ref, e_ref, m_ref, q_ref, state_ref,
    e_out, m_out, out_ref, state_out,
    hot_s, sh_s, mom_s, cnt_s, log_s, ltp_s, par_s, gl_s, sc_s,
):
    x_refs = (left_ref, mid_ref, right_ref)
    posterior_sums(x_refs, e_ref, m_ref, q_ref, hot_s, sh_s, mom_s, cnt_s, True)
    log_rows, state, log_weight = new_cells(genes, mom_s, cnt_s, state_ref)
    cells = log_rows.shape[1]
    state_out[...] = jnp.concatenate(list(state) + [jnp.zeros((3, cells), f32)], axis=0)
    set_tables(log_rows, state, log_weight, log_s, ltp_s, par_s)
    out_ref[...] = jnp.zeros(out_ref.shape, f32)
    for side, x_ref in enumerate(x_refs):

        @pl.loop(0, 3)
        def _(source):
            hot = hot_s[source * 3 + side]
            score_block(x_ref, source, side, hot, ltp_s, par_s, gl_s, sc_s, e_out, m_out, out_ref)


def last_kernel(
    genes,
    left_ref, mid_ref, right_ref, e_ref, m_ref, q_ref, state_ref,
    profile_ref, cells_ref,
    hot_s, sh_s, mom_s, cnt_s,
):
    posterior_sums((left_ref, mid_ref, right_ref), e_ref, m_ref, q_ref, hot_s, sh_s, mom_s, cnt_s, False)
    log_rows, state, log_weight = new_cells(genes, mom_s, cnt_s, state_ref)
    profile_ref[...] = log_rows
    mu_row, mu_col, rr, rc, cc = state
    cells_ref[...] = jnp.concatenate(
        [mu_row, mu_col, 0.5 * jnp.log(rr), 0.5 * jnp.log(cc), rc / jnp.sqrt(rr * cc), log_weight],
        axis=0,
    )


def body(
    positions, genes, candidates, block_counts, profile_weights, centroids, spreads, correlation
):
    gene_total = profile_weights.shape[0]
    cells = profile_weights.shape[3]
    tokens, slots = candidates.shape[2:]
    tiles = tokens // LANES
    group = lax.axis_size("row") * lax.axis_size("col")
    padded = -(-gene_total // LANES) * LANES
    pairs = 9 * tokens * cells

    packed, = call(
        pack_kernel, "pack", [((slots + FEATURES, tokens), f32)],
        [SMEM, VMEM, VMEM, VMEM], [], tokens * slots,
        (
            block_counts.reshape(-1),
            candidates.reshape(tokens, slots),
            positions.reshape(2 * tiles, LANES),
            genes.reshape(tiles, LANES),
        ),
    )
    from_up = shifted(packed, "row", 1)
    from_down = shifted(packed, "row", -1)
    three = ((3, cells + FEATURES, tokens), f32)
    to_left, mid, to_right = call(
        functools.partial(multiple_kernel, cells), "multiple", [three] * 3, [VMEM] * 3,
        [pltpu.VMEM((tiles, slots, LANES), i32)] * 2, pairs * 40,
        (from_up, packed, from_down),
    )
    from_right = shifted(to_left, "col", -1)
    from_left = shifted(to_right, "col", 1)
    x = (from_left, mid, from_right)

    kept = ((9, cells, tokens), f32)
    tops = ((9, 2 * tiles, LANES), f32)
    chunks = ((group, 2 * tiles, LANES), f32)
    rows = ((8, cells), f32)
    table_scratch = [
        pltpu.VMEM((padded, cells), f32),
        pltpu.VMEM((PARTS * cells, padded), bf16),
        pltpu.VMEM((6, cells, LANES), f32),
        pltpu.VMEM((PARTS * cells, tokens), f32),
        pltpu.VMEM((cells, tokens), f32),
    ]

    def sum_scratch(count):
        return [
            pltpu.VMEM((count, padded, tokens), bf16),
            pltpu.VMEM((cells, tokens), bf16),
            pltpu.VMEM((6, cells, LANES), f32),
            pltpu.VMEM((padded, cells), f32),
        ]

    def exchange(parts):
        back = lax.all_to_all(parts, ("row", "col"), 0, 0)
        joined, = call(join_kernel, "join", [chunks], [VMEM], [], tokens * 100, (back,))
        return lax.all_to_all(joined, ("row", "col"), 0, 0)

    e, m, parts, state = call(
        first_kernel, "first", [kept, tops, chunks, rows], [VMEM] * 7, table_scratch, pairs * 100,
        (
            profile_weights.reshape(gene_total, cells),
            centroids.reshape(2, cells),
            spreads.reshape(2, cells),
            correlation.reshape(1, cells),
            *x,
        ),
    )
    for _ in range(ITERS - 1):
        told = exchange(parts)
        e, m, parts, state = call(
            functools.partial(middle_kernel, gene_total), "middle", [kept, tops, chunks, rows],
            [VMEM] * 7, sum_scratch(9) + table_scratch, pairs * 200,
            (*x, e, m, told, state),
        )
    told = exchange(parts)
    final_profile, final_cells = call(
        functools.partial(last_kernel, gene_total), "last",
        [((gene_total, cells), f32), ((6, cells), f32)],
        [VMEM] * 7, sum_scratch(1), pairs * 100,
        (*x, e, m, told, state),
    )
    return (final_profile.reshape(gene_total, 1, 1, cells), final_cells.reshape(6, 1, 1, cells))


def solution(mesh):
    tiles = P(("groups", "row"), "col")
    stacked = P(None, ("groups", "row"), "col", None)
    return jax.shard_map(
        body,
        mesh=mesh,
        in_specs=(
            stacked,
            P(("groups", "row"), "col", None),
            P(("groups", "row"), "col", None, None),
            P(("groups", "row"), "col", None),
            stacked,
            stacked,
            stacked,
            P(("groups", "row"), "col", None),
        ),
        out_specs=(stacked, stacked),
        check_vma=False,
    )
```

time: 233 us -> 110 us (0.47)
  the two profiles are of different devices: /device:TPU:14 before, /device:TPU:0 now
where the time goes in v1:
time: 110 us
  blocking collectives  50.7 us (46%)
  Pallas kernels  31.7 us (29%)
  waiting for transfers between devices  10.7 us (10%)
  starting transfers between devices  9.53 us (9%)
  local copies, waits for them, and re-layouts  6.5 us (6%)
    all_to_all x2, blocking collectives, exchange(): back = lax.all_to_all(parts, ('row', 'col'), 0, 0)  31.8 us
    pallas_call x7, Pallas kernels, call(): pl.pallas_call(kernel, name=name, out_shape=shapes, in_specs=in_specs, ou...  31.7 us
    all_to_all x2, blocking collectives, exchange(): return lax.all_to_all(joined, ('row', 'col'), 0, 0)  19 us
    ppermute x4, waiting for transfers between devices, shifted(): return lax.ppermute(x, axis, pairs)  10.7 us
    ppermute x4, starting transfers between devices, shifted(): return lax.ppermute(x, axis, pairs)  9.53 us
    unnamed x17, local copies, waits for them, and re-layouts  6.5 us
  transfers between devices with their start and end apart: 4, of which 4 were waited for; matrix products, arithmetic and copies ran while one was open for 0% of the time, Pallas kernels for 0%

profile of v1, /device:TPU:0, one launch (start us, length us, event | category | flops | bytes accessed | tf_op | source)
XLA Modules:
  0.0 109.8 jit_solution(3866132439843443371)
XLA Ops:
  0.6 0.0 copy-start
  0.6 0.9 copy-done
  1.6 0.0 copy-start.2
  1.6 0.7 copy-done.2
  2.3 0.0 copy-start.3
  2.3 0.7 copy-done.3
  3.0 0.0 copy-start.6
  3.0 0.7 copy-done.6
  3.6 0.7 pack.1.own_ref
  4.3 1.3 %collective-permute-start.1 = (f32[136,512]{1,0:T(8,128)S(1)}, f32[136,512]{1,0:T(8,128)S(1)}, u32[]{:S(2)}, u32[]{:S(2)}) collective-permute-start(f32[136,512]{1,0:T(8,128)S(1)} %pack.1.own_ref), channel_id=1, source_target_pairs={{4,0},{8,4},{12,8},{5,1},{9,5},{13,9},{6,2},{10,6},{14,10},{7,3},{... | collective-permute-start | bytes 835592 | tf_op jit(solution)/shard_map/ppermute | solution.py:28
  5.6 5.6 %collective-permute-start = (f32[136,512]{1,0:T(8,128)S(1)}, f32[136,512]{1,0:T(8,128)S(1)}, u32[]{:S(2)}, u32[]{:S(2)}) collective-permute-start(f32[136,512]{1,0:T(8,128)S(1)} %pack.1.own_ref), channel_id=1, source_target_pairs={{0,4},{4,8},{8,12},{1,5},{5,9},{9,13},{2,6},{6,10},{10,14},{3,7},{... | collective-permute-start | bytes 835592 | tf_op jit(solution)/shard_map/ppermute | solution.py:28
  11.2 4.7 %collective-permute-done.1.down_ref = f32[136,512]{1,0:T(8,128)S(1)} collective-permute-done((f32[136,512]{1,0:T(8,128)S(1)}, f32[136,512]{1,0:T(8,128)S(1)}, u32[]{:S(2)}, u32[]{:S(2)}) %collective-permute-start.1) | collective-permute-done | bytes 278560 | tf_op jit(solution)/shard_map/ppermute | solution.py:28
  15.9 1.2 %collective-permute-done.up_ref = f32[136,512]{1,0:T(8,128)S(1)} collective-permute-done((f32[136,512]{1,0:T(8,128)S(1)}, f32[136,512]{1,0:T(8,128)S(1)}, u32[]{:S(2)}, u32[]{:S(2)}) %collective-permute-start) | collective-permute-done | bytes 278560 | tf_op jit(solution)/shard_map/ppermute | solution.py:28
  17.1 5.9 %multiple.1 = (f32[3,136,512]{2,1,0:T(8,128)S(1)}, f32[3,136,512]{2,1,0:T(8,128)S(1)}, f32[3,136,512]{2,1,0:T(8,128)S(1)}) custom-call(f32[136,512]{1,0:T(8,128)S(1)} %collective-permute-done.up_ref, f32[136,512]{1,0:T(8,128)S(1)} %pack.1.own_ref, f32[136,512]{1,0:T(8,128)S(1)} %collective-permute-done.1.down_ref), custom_call_target="tpu_custom_call" | custom-call | flops 23592960 | bytes 1048576 | tf_op jit(solution)/shard_map/multiple/pallas_call | solution.py:41
  22.9 1.3 %collective-permute-start.2 = (f32[3,136,512]{2,1,0:T(8,128)S(1)}, f32[3,136,512]{2,1,0:T(8,128)S(1)}, u32[]{:S(2)}, u32[]{:S(2)}) collective-permute-start(f32[3,136,512]{2,1,0:T(8,128)S(1)} %get-tuple-element.15), channel_id=1, source_target_pairs={{0,1},{1,2},{2,3},{4,5},{5,6},{6,7},{8,9},{9,10},{10,11},{12,13},{... | collective-permute-start | bytes 2506760 | tf_op jit(solution)/shard_map/ppermute | solution.py:28
  24.3 1.3 %collective-permute-start.3 = (f32[3,136,512]{2,1,0:T(8,128)S(1)}, f32[3,136,512]{2,1,0:T(8,128)S(1)}, u32[]{:S(2)}, u32[]{:S(2)}) collective-permute-start(f32[3,136,512]{2,1,0:T(8,128)S(1)} %get-tuple-element.17), channel_id=1, source_target_pairs={{1,0},{2,1},{3,2},{5,4},{6,5},{7,6},{9,8},{10,9},{11,10},{13,12},{... | collective-permute-start | bytes 2506760 | tf_op jit(solution)/shard_map/ppermute | solution.py:28
  25.6 0.6 collective-permute-done.2.left_ref
  26.2 4.2 %collective-permute-done.3.right_ref = f32[3,136,512]{2,1,0:T(8,128)S(1)} collective-permute-done((f32[3,136,512]{2,1,0:T(8,128)S(1)}, f32[3,136,512]{2,1,0:T(8,128)S(1)}, u32[]{:S(2)}, u32[]{:S(2)}) %collective-permute-start.3) | collective-permute-done | bytes 835616 | tf_op jit(solution)/shard_map/ppermute | solution.py:28
  30.4 0.0 copy-start.1
  30.4 0.9 copy-done.1
  31.3 0.0 copy-start.4
  31.3 0.7 copy-done.4
  32.0 0.0 copy-start.5
  32.0 0.7 copy-done.5
  32.7 0.0 copy-start.7
  32.7 0.7 copy-done.7
  33.3 6.9 %first.1 = (f32[9,128,512]{2,1,0:T(8,128)S(1)}, f32[9,8,128]{2,1,0:T(8,128)S(1)}, f32[16,8,128]{2,1,0:T(8,128)S(1)}, f32[8,128]{1,0:T(8,128)S(1)}) custom-call(f32[480,128]{1,0:T(8,128)S(1)} %bitcast.13, f32[2,128]{1,0:T(2,128)S(1)} %bitcast.17, f32[2,128]{1,0:T(2,128)S(1)} %bitcast.18, f32[1,128]{1,0:T(1,128)S(1)} %bitcast.20, ...), custom_call_target="tpu_custom_call" | custom-call | flops 58982400 | bytes 1048576 | tf_op jit(solution)/shard_map/first/pallas_call | solution.py:41
  40.2 22.3 %all_to_all.20.in_ref = f32[16,8,128]{2,1,0:T(8,128)S(1)} all-to-all(f32[16,8,128]{2,1,0:T(8,128)S(1)} %get-tuple-element.20), channel_id=1, replica_groups=mesh['groups'=2,'row'=4,'col'=4] {'row','col'}, dimensions={0} | all-to-all | bytes 131072 | tf_op jit(solution)/shard_map/all_to_all | solution.py:417
  62.5 9.5 %all_to_all.21.q_ref = f32[16,8,128]{2,1,0:T(8,128)S(1)} all-to-all(f32[16,8,128]{2,1,0:T(8,128)S(1)} %join.2), channel_id=1, replica_groups=mesh['groups'=2,'row'=4,'col'=4] {'row','col'}, dimensions={0} | all-to-all | bytes 131072 | tf_op jit(solution)/shard_map/all_to_all | solution.py:419
  72.0 12.1 %middle.1 = (f32[9,128,512]{2,1,0:T(8,128)S(1)}, f32[9,8,128]{2,1,0:T(8,128)S(1)}, f32[16,8,128]{2,1,0:T(8,128)S(1)}, f32[8,128]{1,0:T(8,128)S(1)}) custom-call(f32[3,136,512]{2,1,0:T(8,128)S(1)} %collective-permute-done.2.left_ref, f32[3,136,512]{2,1,0:T(8,128)S(1)} %get-tuple-element.16.mid_ref, f32[3,136,512]{2,1,0:T(8,128)S(1)} %collective-permute-done.3.right_ref, ...), custom_call_target="tpu_custom_call" | custom-call | flops 117964800 | bytes 1048576 | tf_op jit(solution)/shard_map/middle/pallas_call | solution.py:41
  84.1 9.5 %all_to_all.22.in_ref = f32[16,8,128]{2,1,0:T(8,128)S(1)} all-to-all(f32[16,8,128]{2,1,0:T(8,128)S(1)} %get-tuple-element.24), channel_id=1, replica_groups=mesh['groups'=2,'row'=4,'col'=4] {'row','col'}, dimensions={0} | all-to-all | bytes 131072 | tf_op jit(solution)/shard_map/all_to_all | solution.py:417
  93.7 9.5 %all_to_all.23.q_ref = f32[16,8,128]{2,1,0:T(8,128)S(1)} all-to-all(f32[16,8,128]{2,1,0:T(8,128)S(1)} %join.3), channel_id=1, replica_groups=mesh['groups'=2,'row'=4,'col'=4] {'row','col'}, dimensions={0} | all-to-all | bytes 131072 | tf_op jit(solution)/shard_map/all_to_all | solution.py:419
  103.1 6.1 %last.1 = (f32[480,128]{1,0:T(8,128)}, f32[6,128]{1,0:T(8,128)S(1)}) custom-call(f32[3,136,512]{2,1,0:T(8,128)S(1)} %collective-permute-done.2.left_ref, f32[3,136,512]{2,1,0:T(8,128)S(1)} %get-tuple-element.16.mid_ref, f32[3,136,512]{2,1,0:T(8,128)S(1)} %collective-permute-done.3.right_ref, f32[9,128,512]{2,1,0:T(8,128)S(1)} %get-tuple-element.22.e_ref, ...), custom_call_target="tpu_custom_call" | custom-call | flops 58982400 | bytes 1048576 | tf_op jit(solution)/shard_map/last/pallas_call | solution.py:41
  109.3 0.6 copy.11
  (2 shorter events, 0.1 us)
Async XLA Ops:
  0.6 1.0 copy-start
  1.6 0.7 copy-start.2
  2.3 0.7 copy-start.3
  3.0 0.7 copy-start.6
  4.3 11.6 %collective-permute-start.1 = (f32[136,512]{1,0:T(8,128)S(1)}, f32[136,512]{1,0:T(8,128)S(1)}, u32[]{:S(2)}, u32[]{:S(2)}) collective-permute-start(f32[136,512]{1,0:T(8,128)S(1)} %pack.1.own_ref), channel_id=1, source_target_pairs={{4,0},{8,4},{12,8},{5,1},{9,5},{13,9},{6,2},{10,6},{14,10},{7,3},{... | collective-permute-start | bytes 835592 | tf_op jit(solution)/shard_map/ppermute | solution.py:28
  5.6 11.5 %collective-permute-start = (f32[136,512]{1,0:T(8,128)S(1)}, f32[136,512]{1,0:T(8,128)S(1)}, u32[]{:S(2)}, u32[]{:S(2)}) collective-permute-start(f32[136,512]{1,0:T(8,128)S(1)} %pack.1.own_ref), channel_id=1, source_target_pairs={{0,4},{4,8},{8,12},{1,5},{5,9},{9,13},{2,6},{6,10},{10,14},{3,7},{... | collective-permute-start | bytes 835592 | tf_op jit(solution)/shard_map/ppermute | solution.py:28
  22.9 3.3 %collective-permute-start.2 = (f32[3,136,512]{2,1,0:T(8,128)S(1)}, f32[3,136,512]{2,1,0:T(8,128)S(1)}, u32[]{:S(2)}, u32[]{:S(2)}) collective-permute-start(f32[3,136,512]{2,1,0:T(8,128)S(1)} %get-tuple-element.15), channel_id=1, source_target_pairs={{0,1},{1,2},{2,3},{4,5},{5,6},{6,7},{8,9},{9,10},{10,11},{12,13},{... | collective-permute-start | bytes 2506760 | tf_op jit(solution)/shard_map/ppermute | solution.py:28
  24.3 6.1 %collective-permute-start.3 = (f32[3,136,512]{2,1,0:T(8,128)S(1)}, f32[3,136,512]{2,1,0:T(8,128)S(1)}, u32[]{:S(2)}, u32[]{:S(2)}) collective-permute-start(f32[3,136,512]{2,1,0:T(8,128)S(1)} %get-tuple-element.17), channel_id=1, source_target_pairs={{1,0},{2,1},{3,2},{5,4},{6,5},{7,6},{9,8},{10,9},{11,10},{13,12},{... | collective-permute-start | bytes 2506760 | tf_op jit(solution)/shard_map/ppermute | solution.py:28
  30.4 0.9 copy-start.1
  31.3 0.7 copy-start.4
  32.0 0.7 copy-start.5
  32.7 0.7 copy-start.7

commit v2 on v1

v2 whole, which is shorter than its diff:
```python
import functools

import jax
import jax.numpy as jnp
from jax import lax
from jax.experimental import pallas as pl
from jax.experimental.pallas import tpu as pltpu
from jax.sharding import PartitionSpec as P

BLOCK = 256
LANES = 128
FEATURES = 8
PARTS = 3
NEVER = -1e30
UNROLL = False

pseudo_count = 0.05
prior_weight = 1.0

f32 = jnp.float32
bf16 = jnp.bfloat16
i32 = jnp.int32


def shifted(x, axis, by):
    count = lax.axis_size(axis)
    pairs = [(i, i + by) for i in range(count) if 0 <= i + by < count]
    return lax.ppermute(x, axis, pairs)


def params(mib=40):
    return pltpu.CompilerParams(vmem_limit_bytes=mib << 20)


def cost(flops, size):
    return pl.CostEstimate(flops=flops, bytes_accessed=size, transcendentals=0)


def call(kernel, name, outs, in_specs, scratch, flops, args):
    shapes = [jax.ShapeDtypeStruct(s, d) for s, d in outs]
    return pl.pallas_call(
        kernel,
        name=name,
        out_shape=shapes,
        in_specs=in_specs,
        out_specs=[pl.BlockSpec(memory_space=pltpu.VMEM)] * len(shapes),
        scratch_shapes=scratch,
        compiler_params=params(),
        cost_estimate=cost(flops, 1 << 20),
    )(*args)


VMEM = pl.BlockSpec(memory_space=pltpu.VMEM)
SMEM = pl.BlockSpec(memory_space=pltpu.SMEM)
ANY = pl.BlockSpec(memory_space=pltpu.HBM)


def lane_tile(k):
    return pl.ds(k * LANES, LANES)


def padded_to(size, unit):
    return -(-size // unit) * unit


def sources(step):
    if UNROLL:
        for source in range(3):
            step(source)
    else:
        pl.loop(0, 3)(step)


def as_float(x):
    return x.astype(f32) if hasattr(x, "astype") else float(x)


def table_rows(profile, state, log_weight):
    genes, cells = profile.shape
    mu_row, mu_col, rr, rc, cc = state
    det = rr * cc - rc * rc
    rows = [jnp.log(profile)]
    if genes % 8:
        rows.append(jnp.zeros((-genes % 8, cells), f32))
    rows += [
        mu_row,
        mu_col,
        -0.5 * (cc / det),
        rc / det,
        -0.5 * (rr / det),
        log_weight - 0.5 * jnp.log(det),
        jnp.zeros((2, cells), f32),
    ]
    return jnp.concatenate(rows, axis=0)


def state_rows(state):
    return jnp.concatenate(list(state) + [jnp.zeros((3, state[0].shape[1]), f32)], axis=0)


def pack_kernel(
    count_ref, cand_hbm, pos_hbm, gene_hbm, weight_hbm, centre_hbm, spread_hbm, corr_hbm,
    out_ref, table_ref, state_ref,
    cand_ref, pos_ref, gene_ref, weight_ref, centre_ref, spread_ref, corr_ref, sems,
):
    pairs = (
        (cand_hbm, cand_ref), (pos_hbm, pos_ref), (gene_hbm, gene_ref), (weight_hbm, weight_ref),
        (centre_hbm, centre_ref), (spread_hbm, spread_ref), (corr_hbm, corr_ref),
    )
    copies = [pltpu.make_async_copy(a, b, sems.at[n]) for n, (a, b) in enumerate(pairs)]
    for copy in copies:
        copy.start()
    for copy in copies[:3]:
        copy.wait()
    tokens, slots = cand_ref.shape
    tiles = tokens // LANES
    out_ref[0:slots, :] = cand_ref[...].astype(f32).T
    lane = lax.broadcasted_iota(i32, (1, LANES), 1)
    for k in range(tiles):
        start = k * LANES
        live = (start % BLOCK + lane) < count_ref[start // BLOCK]
        rows = [
            pos_ref[k : k + 1, :],
            pos_ref[tiles + k : tiles + k + 1, :],
            gene_ref[k : k + 1, :].astype(f32),
            live.astype(f32),
            jnp.zeros((FEATURES - 4, LANES), f32),
        ]
        out_ref[slots : slots + FEATURES, lane_tile(k)] = jnp.concatenate(rows, axis=0)
    for copy in copies[3:]:
        copy.wait()
    weights = weight_ref[...]
    spread_row, spread_col = spread_ref[0:1, :], spread_ref[1:2, :]
    state = (
        centre_ref[0:1, :],
        centre_ref[1:2, :],
        spread_row * spread_row,
        corr_ref[0:1, :] * spread_row * spread_col,
        spread_col * spread_col,
    )
    state_ref[...] = state_rows(state)
    profile = weights / jnp.sum(weights, axis=0, keepdims=True)
    table_ref[...] = table_rows(profile, state, jnp.zeros_like(spread_row))


def count_source(source, z_ref, cells, outs, word_s, unit_s):
    rows, tokens = z_ref.shape
    slots = rows - FEATURES
    words = cells // 8
    shift = cells.bit_length() - 1
    word_shift = words.bit_length() - 1
    held = 3 * words // 8
    per_tile = words // 8
    sub = lax.broadcasted_iota(i32, (8, LANES), 0)
    nibbles = jnp.full((8, LANES), 0x0F0F0F0F, i32)
    for k in range(tokens // LANES):
        local = z_ref[0:slots, lane_tile(k)].astype(i32) - (2 - source) * 3 * cells
        word_s[k] = (local >> shift) * words + (local & (words - 1))
        unit_s[k] = 1 << (((local & (cells - 1)) >> word_shift) * 4)

    def some(k, start, amount, carry):
        low, high = carry
        word = [jnp.zeros((8, LANES), i32) for _ in range(held)]
        for j in range(amount):
            which = word_s[k, pl.ds(start + j, 8, stride=0), :]
            unit = unit_s[k, pl.ds(start + j, 8, stride=0), :]
            for n in range(held):
                word[n] = word[n] + jnp.where(which == sub + 8 * n, unit, 0)
        low = [a + (w & nibbles) for a, w in zip(low, word)]
        high = [a + ((w >> 4) & nibbles) for a, w in zip(high, word)]
        return low, high

    for k in range(tokens // LANES):
        zero = [jnp.zeros((8, LANES), i32) for _ in range(held)]
        whole = slots // 15
        carry = lax.fori_loop(
            0, whole, lambda g, carry: some(k, g * 15, 15, carry), (zero, list(zero))
        )
        if slots % 15:
            carry = some(k, whole * 15, slots % 15, carry)
        low, high = carry
        live = z_ref[slots + 3 : slots + 4, lane_tile(k)]
        for n in range(held):
            for field in range(8):
                part = low[n] if field % 2 == 0 else high[n]
                value = ((part >> (8 * (field // 2))) & 255).astype(f32) * live
                row = field * words + (n % per_tile) * 8
                outs[n // per_tile][row : row + 8, lane_tile(k)] = value
    for out in outs:
        out[cells : cells + FEATURES, :] = z_ref[slots : slots + FEATURES, :]


def own_counts_kernel(cells, own_ref, left_ref, mid_ref, right_ref, word_s, unit_s):
    count_source(1, own_ref, cells, (left_ref, mid_ref, right_ref), word_s, unit_s)


def counts_kernel(
    cells, up_ref, down_ref, own_left, own_mid, own_right, ltp_hbm,
    left_ref, mid_ref, right_ref, word_s, unit_s,
):
    outs = (left_ref, mid_ref, right_ref)
    for out, own in zip(outs, (own_left, own_mid, own_right)):
        out[1] = own[...]
    for source, z_ref in ((0, up_ref), (2, down_ref)):
        count_source(source, z_ref, cells, [out.at[source] for out in outs], word_s, unit_s)


def load_table(table_ref, ltp_s, par_s):
    cells = table_ref.shape[1]
    padded = ltp_s.shape[1]
    genes = table_ref.shape[0] - 8
    logs = [table_ref[0:genes, :]]
    if padded > genes:
        logs.append(jnp.zeros((padded - genes, cells), f32))
    rest = jnp.concatenate(logs, axis=0).T
    for part in range(PARTS):
        piece = rest.astype(bf16)
        ltp_s[part * cells : (part + 1) * cells, :] = piece
        if part + 1 < PARTS:
            rest = rest - piece.astype(f32)
    rows = [table_ref[genes : genes + 8, :], jnp.zeros((LANES - 8, cells), f32)]
    columns = jnp.concatenate(rows, axis=0).T
    for n in range(6):
        par_s[n] = jnp.broadcast_to(columns[:, n : n + 1], (cells, LANES))


def tables_kernel(left_ref, own_ref, right_ref, ltp_ref, par_ref):
    for side, table in enumerate((left_ref, own_ref, right_ref)):
        load_table(table, ltp_ref.at[side], par_ref.at[side])


def gene_hot(x_ref, source, cells, padded):
    tokens = x_ref.shape[2]
    gene = x_ref[source, cells + 2 : cells + 3, :].astype(i32)
    axis = lax.broadcasted_iota(i32, (padded, tokens), 0)
    return jnp.where(axis == gene, 1.0, 0.0).astype(bf16)


def features(x_ref, source, cells, row_step, col_step):
    y0 = x_ref[source, cells : cells + 1, :] + row_step
    y1 = x_ref[source, cells + 1 : cells + 2, :] + col_step
    return y0, y1


def score_rows(at, y0, y1, gl_s, par_s, cells):
    tiles = y0.shape[1] // LANES
    p = [jnp.concatenate([par_s[n, at : at + 8, :]] * tiles, axis=1) for n in range(6)]
    d0 = y0 - p[0]
    d1 = y1 - p[1]
    logs = gl_s[at : at + 8, :]
    for part in range(1, PARTS):
        logs = logs + gl_s[part * cells + at : part * cells + at + 8, :]
    return logs + p[5] + (d0 * (p[2] * d0 + p[3] * d1) + p[4] * d1 * d1)


def row_of(ref, index, first, tiles):
    return jnp.concatenate([ref[index + (pl.ds(first + k, 1), slice(None))] for k in range(tiles)], axis=1)


def to_tiles(row):
    return jnp.concatenate([row[:, k * LANES : (k + 1) * LANES] for k in range(row.shape[1] // LANES)], axis=0)


def spread_rows(part_s, out_ref):
    rows = out_ref.shape[0]
    half = part_s.shape[-2] // 2
    shape = out_ref.shape[2:]
    level = lax.broadcasted_iota(i32, shape, len(shape) - 2)
    nothing = jnp.where(level < half, NEVER, 0.0)
    row = lax.axis_index("row")

    @pl.loop(0, rows)
    def _(at):
        for slot in range(3):
            source = at - row + slot
            inside = (source >= 0) & (source < 3)
            out_ref[at, slot] = jnp.where(inside, part_s[jnp.clip(source, 0, 2)], nothing)


def joined(parts):
    half = parts[0].shape[-2] // 2
    tops = [p[..., 0:half, :] for p in parts]
    top = functools.reduce(jnp.maximum, tops)
    total = sum(p[..., half:, :] * jnp.exp(m - top) for p, m in zip(parts, tops))
    return top, total


def gather_rows(in_ref):
    rows = in_ref.shape[0]
    row = lax.axis_index("row")
    shape = in_ref.shape[1:]
    half = shape[-2] // 2
    level = lax.broadcasted_iota(i32, shape, len(shape) - 2)
    nothing = jnp.where(level < half, NEVER, 0.0)
    parts = []
    for step in range(-2, 3):
        inside = (row + step >= 0) & (row + step < rows)
        parts.append(jnp.where(inside, in_ref[jnp.clip(row + step, 0, rows - 1)], nothing))
    return joined(parts)


def told(top, total):
    return jnp.concatenate([top, jnp.where(total > 0.0, 1.0 / total, 0.0)], axis=-2)


def row_parts_kernel(
    left_ref, mid_ref, right_ref, ltp_s, par_s, out_ref, part_s, gl_s, sc_s
):
    x_refs = (left_ref, mid_ref, right_ref)
    cells, tokens = sc_s.shape[1:]

    def step(source):
        hot = gene_hot(mid_ref, source, cells, ltp_s.shape[2])
        for side in range(3):
            gl_s[side] = jnp.dot(ltp_s[side], hot, preferred_element_type=f32)
        top = jnp.full((8, tokens), NEVER, f32)
        for side in range(3):
            y0, y1 = features(mid_ref, source, cells, as_float(source) - 1.0, 1.0 - side)
            for at in range(0, cells, 8):
                score = score_rows(at, y0, y1, gl_s.at[side], par_s.at[side], cells)
                score = jnp.where(x_refs[side][source, at : at + 8, :] > 0.0, score, NEVER)
                sc_s[side, at : at + 8, :] = score
                top = jnp.maximum(top, score)
        top = jnp.max(top, axis=0, keepdims=True)
        total = jnp.zeros((8, tokens), f32)
        for side in range(3):
            for at in range(0, cells, 8):
                count = x_refs[side][source, at : at + 8, :]
                total = total + count * jnp.exp(sc_s[side, at : at + 8, :] - top)
        total = jnp.sum(total, axis=0, keepdims=True)
        part_s[source] = jnp.concatenate([to_tiles(top), to_tiles(total)], axis=0)

    sources(step)
    spread_rows(part_s, out_ref)


def row_join_kernel(in_ref, out_ref):
    out_ref[...] = told(*gather_rows(in_ref))


def part_join_kernel(in_ref, out_ref):
    out_ref[...] = jnp.concatenate(gather_rows(in_ref), axis=-2)


def add_moments(p, y0, y1, sums):
    def fold(x):
        parts = [x[:, k * LANES : (k + 1) * LANES] for k in range(x.shape[1] // LANES)]
        return functools.reduce(jnp.add, parts)

    weights = (None, y0, y1, y0 * y0, y0 * y1, y1 * y1)
    return [s + fold(p if w is None else p * w) for s, w in zip(sums, weights)]


def add_counts(hot, sh_s, cnt_s):
    cnt_s[...] += lax.dot_general(hot, sh_s[...], (((1,), (1,)), ((), ())), preferred_element_type=f32)


def new_cells(genes, mom_s, cnt_s, state_ref):
    weight, s0, s1, s00, s01, s11 = [jnp.sum(mom_s[n].T, axis=0, keepdims=True) for n in range(6)]
    mu_row, mu_col, rr, rc, cc = [state_ref[n : n + 1, :] for n in range(5)]
    counts = cnt_s[0:genes, :]
    profile = (counts + pseudo_count) / (
        jnp.sum(counts, axis=0, keepdims=True) + genes * pseudo_count
    )
    denominator = weight + prior_weight
    new_row = (s0 + prior_weight * mu_row) / denominator
    new_col = (s1 + prior_weight * mu_col) / denominator
    q_rr = s00 - 2.0 * new_row * s0 + weight * new_row * new_row
    q_rc = s01 - new_row * s1 - new_col * s0 + weight * new_row * new_col
    q_cc = s11 - 2.0 * new_col * s1 + weight * new_col * new_col
    state = (
        new_row,
        new_col,
        (q_rr + prior_weight * rr) / denominator,
        (q_rc + prior_weight * rc) / denominator,
        (q_cc + prior_weight * cc) / denominator,
    )
    return profile, state, jnp.log(weight + 1.0)


def middle_kernel(
    genes,
    left_ref, mid_ref, right_ref, ltp_ref, par_ref, state_ref, told_ref,
    e_ref, m_ref, out_ref, state_out,
    hot_s, sh_s, mom_s, cnt_s, ltp_s, par_s, gl_s, sc_s, table_s, part_s,
):
    x_refs = (left_ref, mid_ref, right_ref)
    cells, tokens = sc_s.shape[1:]
    tiles = tokens // LANES
    padded = cnt_s.shape[0]
    cols = told_ref.shape[0]
    col = lax.axis_index("col")
    mom_s[...] = jnp.zeros(mom_s.shape, f32)
    cnt_s[...] = jnp.zeros(cnt_s.shape, f32)

    def posterior(source):
        for side, x_ref in enumerate(x_refs):
            hot_s[source, side] = gene_hot(x_ref, source, cells, padded)
            gl_s[side] = jnp.dot(ltp_ref[1], hot_s[source, side], preferred_element_type=f32)
        for side, x_ref in enumerate(x_refs):
            at_col = jnp.clip(col + side - 1, 0, cols - 1)
            top = row_of(told_ref, (at_col, source), 0, tiles)
            factor = row_of(told_ref, (at_col, source), tiles, tiles)
            y0, y1 = features(x_ref, source, cells, as_float(source) - 1.0, side - 1.0)
            for at in range(0, cells, 16):
                halves = []
                for a in (at, at + 8):
                    score = score_rows(a, y0, y1, gl_s.at[side], par_ref.at[1], cells)
                    count = x_ref[source, a : a + 8, :]
                    p = count * jnp.exp(jnp.minimum(score - top, 0.0)) * factor
                    sums = [mom_s[n, a : a + 8, :] for n in range(6)]
                    sums = add_moments(p, y0, y1, sums)
                    for n in range(6):
                        mom_s[n, a : a + 8, :] = sums[n]
                    halves.append(p)
                sh_s[side, at : at + 16, :] = jnp.concatenate(halves, axis=0).astype(bf16)
            add_counts(hot_s[source, side], sh_s.at[side], cnt_s)

    sources(posterior)
    profile, state, log_weight = new_cells(genes, mom_s, cnt_s, state_ref)
    state_out[...] = state_rows(state)
    table_s[...] = table_rows(profile, state, log_weight)
    load_table(table_s, ltp_s, par_s)

    def score(source):
        for side in range(3):
            gl_s[side] = jnp.dot(ltp_s[...], hot_s[source, side], preferred_element_type=f32)
        for side, x_ref in enumerate(x_refs):
            y0, y1 = features(x_ref, source, cells, as_float(source) - 1.0, side - 1.0)
            top = jnp.full((8, tokens), NEVER, f32)
            for at in range(0, cells, 8):
                value = score_rows(at, y0, y1, gl_s.at[side], par_s, cells)
                value = jnp.where(x_ref[source, at : at + 8, :] > 0.0, value, NEVER)
                sc_s[side, at : at + 8, :] = value
                top = jnp.maximum(top, value)
            top = jnp.max(top, axis=0, keepdims=True)
            total = jnp.zeros((8, tokens), f32)
            for at in range(0, cells, 8):
                e = x_ref[source, at : at + 8, :] * jnp.exp(sc_s[side, at : at + 8, :] - top)
                e_ref[source, side, at : at + 8, :] = e
                total = total + e
            total = jnp.sum(total, axis=0, keepdims=True)
            part_s[source, side] = jnp.concatenate([to_tiles(top), to_tiles(total)], axis=0)

    sources(score)
    m_ref[...] = part_s[...]
    spread_rows(part_s, out_ref)


def last_kernel(
    genes,
    left_ref, mid_ref, right_ref, e_ref, m_ref, told_ref, state_ref,
    profile_ref, cells_ref,
    sh_s, mom_s, cnt_s,
):
    x_refs = (left_ref, mid_ref, right_ref)
    cells, tokens = sh_s.shape[1:]
    tiles = tokens // LANES
    cols = told_ref.shape[0]
    col = lax.axis_index("col")
    mom_s[...] = jnp.zeros(mom_s.shape, f32)
    cnt_s[...] = jnp.zeros(cnt_s.shape, f32)
    shape = m_ref.shape[2:]
    nothing = jnp.where(lax.broadcasted_iota(i32, shape, 0) < shape[0] // 2, NEVER, 0.0)

    def posterior(source):
        for side, x_ref in enumerate(x_refs):
            parts = []
            for step in range(-1, 2):
                owner = col + side - 1 + step
                inside = (owner >= 0) & (owner < cols)
                part = told_ref[jnp.clip(owner, 0, cols - 1), source, 1 - step]
                parts.append(jnp.where(inside, part, nothing))
            top, total = joined(parts)
            scale = jnp.exp(m_ref[source, side][0:tiles] - top)
            scale = jnp.where(total > 0.0, scale / total, 0.0)
            factor = jnp.concatenate([scale[k : k + 1, :] for k in range(tiles)], axis=1)
            y0, y1 = features(x_ref, source, cells, as_float(source) - 1.0, side - 1.0)
            for at in range(0, cells, 16):
                halves = []
                for a in (at, at + 8):
                    p = e_ref[source, side, a : a + 8, :] * factor
                    sums = [mom_s[n, a : a + 8, :] for n in range(6)]
                    sums = add_moments(p, y0, y1, sums)
                    for n in range(6):
                        mom_s[n, a : a + 8, :] = sums[n]
                    halves.append(p)
                sh_s[side, at : at + 16, :] = jnp.concatenate(halves, axis=0).astype(bf16)
            add_counts(gene_hot(x_ref, source, cells, cnt_s.shape[0]), sh_s.at[side], cnt_s)

    sources(posterior)
    profile, state, log_weight = new_cells(genes, mom_s, cnt_s, state_ref)
    profile_ref[...] = jnp.log(profile)
    mu_row, mu_col, rr, rc, cc = state
    final = (mu_row, mu_col, 0.5 * jnp.log(rr), 0.5 * jnp.log(cc), rc / jnp.sqrt(rr * cc), log_weight)
    for n, row in enumerate(final):
        cells_ref[n] = row


def body(
    positions, genes, candidates, block_counts, profile_weights, centroids, spreads, correlation
):
    gene_total = profile_weights.shape[0]
    cells = profile_weights.shape[3]
    tokens, slots = candidates.shape[2:]
    tiles = tokens // LANES
    rows = lax.axis_size("row")
    padded = padded_to(gene_total, LANES)
    pairs = 9 * tokens * cells
    table = ((padded_to(gene_total, 8) + 8, cells), f32)
    state = ((8, cells), f32)
    vmem = pltpu.VMEM

    packed, table_own, state_own = call(
        pack_kernel, "pack", [((slots + FEATURES, tokens), f32), table, state],
        [SMEM] + [ANY] * 7,
        [
            vmem((tokens, slots), i32),
            vmem((2 * tiles, LANES), f32),
            vmem((tiles, LANES), i32),
            vmem((gene_total, cells), f32),
            vmem((2, cells), f32),
            vmem((2, cells), f32),
            vmem((1, cells), f32),
            pltpu.SemaphoreType.DMA((7,)),
        ],
        tokens * slots,
        (
            block_counts.reshape(-1),
            candidates.reshape(tokens, slots),
            positions.reshape(2 * tiles, LANES),
            genes.reshape(tiles, LANES),
            profile_weights.reshape(gene_total, cells),
            centroids.reshape(2, cells),
            spreads.reshape(2, cells),
            correlation.reshape(1, cells),
        ),
    )
    from_up = shifted(packed, "row", 1)
    from_down = shifted(packed, "row", -1)
    table_left = shifted(table_own, "col", 1)
    table_right = shifted(table_own, "col", -1)
    ltp, par = call(
        tables_kernel, "tables",
        [((3, PARTS * cells, padded), bf16), ((3, 6, cells, LANES), f32)], [VMEM] * 3, [],
        tokens * slots, (table_left, table_own, table_right),
    )
    one = ((cells + FEATURES, tokens), f32)
    three = ((3, cells + FEATURES, tokens), f32)
    count_scratch = [vmem((tiles, slots, LANES), i32)] * 2
    own = call(
        functools.partial(own_counts_kernel, cells), "own_counts", [one] * 3, [VMEM],
        count_scratch, pairs * 40, (packed,),
    )
    to_left, mid, to_right = call(
        functools.partial(counts_kernel, cells), "counts", [three] * 3, [VMEM] * 5 + [ANY],
        count_scratch, pairs * 80, (from_up, from_down, *own, ltp),
    )
    from_right = shifted(to_left, "col", -1)
    from_left = shifted(to_right, "col", 1)

    chunk = (2 * tiles, LANES)
    parts, = call(
        row_parts_kernel, "row_parts", [((rows, 3) + chunk, f32)], [VMEM] * 5,
        [
            vmem((3,) + chunk, f32),
            vmem((3, PARTS * cells, tokens), f32),
            vmem((3, cells, tokens), f32),
        ],
        pairs * 100,
        (to_left, mid, to_right, ltp, par),
    )
    back = lax.all_to_all(parts, "row", 0, 0)
    sums, = call(row_join_kernel, "row_join", [((3,) + chunk, f32)], [VMEM], [], tokens * 100, (back,))
    told_all = lax.all_gather(sums, "col", axis=0)

    x = (from_left, mid, from_right)
    sum_scratch = [
        vmem((3, cells, tokens), bf16),
        vmem((6, cells, LANES), f32),
        vmem((padded, cells), f32),
    ]
    e, m, parts, state_own = call(
        functools.partial(middle_kernel, gene_total), "middle",
        [((3, 3, cells, tokens), f32), ((3, 3) + chunk, f32), ((rows, 3, 3) + chunk, f32), state],
        [VMEM] * 7,
        [vmem((3, 3, padded, tokens), bf16)] + sum_scratch + [
            vmem((PARTS * cells, padded), bf16),
            vmem((6, cells, LANES), f32),
            vmem((3, PARTS * cells, tokens), f32),
            vmem((3, cells, tokens), f32),
            vmem(*table),
            vmem((3, 3) + chunk, f32),
        ],
        pairs * 200,
        (*x, ltp, par, state_own, told_all),
    )
    back = lax.all_to_all(parts, "row", 0, 0)
    sums, = call(part_join_kernel, "part_join", [((3, 3) + chunk, f32)], [VMEM], [], tokens * 100, (back,))
    told_all = lax.all_gather(sums, "col", axis=0)
    final_profile, final_cells = call(
        functools.partial(last_kernel, gene_total), "last",
        [((gene_total, cells), f32), ((6, 1, cells), f32)],
        [VMEM] * 7, sum_scratch, pairs * 100,
        (*x, e, m, told_all, state_own),
    )
    return (final_profile.reshape(gene_total, 1, 1, cells), final_cells.reshape(6, 1, 1, cells))


def solution(mesh):
    tiles = P(("groups", "row"), "col")
    stacked = P(None, ("groups", "row"), "col", None)
    return jax.shard_map(
        body,
        mesh=mesh,
        in_specs=(
            stacked,
            P(("groups", "row"), "col", None),
            P(("groups", "row"), "col", None, None),
            P(("groups", "row"), "col", None),
            stacked,
            stacked,
            stacked,
            P(("groups", "row"), "col", None),
        ),
        out_specs=(stacked, stacked),
        check_vma=False,
    )
```

time: 110 us -> 80.3 us (0.73)
  blocking collectives: 50.7 us -> 32.5 us
  waiting for transfers between devices: 10.7 us -> 0.02 us
  Pallas kernels: 31.7 us -> 23.3 us
  starting transfers between devices: 9.53 us -> 17.3 us
    all_to_all x4 -> x2, blocking collectives: 50.7 us -> 18.9 us  [body(): back = lax.all_to_all(parts, 'row', 0, 0)]
    all_gather x0 -> x2, blocking collectives: none -> 13.5 us  [body(): told_all = lax.all_gather(sums, 'col', axis=0)]
    ppermute x4 -> x6, waiting for transfers between devices: 10.7 us -> 0.02 us  [shifted(): return lax.ppermute(x, axis, pairs)]
    pallas_call x7 -> x9, Pallas kernels: 31.7 us -> 23.3 us  [call(): pl.pallas_call(kernel, name=name, out_shape=shapes, in_specs=in_specs, ou...]
    ppermute x4 -> x6, starting transfers between devices: 9.53 us -> 17.3 us  [shifted(): return lax.ppermute(x, axis, pairs)]
    unnamed x17 -> x16, local copies, waits for them, and re-layouts: 6.5 us -> 5.92 us
  transfers between devices with their start and end apart: 4 -> 6, of which waited for: 4 -> 0; matrix products, arithmetic and copies ran while one was open for 0% -> 0% of each run, Pallas kernels for 0% -> 7%
where the time goes in v2:
time: 80.3 us; the launch traced here: 79.8 us
  blocking collectives  32.5 us (40%)
  Pallas kernels  23.3 us (29%)
  starting transfers between devices  17.3 us (22%)
  local copies, waits for them, and re-layouts  5.92 us (7%)
    pallas_call x9, Pallas kernels, call(): pl.pallas_call(kernel, name=name, out_shape=shapes, in_specs=in_specs, ou...  23.3 us
    all_to_all x2, blocking collectives, body(): back = lax.all_to_all(parts, 'row', 0, 0)  18.9 us
    ppermute x6, starting transfers between devices, shifted(): return lax.ppermute(x, axis, pairs)  17.3 us
    all_gather x2, blocking collectives, body(): told_all = lax.all_gather(sums, 'col', axis=0)  13.5 us
    unnamed x16, local copies, waits for them, and re-layouts  5.92 us
  transfers between devices with their start and end apart: 6, of which 0 were waited for; matrix products, arithmetic and copies ran while one was open for 0% of the time, Pallas kernels for 7%

profile of v2, /device:TPU:0, one launch (start us, length us, event | category | flops | bytes accessed | tf_op | source)
XLA Modules:
  0.0 79.8 jit_solution(2870720473680720919)
XLA Ops:
  0.6 0.0 copy-start
  0.6 0.9 %copy-done = s32[1,1,512,128]{3,2,1,0:T(8,128)S(1)} copy-done((s32[1,1,512,128]{3,2,1,0:T(8,128)S(1)}, s32[1,1,512,128]{3,2,1,0:T(8,128)}, u32[]{:S(2)}) %copy-start) | copy-done | bytes 262168
  1.6 0.0 copy-start.1
  1.6 0.9 %copy-done.1 = f32[480,1,1,128]{3,2,1,0:T(1,128)S(1)} copy-done((f32[480,1,1,128]{3,2,1,0:T(1,128)S(1)}, f32[480,1,1,128]{3,2,1,0:T(1,128)}, u32[]{:S(2)}) %copy-start.1) | copy-done | bytes 245784
  2.5 0.0 copy-start.2
  2.5 0.7 copy-done.2
  3.2 0.0 copy-start.3
  3.2 0.7 copy-done.3
  3.9 0.0 copy-start.4
  3.9 0.7 copy-done.4
  4.6 0.0 copy-start.5
  4.6 0.7 copy-done.5
  5.3 0.0 copy-start.6
  5.3 0.7 copy-done.6
  5.9 0.0 copy-start.7
  5.9 0.7 copy-done.7
  6.6 1.2 %pack.1 = (f32[136,512]{1,0:T(8,128)S(1)}, f32[488,128]{1,0:T(8,128)S(1)}, f32[8,128]{1,0:T(8,128)S(1)}) custom-call(s32[2]{0:T(128)S(1)} %bitcast.24, s32[512,128]{1,0:T(8,128)S(1)} %bitcast.17, f32[8,128]{1,0:T(8,128)S(1)} %bitcast.20, s32[4,128]{1,0:T(4,128)S(1)} %bitcast.21, f32[480,128]{1,0:T(8,128)S(1)} %bitcast.18, f32[2,128]{1,0:T(2,128)S(1)} %bitcast.22, ...), custom_call_target="tpu_custom_call" | custom-call | flops 65536 | bytes 1048576 | tf_op jit(solution)/shard_map/pack/pallas_call | solution.py:41
  7.8 1.3 %collective-permute-start.1 = (f32[136,512]{1,0:T(8,128)S(1)}, f32[136,512]{1,0:T(8,128)S(1)}, u32[]{:S(2)}, u32[]{:S(2)}) collective-permute-start(f32[136,512]{1,0:T(8,128)S(1)} %get-tuple-element.19.own_ref), channel_id=1, source_target_pairs={{4,0},{8,4},{12,8},{5,1},{9,5},{13,9},{6,2},{10,6},{14,10},{7,3},{... | collective-permute-start | bytes 835592 | tf_op jit(solution)/shard_map/ppermute | solution.py:28
  9.1 5.6 %collective-permute-start = (f32[136,512]{1,0:T(8,128)S(1)}, f32[136,512]{1,0:T(8,128)S(1)}, u32[]{:S(2)}, u32[]{:S(2)}) collective-permute-start(f32[136,512]{1,0:T(8,128)S(1)} %get-tuple-element.19.own_ref), channel_id=1, source_target_pairs={{0,4},{4,8},{8,12},{1,5},{5,9},{9,13},{2,6},{6,10},{10,14},{3,7},{... | collective-permute-start | bytes 835592 | tf_op jit(solution)/shard_map/ppermute | solution.py:28
  14.7 1.3 %collective-permute-start.3 = (f32[488,128]{1,0:T(8,128)S(1)}, f32[488,128]{1,0:T(8,128)S(1)}, u32[]{:S(2)}, u32[]{:S(2)}) collective-permute-start(f32[488,128]{1,0:T(8,128)S(1)} %get-tuple-element.23.own_ref), channel_id=1, source_target_pairs={{1,0},{2,1},{3,2},{5,4},{6,5},{7,6},{9,8},{10,9},{11,10},{13,12},{... | collective-permute-start | bytes 749576 | tf_op jit(solution)/shard_map/ppermute | solution.py:28
  16.0 3.0 %collective-permute-start.2 = (f32[488,128]{1,0:T(8,128)S(1)}, f32[488,128]{1,0:T(8,128)S(1)}, u32[]{:S(2)}, u32[]{:S(2)}) collective-permute-start(f32[488,128]{1,0:T(8,128)S(1)} %get-tuple-element.23.own_ref), channel_id=1, source_target_pairs={{0,1},{1,2},{2,3},{4,5},{5,6},{6,7},{8,9},{9,10},{10,11},{12,13},{... | collective-permute-start | bytes 749576 | tf_op jit(solution)/shard_map/ppermute | solution.py:28
  19.0 1.8 %own_counts.1 = (f32[136,512]{1,0:T(8,128)S(1)}, f32[136,512]{1,0:T(8,128)S(1)}, f32[136,512]{1,0:T(8,128)S(1)}) custom-call(f32[136,512]{1,0:T(8,128)S(1)} %get-tuple-element.19.own_ref), custom_call_target="tpu_custom_call" | custom-call | flops 23592960 | bytes 1048576 | tf_op jit(solution)/shard_map/own_counts/pallas_call | solution.py:41
  20.9 0.0 collective-permute-done.3.right_ref
  20.9 0.0 collective-permute-done.2.left_ref
  20.9 0.7 tables.1
  21.6 0.0 collective-permute-done.1.down_ref
  21.6 0.0 collective-permute-done.up_ref
  21.6 3.7 %counts.1 = (f32[3,136,512]{2,1,0:T(8,128)S(1)}, f32[3,136,512]{2,1,0:T(8,128)S(1)}, f32[3,136,512]{2,1,0:T(8,128)S(1)}) custom-call(f32[136,512]{1,0:T(8,128)S(1)} %collective-permute-done.up_ref, f32[136,512]{1,0:T(8,128)S(1)} %collective-permute-done.1.down_ref, f32[136,512]{1,0:T(8,128)S(1)} %get-tuple-element.20.own_left, ...), custom_call_target="tpu_custom_call" | custom-call | flops 47185920 | bytes 1048576 | tf_op jit(solution)/shard_map/counts/pallas_call | solution.py:41
  25.4 4.8 %collective-permute-start.4 = (f32[3,136,512]{2,1,0:T(8,128)S(1)}, f32[3,136,512]{2,1,0:T(8,128)S(1)}, u32[]{:S(2)}, u32[]{:S(2)}) collective-permute-start(f32[3,136,512]{2,1,0:T(8,128)S(1)} %get-tuple-element.25.right_ref), channel_id=1, source_target_pairs={{0,1},{1,2},{2,3},{4,5},{5,6},{6,7},{8,9},{9,10},{10,11},{12,13},{... | collective-permute-start | bytes 2506760 | tf_op jit(solution)/shard_map/ppermute | solution.py:28
  30.2 1.3 %collective-permute-start.5 = (f32[3,136,512]{2,1,0:T(8,128)S(1)}, f32[3,136,512]{2,1,0:T(8,128)S(1)}, u32[]{:S(2)}, u32[]{:S(2)}) collective-permute-start(f32[3,136,512]{2,1,0:T(8,128)S(1)} %get-tuple-element.27.left_ref), channel_id=1, source_target_pairs={{1,0},{2,1},{3,2},{5,4},{6,5},{7,6},{9,8},{10,9},{11,10},{13,12},{... | collective-permute-start | bytes 2506760 | tf_op jit(solution)/shard_map/ppermute | solution.py:28
  31.5 3.3 %row_parts.1 = f32[4,3,8,128]{3,2,1,0:T(8,128)S(1)} custom-call(f32[3,136,512]{2,1,0:T(8,128)S(1)} %get-tuple-element.27.left_ref, f32[3,136,512]{2,1,0:T(8,128)S(1)} %get-tuple-element.26.mid_ref, f32[3,136,512]{2,1,0:T(8,128)S(1)} %get-tuple-element.25.right_ref, bf16[3,384,512]{2,1,0:T(8,128)(2,1)S(1)} %get-tuple-element.24.ltp_hbm.ltp_s.ltp_ref, ...), custom_call_target="tpu_custom_call" | custom-call | flops 58982400 | bytes 1048576 | tf_op jit(solution)/shard_map/row_parts/pallas_call | solution.py:41
  34.8 9.4 %all_to_all.10.in_ref = f32[4,3,8,128]{3,2,1,0:T(8,128)S(1)} all-to-all(f32[4,3,8,128]{3,2,1,0:T(8,128)S(1)} %row_parts.1), channel_id=1, replica_groups=mesh['groups'=2,'row'=4,'col'=4] {'row'}, dimensions={0} | all-to-all | bytes 98304 | tf_op jit(solution)/shard_map/all_to_all | solution.py:573
  44.2 7.9 %all-gather = f32[12,8,128]{2,1,0:T(8,128)S(1)} all-gather(f32[3,8,128]{2,1,0:T(8,128)S(1)} %row_join.1), channel_id=2, replica_groups=mesh['groups'=2,'row'=4,'col'=4] {'col'}, dimensions={0}, use_global_device_ids=true | all-gather | bytes 61440 | tf_op jit(solution)/shard_map/all_gather | solution.py:575
  52.1 0.0 collective-permute-done.4.left_ref
  52.1 0.0 collective-permute-done.5.right_ref
  52.1 8.9 %middle.1 = (f32[3,3,128,512]{3,2,1,0:T(8,128)S(1)}, f32[3,3,8,128]{3,2,1,0:T(8,128)S(1)}, f32[4,3,3,8,128]{4,3,2,1,0:T(8,128)S(1)}, f32[8,128]{1,0:T(8,128)S(1)}) custom-call(f32[3,136,512]{2,1,0:T(8,128)S(1)} %collective-permute-done.4.left_ref, f32[3,136,512]{2,1,0:T(8,128)S(1)} %get-tuple-element.26.mid_ref, ...), custom_call_target="tpu_custom_call" | custom-call | flops 117964800 | bytes 1048576 | tf_op jit(solution)/shard_map/middle/pallas_call | solution.py:41
  61.0 9.6 %all_to_all.11.in_ref = f32[4,3,3,8,128]{4,3,2,1,0:T(8,128)S(1)} all-to-all(f32[4,3,3,8,128]{4,3,2,1,0:T(8,128)S(1)} %get-tuple-element.32), channel_id=1, replica_groups=mesh['groups'=2,'row'=4,'col'=4] {'row'}, dimensions={0} | all-to-all | bytes 294912 | tf_op jit(solution)/shard_map/all_to_all | solution.py:598
  70.6 0.1 part_join.1
  70.6 5.6 %all-gather.1 = f32[12,3,8,128]{3,2,1,0:T(8,128)S(1)} all-gather(f32[3,3,8,128]{3,2,1,0:T(8,128)S(1)} %part_join.1), channel_id=3, replica_groups=mesh['groups'=2,'row'=4,'col'=4] {'col'}, dimensions={0}, use_global_device_ids=true | all-gather | bytes 184320 | tf_op jit(solution)/shard_map/all_gather | solution.py:600
  76.2 3.5 %last.1 = (f32[480,128]{1,0:T(8,128)}, f32[6,1,128]{2,1,0:T(1,128)}) custom-call(f32[3,136,512]{2,1,0:T(8,128)S(1)} %collective-permute-done.4.left_ref, f32[3,136,512]{2,1,0:T(8,128)S(1)} %get-tuple-element.26.mid_ref, f32[3,136,512]{2,1,0:T(8,128)S(1)} %collective-permute-done.5.right_ref, f32[3,3,128,512]{3,2,1,0:T(8,128)S(1)} %get-tuple-element.30.e_ref, ...), custom_call_target="tpu_custom_call" | custom-call | flops 58982400 | bytes 1048576 | tf_op jit(solution)/shard_map/last/pallas_call | solution.py:41
  (1 shorter events, 0.0 us)
Async XLA Ops:
  0.6 1.0 %copy-start = (s32[1,1,512,128]{3,2,1,0:T(8,128)S(1)}, s32[1,1,512,128]{3,2,1,0:T(8,128)}, u32[]{:S(2)}) copy-start(s32[1,1,512,128]{3,2,1,0:T(8,128)} %param.10) | copy-start | bytes 786436
  1.6 0.9 %copy-start.1 = (f32[480,1,1,128]{3,2,1,0:T(1,128)S(1)}, f32[480,1,1,128]{3,2,1,0:T(1,128)}, u32[]{:S(2)}) copy-start(f32[480,1,1,128]{3,2,1,0:T(1,128)} %param.12) | copy-start | bytes 737284
  2.5 0.7 copy-start.2
  3.2 0.7 copy-start.3
  3.9 0.7 copy-start.4
  4.6 0.7 copy-start.5
  5.3 0.7 copy-start.6
  5.9 0.7 copy-start.7
  7.8 13.8 %collective-permute-start.1 = (f32[136,512]{1,0:T(8,128)S(1)}, f32[136,512]{1,0:T(8,128)S(1)}, u32[]{:S(2)}, u32[]{:S(2)}) collective-permute-start(f32[136,512]{1,0:T(8,128)S(1)} %get-tuple-element.19.own_ref), channel_id=1, source_target_pairs={{4,0},{8,4},{12,8},{5,1},{9,5},{13,9},{6,2},{10,6},{14,10},{7,3},{... | collective-permute-start | bytes 835592 | tf_op jit(solution)/shard_map/ppermute | solution.py:28
  9.1 12.6 %collective-permute-start = (f32[136,512]{1,0:T(8,128)S(1)}, f32[136,512]{1,0:T(8,128)S(1)}, u32[]{:S(2)}, u32[]{:S(2)}) collective-permute-start(f32[136,512]{1,0:T(8,128)S(1)} %get-tuple-element.19.own_ref), channel_id=1, source_target_pairs={{0,4},{4,8},{8,12},{1,5},{5,9},{9,13},{2,6},{6,10},{10,14},{3,7},{... | collective-permute-start | bytes 835592 | tf_op jit(solution)/shard_map/ppermute | solution.py:28
  14.7 6.2 %collective-permute-start.3 = (f32[488,128]{1,0:T(8,128)S(1)}, f32[488,128]{1,0:T(8,128)S(1)}, u32[]{:S(2)}, u32[]{:S(2)}) collective-permute-start(f32[488,128]{1,0:T(8,128)S(1)} %get-tuple-element.23.own_ref), channel_id=1, source_target_pairs={{1,0},{2,1},{3,2},{5,4},{6,5},{7,6},{9,8},{10,9},{11,10},{13,12},{... | collective-permute-start | bytes 749576 | tf_op jit(solution)/shard_map/ppermute | solution.py:28
  16.0 4.9 %collective-permute-start.2 = (f32[488,128]{1,0:T(8,128)S(1)}, f32[488,128]{1,0:T(8,128)S(1)}, u32[]{:S(2)}, u32[]{:S(2)}) collective-permute-start(f32[488,128]{1,0:T(8,128)S(1)} %get-tuple-element.23.own_ref), channel_id=1, source_target_pairs={{0,1},{1,2},{2,3},{4,5},{5,6},{6,7},{8,9},{9,10},{10,11},{12,13},{... | collective-permute-start | bytes 749576 | tf_op jit(solution)/shard_map/ppermute | solution.py:28
  25.4 26.7 %collective-permute-start.4 = (f32[3,136,512]{2,1,0:T(8,128)S(1)}, f32[3,136,512]{2,1,0:T(8,128)S(1)}, u32[]{:S(2)}, u32[]{:S(2)}) collective-permute-start(f32[3,136,512]{2,1,0:T(8,128)S(1)} %get-tuple-element.25.right_ref), channel_id=1, source_target_pairs={{0,1},{1,2},{2,3},{4,5},{5,6},{6,7},{8,9},{9,10},{10,11},{12,13},{... | collective-permute-start | bytes 2506760 | tf_op jit(solution)/shard_map/ppermute | solution.py:28
  30.2 21.9 %collective-permute-start.5 = (f32[3,136,512]{2,1,0:T(8,128)S(1)}, f32[3,136,512]{2,1,0:T(8,128)S(1)}, u32[]{:S(2)}, u32[]{:S(2)}) collective-permute-start(f32[3,136,512]{2,1,0:T(8,128)S(1)} %get-tuple-element.27.left_ref), channel_id=1, source_target_pairs={{1,0},{2,1},{3,2},{5,4},{6,5},{7,6},{9,8},{10,9},{11,10},{13,12},{... | collective-permute-start | bytes 2506760 | tf_op jit(solution)/shard_map/ppermute | solution.py:28

commit v3 on v2

--- a/solution.py
+++ b/solution.py
@@ -10,9 +10,9 @@
 BLOCK = 256
 LANES = 128
 FEATURES = 8
-PARTS = 3
+PARTS = 2
 NEVER = -1e30
-UNROLL = False
+UNROLL = True
 
 pseudo_count = 0.05
 prior_weight = 1.0
@@ -99,18 +99,18 @@
 
 
 def pack_kernel(
-    count_ref, cand_hbm, pos_hbm, gene_hbm, weight_hbm, centre_hbm, spread_hbm, corr_hbm,
+    count_hbm, cand_hbm, pos_hbm, gene_hbm, weight_hbm, centre_hbm, spread_hbm, corr_hbm,
     out_ref, table_ref, state_ref,
-    cand_ref, pos_ref, gene_ref, weight_ref, centre_ref, spread_ref, corr_ref, sems,
+    count_ref, cand_ref, pos_ref, gene_ref, weight_ref, centre_ref, spread_ref, corr_ref, sems,
 ):
     pairs = (
-        (cand_hbm, cand_ref), (pos_hbm, pos_ref), (gene_hbm, gene_ref), (weight_hbm, weight_ref),
+        (count_hbm, count_ref), (cand_hbm, cand_ref), (pos_hbm, pos_ref), (gene_hbm, gene_ref), (weight_hbm, weight_ref),
         (centre_hbm, centre_ref), (spread_hbm, spread_ref), (corr_hbm, corr_ref),
     )
     copies = [pltpu.make_async_copy(a, b, sems.at[n]) for n, (a, b) in enumerate(pairs)]
     for copy in copies:
         copy.start()
-    for copy in copies[:3]:
+    for copy in copies[:4]:
         copy.wait()
     tokens, slots = cand_ref.shape
     tiles = tokens // LANES
@@ -118,7 +118,7 @@
     lane = lax.broadcasted_iota(i32, (1, LANES), 1)
     for k in range(tiles):
         start = k * LANES
-        live = (start % BLOCK + lane) < count_ref[start // BLOCK]
+        live = (start % BLOCK + lane) < count_ref[:, start // BLOCK : start // BLOCK + 1]
         rows = [
             pos_ref[k : k + 1, :],
             pos_ref[tiles + k : tiles + k + 1, :],
@@ -127,7 +127,7 @@
             jnp.zeros((FEATURES - 4, LANES), f32),
         ]
         out_ref[slots : slots + FEATURES, lane_tile(k)] = jnp.concatenate(rows, axis=0)
-    for copy in copies[3:]:
+    for copy in copies[4:]:
         copy.wait()
     weights = weight_ref[...]
     spread_row, spread_col = spread_ref[0:1, :], spread_ref[1:2, :]
@@ -155,8 +155,8 @@
     nibbles = jnp.full((8, LANES), 0x0F0F0F0F, i32)
     for k in range(tokens // LANES):
         local = z_ref[0:slots, lane_tile(k)].astype(i32) - (2 - source) * 3 * cells
-        word_s[k] = (local >> shift) * words + (local & (words - 1))
-        unit_s[k] = 1 << (((local & (cells - 1)) >> word_shift) * 4)
+        word_s[k, 0:slots, :] = (local >> shift) * words + (local & (words - 1))
+        unit_s[k, 0:slots, :] = 1 << (((local & (cells - 1)) >> word_shift) * 4)
 
     def some(k, start, amount, carry):
         low, high = carry
@@ -231,9 +231,9 @@
 
 def gene_hot(x_ref, source, cells, padded):
     tokens = x_ref.shape[2]
-    gene = x_ref[source, cells + 2 : cells + 3, :].astype(i32)
-    axis = lax.broadcasted_iota(i32, (padded, tokens), 0)
-    return jnp.where(axis == gene, 1.0, 0.0).astype(bf16)
+    gene = x_ref[source, cells + 2 : cells + 3, :].astype(i32).astype(jnp.int16)
+    axis = lax.broadcasted_iota(jnp.int16, (padded, tokens), 0)
+    return jnp.where(axis == gene, jnp.ones((), bf16), jnp.zeros((), bf16))
 
 
 def features(x_ref, source, cells, row_step, col_step):
@@ -513,8 +513,9 @@
 
     packed, table_own, state_own = call(
         pack_kernel, "pack", [((slots + FEATURES, tokens), f32), table, state],
-        [SMEM] + [ANY] * 7,
+        [ANY] * 8,
         [
+            vmem((1, block_counts.shape[2]), i32),
             vmem((tokens, slots), i32),
             vmem((2 * tiles, LANES), f32),
             vmem((tiles, LANES), i32),
@@ -522,19 +523,22 @@
             vmem((2, cells), f32),
             vmem((2, cells), f32),
             vmem((1, cells), f32),
-            pltpu.SemaphoreType.DMA((7,)),
+            pltpu.SemaphoreType.DMA((8,)),
         ],
         tokens * slots,
-        (
-            block_counts.reshape(-1),
-            candidates.reshape(tokens, slots),
-            positions.reshape(2 * tiles, LANES),
-            genes.reshape(tiles, LANES),
-            profile_weights.reshape(gene_total, cells),
-            centroids.reshape(2, cells),
-            spreads.reshape(2, cells),
-            correlation.reshape(1, cells),
-        ),
+        [
+            pltpu.with_memory_space_constraint(a, pltpu.HBM)
+            for a in (
+                block_counts.reshape(1, -1),
+                candidates.reshape(tokens, slots),
+                positions.reshape(2 * tiles, LANES),
+                genes.reshape(tiles, LANES),
+                profile_weights.reshape(gene_total, cells),
+                centroids.reshape(2, cells),
+                spreads.reshape(2, cells),
+                correlation.reshape(1, cells),
+            )
+        ],
     )
     from_up = shifted(packed, "row", 1)
     from_down = shifted(packed, "row", -1)
@@ -547,7 +551,7 @@
     )
     one = ((cells + FEATURES, tokens), f32)
     three = ((3, cells + FEATURES, tokens), f32)
-    count_scratch = [vmem((tiles, slots, LANES), i32)] * 2
+    count_scratch = [vmem((tiles, slots + 8, LANES), i32)] * 2
     own = call(
         functools.partial(own_counts_kernel, cells), "own_counts", [one] * 3, [VMEM],
         count_scratch, pairs * 40, (packed,),

time: 80.3 us -> 70.1 us (0.87)
  local copies, waits for them, and re-layouts: 5.92 us -> 0 us
  Pallas kernels: 23.3 us -> 19.2 us
    unnamed x16 -> x0, local copies, waits for them, and re-layouts: 5.92 us -> none
    pallas_call x9, Pallas kernels: 23.3 us -> 19.2 us  [call(): pl.pallas_call(kernel, name=name, out_shape=shapes, in_specs=in_specs, ou...]
where the time goes in v3:
time: 70.1 us; the launch traced here: 69.7 us
  blocking collectives  32.5 us (46%)
  Pallas kernels  19.2 us (27%)
  starting transfers between devices  17.3 us (25%)
  between operations  0.76 us (1%)
    pallas_call x9, Pallas kernels, call(): pl.pallas_call(kernel, name=name, out_shape=shapes, in_specs=in_specs, ou...  19.2 us
    all_to_all x2, blocking collectives, body(): back = lax.all_to_all(parts, 'row', 0, 0)  18.9 us
    ppermute x6, starting transfers between devices, shifted(): return lax.ppermute(x, axis, pairs)  17.3 us
    all_gather x2, blocking collectives, body(): told_all = lax.all_gather(sums, 'col', axis=0)  13.5 us
  transfers between devices with their start and end apart: 6, of which 0 were waited for; matrix products, arithmetic and copies ran while one was open for 0% of the time, Pallas kernels for 7%

profile of v3, /device:TPU:0, one launch (start us, length us, event | category | flops | bytes accessed | tf_op | source)
XLA Modules:
  0.0 69.7 jit_solution(6819597187628853658)
XLA Ops:
  0.6 1.3 %pack.1 = (f32[136,512]{1,0:T(8,128)S(1)}, f32[488,128]{1,0:T(8,128)S(1)}, f32[8,128]{1,0:T(8,128)S(1)}) custom-call(s32[1,2]{1,0:T(1,128)} %bitcast.24, s32[512,128]{1,0:T(8,128)} %bitcast.18, f32[8,128]{1,0:T(8,128)} %bitcast.20, s32[4,128]{1,0:T(4,128)} %bitcast.21, f32[480,128]{1,0:T(8,128)} %bitcast.19, f32[2,128]{1,0:T(2,128)} %bitcast.22, ...), custom_call_target="tpu_custom_call" | custom-call | flops 65536 | bytes 1048576 | tf_op jit(solution)/shard_map/pack/pallas_call | solution.py:41
  2.0 1.3 %collective-permute-start.1 = (f32[136,512]{1,0:T(8,128)S(1)}, f32[136,512]{1,0:T(8,128)S(1)}, u32[]{:S(2)}, u32[]{:S(2)}) collective-permute-start(f32[136,512]{1,0:T(8,128)S(1)} %get-tuple-element.19.own_ref), channel_id=1, source_target_pairs={{4,0},{8,4},{12,8},{5,1},{9,5},{13,9},{6,2},{10,6},{14,10},{7,3},{... | collective-permute-start | bytes 835592 | tf_op jit(solution)/shard_map/ppermute | solution.py:28
  3.3 5.6 %collective-permute-start = (f32[136,512]{1,0:T(8,128)S(1)}, f32[136,512]{1,0:T(8,128)S(1)}, u32[]{:S(2)}, u32[]{:S(2)}) collective-permute-start(f32[136,512]{1,0:T(8,128)S(1)} %get-tuple-element.19.own_ref), channel_id=1, source_target_pairs={{0,4},{4,8},{8,12},{1,5},{5,9},{9,13},{2,6},{6,10},{10,14},{3,7},{... | collective-permute-start | bytes 835592 | tf_op jit(solution)/shard_map/ppermute | solution.py:28
  8.9 1.3 %collective-permute-start.3 = (f32[488,128]{1,0:T(8,128)S(1)}, f32[488,128]{1,0:T(8,128)S(1)}, u32[]{:S(2)}, u32[]{:S(2)}) collective-permute-start(f32[488,128]{1,0:T(8,128)S(1)} %get-tuple-element.23.own_ref), channel_id=1, source_target_pairs={{1,0},{2,1},{3,2},{5,4},{6,5},{7,6},{9,8},{10,9},{11,10},{13,12},{... | collective-permute-start | bytes 749576 | tf_op jit(solution)/shard_map/ppermute | solution.py:28
  10.2 3.0 %collective-permute-start.2 = (f32[488,128]{1,0:T(8,128)S(1)}, f32[488,128]{1,0:T(8,128)S(1)}, u32[]{:S(2)}, u32[]{:S(2)}) collective-permute-start(f32[488,128]{1,0:T(8,128)S(1)} %get-tuple-element.23.own_ref), channel_id=1, source_target_pairs={{0,1},{1,2},{2,3},{4,5},{5,6},{6,7},{8,9},{9,10},{10,11},{12,13},{... | collective-permute-start | bytes 749576 | tf_op jit(solution)/shard_map/ppermute | solution.py:28
  13.2 1.8 %own_counts.1 = (f32[136,512]{1,0:T(8,128)S(1)}, f32[136,512]{1,0:T(8,128)S(1)}, f32[136,512]{1,0:T(8,128)S(1)}) custom-call(f32[136,512]{1,0:T(8,128)S(1)} %get-tuple-element.19.own_ref), custom_call_target="tpu_custom_call" | custom-call | flops 23592960 | bytes 1048576 | tf_op jit(solution)/shard_map/own_counts/pallas_call | solution.py:41
  15.1 0.0 collective-permute-done.3.right_ref
  15.1 0.0 collective-permute-done.2.left_ref
  15.1 0.7 %tables.1 = (bf16[3,256,512]{2,1,0:T(8,128)(2,1)S(1)}, f32[3,6,128,128]{3,2,1,0:T(8,128)S(1)}) custom-call(f32[488,128]{1,0:T(8,128)S(1)} %collective-permute-done.2.left_ref, f32[488,128]{1,0:T(8,128)S(1)} %get-tuple-element.23.own_ref, f32[488,128]{1,0:T(8,128)S(1)} %collective-permute-done.3.right_ref), custom_call_target="tpu_custom_call" | custom-call | flops 65536 | bytes 1048576 | tf_op jit(solution)/shard_map/tables/pallas_call | solution.py:41
  15.8 0.0 collective-permute-done.1.down_ref
  15.8 0.0 collective-permute-done.up_ref
  15.8 3.7 %counts.1 = (f32[3,136,512]{2,1,0:T(8,128)S(1)}, f32[3,136,512]{2,1,0:T(8,128)S(1)}, f32[3,136,512]{2,1,0:T(8,128)S(1)}) custom-call(f32[136,512]{1,0:T(8,128)S(1)} %collective-permute-done.up_ref, f32[136,512]{1,0:T(8,128)S(1)} %collective-permute-done.1.down_ref, f32[136,512]{1,0:T(8,128)S(1)} %get-tuple-element.20.own_left, ...), custom_call_target="tpu_custom_call" | custom-call | flops 47185920 | bytes 1048576 | tf_op jit(solution)/shard_map/counts/pallas_call | solution.py:41
  19.6 4.8 %collective-permute-start.4 = (f32[3,136,512]{2,1,0:T(8,128)S(1)}, f32[3,136,512]{2,1,0:T(8,128)S(1)}, u32[]{:S(2)}, u32[]{:S(2)}) collective-permute-start(f32[3,136,512]{2,1,0:T(8,128)S(1)} %get-tuple-element.25.right_ref), channel_id=1, source_target_pairs={{0,1},{1,2},{2,3},{4,5},{5,6},{6,7},{8,9},{9,10},{10,11},{12,13},{... | collective-permute-start | bytes 2506760 | tf_op jit(solution)/shard_map/ppermute | solution.py:28
  24.4 1.3 %collective-permute-start.5 = (f32[3,136,512]{2,1,0:T(8,128)S(1)}, f32[3,136,512]{2,1,0:T(8,128)S(1)}, u32[]{:S(2)}, u32[]{:S(2)}) collective-permute-start(f32[3,136,512]{2,1,0:T(8,128)S(1)} %get-tuple-element.27.left_ref), channel_id=1, source_target_pairs={{1,0},{2,1},{3,2},{5,4},{6,5},{7,6},{9,8},{10,9},{11,10},{13,12},{... | collective-permute-start | bytes 2506760 | tf_op jit(solution)/shard_map/ppermute | solution.py:28
  25.7 2.3 %row_parts.1 = f32[4,3,8,128]{3,2,1,0:T(8,128)S(1)} custom-call(f32[3,136,512]{2,1,0:T(8,128)S(1)} %get-tuple-element.27.left_ref, f32[3,136,512]{2,1,0:T(8,128)S(1)} %get-tuple-element.26.mid_ref, f32[3,136,512]{2,1,0:T(8,128)S(1)} %get-tuple-element.25.right_ref, bf16[3,256,512]{2,1,0:T(8,128)(2,1)S(1)} %get-tuple-element.24.ltp_hbm.ltp_s.ltp_ref, ...), custom_call_target="tpu_custom_call" | custom-call | flops 58982400 | bytes 1048576 | tf_op jit(solution)/shard_map/row_parts/pallas_call | solution.py:41
  27.9 9.4 %all_to_all.10.in_ref = f32[4,3,8,128]{3,2,1,0:T(8,128)S(1)} all-to-all(f32[4,3,8,128]{3,2,1,0:T(8,128)S(1)} %row_parts.1), channel_id=1, replica_groups=mesh['groups'=2,'row'=4,'col'=4] {'row'}, dimensions={0} | all-to-all | bytes 98304 | tf_op jit(solution)/shard_map/all_to_all | solution.py:577
  37.4 7.9 %all-gather = f32[12,8,128]{2,1,0:T(8,128)S(1)} all-gather(f32[3,8,128]{2,1,0:T(8,128)S(1)} %row_join.1), channel_id=2, replica_groups=mesh['groups'=2,'row'=4,'col'=4] {'col'}, dimensions={0}, use_global_device_ids=true | all-gather | bytes 61440 | tf_op jit(solution)/shard_map/all_gather | solution.py:579
  45.3 0.0 collective-permute-done.4.left_ref
  45.3 0.0 collective-permute-done.5.right_ref
  45.3 6.1 %middle.1 = (f32[3,3,128,512]{3,2,1,0:T(8,128)S(1)}, f32[3,3,8,128]{3,2,1,0:T(8,128)S(1)}, f32[4,3,3,8,128]{4,3,2,1,0:T(8,128)S(1)}, f32[8,128]{1,0:T(8,128)S(1)}) custom-call(f32[3,136,512]{2,1,0:T(8,128)S(1)} %collective-permute-done.4.left_ref, f32[3,136,512]{2,1,0:T(8,128)S(1)} %get-tuple-element.26.mid_ref, ...), custom_call_target="tpu_custom_call" | custom-call | flops 117964800 | bytes 1048576 | tf_op jit(solution)/shard_map/middle/pallas_call | solution.py:41
  51.4 9.6 %all_to_all.11.in_ref = f32[4,3,3,8,128]{4,3,2,1,0:T(8,128)S(1)} all-to-all(f32[4,3,3,8,128]{4,3,2,1,0:T(8,128)S(1)} %get-tuple-element.32), channel_id=1, replica_groups=mesh['groups'=2,'row'=4,'col'=4] {'row'}, dimensions={0} | all-to-all | bytes 294912 | tf_op jit(solution)/shard_map/all_to_all | solution.py:602
  61.0 0.1 part_join.1
  61.1 5.6 %all-gather.1 = f32[12,3,8,128]{3,2,1,0:T(8,128)S(1)} all-gather(f32[3,3,8,128]{3,2,1,0:T(8,128)S(1)} %part_join.1), channel_id=3, replica_groups=mesh['groups'=2,'row'=4,'col'=4] {'col'}, dimensions={0}, use_global_device_ids=true | all-gather | bytes 184320 | tf_op jit(solution)/shard_map/all_gather | solution.py:604
  66.7 3.1 %last.1 = (f32[480,128]{1,0:T(8,128)}, f32[6,1,128]{2,1,0:T(1,128)}) custom-call(f32[3,136,512]{2,1,0:T(8,128)S(1)} %collective-permute-done.4.left_ref, f32[3,136,512]{2,1,0:T(8,128)S(1)} %get-tuple-element.26.mid_ref, f32[3,136,512]{2,1,0:T(8,128)S(1)} %collective-permute-done.5.right_ref, f32[3,3,128,512]{3,2,1,0:T(8,128)S(1)} %get-tuple-element.30.e_ref, ...), custom_call_target="tpu_custom_call" | custom-call | flops 58982400 | bytes 1048576 | tf_op jit(solution)/shard_map/last/pallas_call | solution.py:41
  (1 shorter events, 0.0 us)
Async XLA Ops:
  2.0 13.8 %collective-permute-start.1 = (f32[136,512]{1,0:T(8,128)S(1)}, f32[136,512]{1,0:T(8,128)S(1)}, u32[]{:S(2)}, u32[]{:S(2)}) collective-permute-start(f32[136,512]{1,0:T(8,128)S(1)} %get-tuple-element.19.own_ref), channel_id=1, source_target_pairs={{4,0},{8,4},{12,8},{5,1},{9,5},{13,9},{6,2},{10,6},{14,10},{7,3},{... | collective-permute-start | bytes 835592 | tf_op jit(solution)/shard_map/ppermute | solution.py:28
  3.3 12.6 %collective-permute-start = (f32[136,512]{1,0:T(8,128)S(1)}, f32[136,512]{1,0:T(8,128)S(1)}, u32[]{:S(2)}, u32[]{:S(2)}) collective-permute-start(f32[136,512]{1,0:T(8,128)S(1)} %get-tuple-element.19.own_ref), channel_id=1, source_target_pairs={{0,4},{4,8},{8,12},{1,5},{5,9},{9,13},{2,6},{6,10},{10,14},{3,7},{... | collective-permute-start | bytes 835592 | tf_op jit(solution)/shard_map/ppermute | solution.py:28
  8.9 6.2 %collective-permute-start.3 = (f32[488,128]{1,0:T(8,128)S(1)}, f32[488,128]{1,0:T(8,128)S(1)}, u32[]{:S(2)}, u32[]{:S(2)}) collective-permute-start(f32[488,128]{1,0:T(8,128)S(1)} %get-tuple-element.23.own_ref), channel_id=1, source_target_pairs={{1,0},{2,1},{3,2},{5,4},{6,5},{7,6},{9,8},{10,9},{11,10},{13,12},{... | collective-permute-start | bytes 749576 | tf_op jit(solution)/shard_map/ppermute | solution.py:28
  10.2 4.9 %collective-permute-start.2 = (f32[488,128]{1,0:T(8,128)S(1)}, f32[488,128]{1,0:T(8,128)S(1)}, u32[]{:S(2)}, u32[]{:S(2)}) collective-permute-start(f32[488,128]{1,0:T(8,128)S(1)} %get-tuple-element.23.own_ref), channel_id=1, source_target_pairs={{0,1},{1,2},{2,3},{4,5},{5,6},{6,7},{8,9},{9,10},{10,11},{12,13},{... | collective-permute-start | bytes 749576 | tf_op jit(solution)/shard_map/ppermute | solution.py:28
  19.6 25.7 %collective-permute-start.4 = (f32[3,136,512]{2,1,0:T(8,128)S(1)}, f32[3,136,512]{2,1,0:T(8,128)S(1)}, u32[]{:S(2)}, u32[]{:S(2)}) collective-permute-start(f32[3,136,512]{2,1,0:T(8,128)S(1)} %get-tuple-element.25.right_ref), channel_id=1, source_target_pairs={{0,1},{1,2},{2,3},{4,5},{5,6},{6,7},{8,9},{9,10},{10,11},{12,13},{... | collective-permute-start | bytes 2506760 | tf_op jit(solution)/shard_map/ppermute | solution.py:28
  24.4 20.9 %collective-permute-start.5 = (f32[3,136,512]{2,1,0:T(8,128)S(1)}, f32[3,136,512]{2,1,0:T(8,128)S(1)}, u32[]{:S(2)}, u32[]{:S(2)}) collective-permute-start(f32[3,136,512]{2,1,0:T(8,128)S(1)} %get-tuple-element.27.left_ref), channel_id=1, source_target_pairs={{1,0},{2,1},{3,2},{5,4},{6,5},{7,6},{9,8},{10,9},{11,10},{13,12},{... | collective-permute-start | bytes 2506760 | tf_op jit(solution)/shard_map/ppermute | solution.py:28

commit v4 on v3

--- a/solution.py
+++ b/solution.py
@@ -12,7 +12,6 @@
 FEATURES = 8
 PARTS = 2
 NEVER = -1e30
-UNROLL = True
 
 pseudo_count = 0.05
 prior_weight = 1.0
@@ -22,10 +21,13 @@
 i32 = jnp.int32
 
 
-def shifted(x, axis, by):
+def swapped(to_first, to_second, axis):
     count = lax.axis_size(axis)
-    pairs = [(i, i + by) for i in range(count) if 0 <= i + by < count]
-    return lax.ppermute(x, axis, pairs)
+    out = []
+    for start, x in enumerate((to_first, to_second)):
+        pairs = [p for i in range(start, count - 1, 2) for p in ((i, i + 1), (i + 1, i))]
+        out.append(lax.ppermute(x, axis, pairs))
+    return out
 
 
 def params(mib=40):
@@ -63,12 +65,9 @@
     return -(-size // unit) * unit
 
 
-def sources(step):
-    if UNROLL:
-        for source in range(3):
-            step(source)
-    else:
-        pl.loop(0, 3)(step)
+def order(axis):
+    first = 2 * (1 - lax.rem(lax.axis_index(axis), 2))
+    return (first, 1, 2 - first)
 
 
 def as_float(x):
@@ -153,9 +152,11 @@
     per_tile = words // 8
     sub = lax.broadcasted_iota(i32, (8, LANES), 0)
     nibbles = jnp.full((8, LANES), 0x0F0F0F0F, i32)
+    first = order("col")[0]
     for k in range(tokens // LANES):
         local = z_ref[0:slots, lane_tile(k)].astype(i32) - (2 - source) * 3 * cells
-        word_s[k, 0:slots, :] = (local >> shift) * words + (local & (words - 1))
+        place = first + (local >> shift) * (1 - first)
+        word_s[k, 0:slots, :] = place * words + (local & (words - 1))
         unit_s[k, 0:slots, :] = 1 << (((local & (cells - 1)) >> word_shift) * 4)
 
     def some(k, start, amount, carry):
@@ -190,19 +191,20 @@
         out[cells : cells + FEATURES, :] = z_ref[slots : slots + FEATURES, :]
 
 
-def own_counts_kernel(cells, own_ref, left_ref, mid_ref, right_ref, word_s, unit_s):
-    count_source(1, own_ref, cells, (left_ref, mid_ref, right_ref), word_s, unit_s)
+def own_counts_kernel(cells, own_ref, first_ref, mid_ref, second_ref, word_s, unit_s):
+    count_source(1, own_ref, cells, (first_ref, mid_ref, second_ref), word_s, unit_s)
 
 
 def counts_kernel(
-    cells, up_ref, down_ref, own_left, own_mid, own_right, ltp_hbm,
-    left_ref, mid_ref, right_ref, word_s, unit_s,
+    cells, first_ref, second_ref, own_first, own_mid, own_second, ltp_hbm,
+    to_first, mid_ref, to_second, word_s, unit_s,
 ):
-    outs = (left_ref, mid_ref, right_ref)
-    for out, own in zip(outs, (own_left, own_mid, own_right)):
+    outs = (to_first, mid_ref, to_second)
+    for out, own in zip(outs, (own_first, own_mid, own_second)):
         out[1] = own[...]
-    for source, z_ref in ((0, up_ref), (2, down_ref)):
-        count_source(source, z_ref, cells, [out.at[source] for out in outs], word_s, unit_s)
+    first, _, second = order("row")
+    for q, source, z_ref in ((0, first, first_ref), (2, second, second_ref)):
+        count_source(source, z_ref, cells, [out.at[q] for out in outs], word_s, unit_s)
 
 
 def load_table(table_ref, ltp_s, par_s):
@@ -224,8 +226,8 @@
         par_s[n] = jnp.broadcast_to(columns[:, n : n + 1], (cells, LANES))
 
 
-def tables_kernel(left_ref, own_ref, right_ref, ltp_ref, par_ref):
-    for side, table in enumerate((left_ref, own_ref, right_ref)):
+def tables_kernel(first_ref, own_ref, second_ref, ltp_ref, par_ref):
+    for side, table in enumerate((first_ref, own_ref, second_ref)):
         load_table(table, ltp_ref.at[side], par_ref.at[side])
 
 
@@ -304,33 +306,31 @@
 
 
 def row_parts_kernel(
-    left_ref, mid_ref, right_ref, ltp_s, par_s, out_ref, part_s, gl_s, sc_s
+    first_ref, mid_ref, second_ref, ltp_s, par_s, out_ref, part_s, gl_s, sc_s
 ):
-    x_refs = (left_ref, mid_ref, right_ref)
+    x_refs = (first_ref, mid_ref, second_ref)
     cells, tokens = sc_s.shape[1:]
 
-    def step(source):
-        hot = gene_hot(mid_ref, source, cells, ltp_s.shape[2])
+    for q, source in enumerate(order("row")):
+        hot = gene_hot(mid_ref, q, cells, ltp_s.shape[2])
         for side in range(3):
             gl_s[side] = jnp.dot(ltp_s[side], hot, preferred_element_type=f32)
         top = jnp.full((8, tokens), NEVER, f32)
-        for side in range(3):
-            y0, y1 = features(mid_ref, source, cells, as_float(source) - 1.0, 1.0 - side)
+        for side, at_side in enumerate(order("col")):
+            y0, y1 = features(mid_ref, q, cells, as_float(source) - 1.0, 1.0 - as_float(at_side))
             for at in range(0, cells, 8):
                 score = score_rows(at, y0, y1, gl_s.at[side], par_s.at[side], cells)
-                score = jnp.where(x_refs[side][source, at : at + 8, :] > 0.0, score, NEVER)
+                score = jnp.where(x_refs[side][q, at : at + 8, :] > 0.0, score, NEVER)
                 sc_s[side, at : at + 8, :] = score
                 top = jnp.maximum(top, score)
         top = jnp.max(top, axis=0, keepdims=True)
         total = jnp.zeros((8, tokens), f32)
         for side in range(3):
             for at in range(0, cells, 8):
-                count = x_refs[side][source, at : at + 8, :]
+                count = x_refs[side][q, at : at + 8, :]
                 total = total + count * jnp.exp(sc_s[side, at : at + 8, :] - top)
         total = jnp.sum(total, axis=0, keepdims=True)
         part_s[source] = jnp.concatenate([to_tiles(top), to_tiles(total)], axis=0)
-
-    sources(step)
     spread_rows(part_s, out_ref)
 
 
@@ -380,11 +380,11 @@
 
 def middle_kernel(
     genes,
-    left_ref, mid_ref, right_ref, ltp_ref, par_ref, state_ref, told_ref,
+    first_ref, mid_ref, second_ref, ltp_ref, par_ref, state_ref, told_ref,
     e_ref, m_ref, out_ref, state_out,
     hot_s, sh_s, mom_s, cnt_s, ltp_s, par_s, gl_s, sc_s, table_s, part_s,
 ):
-    x_refs = (left_ref, mid_ref, right_ref)
+    x_refs = (first_ref, mid_ref, second_ref)
     cells, tokens = sc_s.shape[1:]
     tiles = tokens // LANES
     padded = cnt_s.shape[0]
@@ -393,20 +393,20 @@
     mom_s[...] = jnp.zeros(mom_s.shape, f32)
     cnt_s[...] = jnp.zeros(cnt_s.shape, f32)
 
-    def posterior(source):
+    for q, source in enumerate(order("row")):
         for side, x_ref in enumerate(x_refs):
-            hot_s[source, side] = gene_hot(x_ref, source, cells, padded)
-            gl_s[side] = jnp.dot(ltp_ref[1], hot_s[source, side], preferred_element_type=f32)
-        for side, x_ref in enumerate(x_refs):
-            at_col = jnp.clip(col + side - 1, 0, cols - 1)
+            hot_s[q, side] = gene_hot(x_ref, q, cells, padded)
+            gl_s[side] = jnp.dot(ltp_ref[1], hot_s[q, side], preferred_element_type=f32)
+        for side, (at_side, x_ref) in enumerate(zip(order("col"), x_refs)):
+            at_col = jnp.clip(col + at_side - 1, 0, cols - 1)
             top = row_of(told_ref, (at_col, source), 0, tiles)
             factor = row_of(told_ref, (at_col, source), tiles, tiles)
-            y0, y1 = features(x_ref, source, cells, as_float(source) - 1.0, side - 1.0)
+            y0, y1 = features(x_ref, q, cells, as_float(source) - 1.0, as_float(at_side) - 1.0)
             for at in range(0, cells, 16):
                 halves = []
                 for a in (at, at + 8):
                     score = score_rows(a, y0, y1, gl_s.at[side], par_ref.at[1], cells)
-                    count = x_ref[source, a : a + 8, :]
+                    count = x_ref[q, a : a + 8, :]
                     p = count * jnp.exp(jnp.minimum(score - top, 0.0)) * factor
                     sums = [mom_s[n, a : a + 8, :] for n in range(6)]
                     sums = add_moments(p, y0, y1, sums)
@@ -414,46 +414,44 @@
                         mom_s[n, a : a + 8, :] = sums[n]
                     halves.append(p)
                 sh_s[side, at : at + 16, :] = jnp.concatenate(halves, axis=0).astype(bf16)
-            add_counts(hot_s[source, side], sh_s.at[side], cnt_s)
-
-    sources(posterior)
+            add_counts(hot_s[q, side], sh_s.at[side], cnt_s)
+
     profile, state, log_weight = new_cells(genes, mom_s, cnt_s, state_ref)
     state_out[...] = state_rows(state)
     table_s[...] = table_rows(profile, state, log_weight)
     load_table(table_s, ltp_s, par_s)
 
-    def score(source):
+    for q, source in enumerate(order("row")):
         for side in range(3):
-            gl_s[side] = jnp.dot(ltp_s[...], hot_s[source, side], preferred_element_type=f32)
-        for side, x_ref in enumerate(x_refs):
-            y0, y1 = features(x_ref, source, cells, as_float(source) - 1.0, side - 1.0)
+            gl_s[side] = jnp.dot(ltp_s[...], hot_s[q, side], preferred_element_type=f32)
+        for side, (at_side, x_ref) in enumerate(zip(order("col"), x_refs)):
+            y0, y1 = features(x_ref, q, cells, as_float(source) - 1.0, as_float(at_side) - 1.0)
             top = jnp.full((8, tokens), NEVER, f32)
             for at in range(0, cells, 8):
                 value = score_rows(at, y0, y1, gl_s.at[side], par_s, cells)
-                value = jnp.where(x_ref[source, at : at + 8, :] > 0.0, value, NEVER)
+                value = jnp.where(x_ref[q, at : at + 8, :] > 0.0, value, NEVER)
                 sc_s[side, at : at + 8, :] = value
                 top = jnp.maximum(top, value)
             top = jnp.max(top, axis=0, keepdims=True)
             total = jnp.zeros((8, tokens), f32)
             for at in range(0, cells, 8):
-                e = x_ref[source, at : at + 8, :] * jnp.exp(sc_s[side, at : at + 8, :] - top)
-                e_ref[source, side, at : at + 8, :] = e
+                e = x_ref[q, at : at + 8, :] * jnp.exp(sc_s[side, at : at + 8, :] - top)
+                e_ref[q, side, at : at + 8, :] = e
                 total = total + e
             total = jnp.sum(total, axis=0, keepdims=True)
-            part_s[source, side] = jnp.concatenate([to_tiles(top), to_tiles(total)], axis=0)
-
-    sources(score)
+            part_s[source, at_side] = jnp.concatenate([to_tiles(top), to_tiles(total)], axis=0)
+
     m_ref[...] = part_s[...]
     spread_rows(part_s, out_ref)
 
 
 def last_kernel(
     genes,
-    left_ref, mid_ref, right_ref, e_ref, m_ref, told_ref, state_ref,
+    first_ref, mid_ref, second_ref, e_ref, m_ref, told_ref, state_ref,
     profile_ref, cells_ref,
     sh_s, mom_s, cnt_s,
 ):
-    x_refs = (left_ref, mid_ref, right_ref)
+    x_refs = (first_ref, mid_ref, second_ref)
     cells, tokens = sh_s.shape[1:]
     tiles = tokens // LANES
     cols = told_ref.shape[0]
@@ -463,32 +461,31 @@
     shape = m_ref.shape[2:]
     nothing = jnp.where(lax.broadcasted_iota(i32, shape, 0) < shape[0] // 2, NEVER, 0.0)
 
-    def posterior(source):
-        for side, x_ref in enumerate(x_refs):
+    for q, source in enumerate(order("row")):
+        for side, (at_side, x_ref) in enumerate(zip(order("col"), x_refs)):
             parts = []
             for step in range(-1, 2):
-                owner = col + side - 1 + step
+                owner = col + at_side - 1 + step
                 inside = (owner >= 0) & (owner < cols)
                 part = told_ref[jnp.clip(owner, 0, cols - 1), source, 1 - step]
                 parts.append(jnp.where(inside, part, nothing))
             top, total = joined(parts)
-            scale = jnp.exp(m_ref[source, side][0:tiles] - top)
+            scale = jnp.exp(m_ref[source, at_side][0:tiles] - top)
             scale = jnp.where(total > 0.0, scale / total, 0.0)
             factor = jnp.concatenate([scale[k : k + 1, :] for k in range(tiles)], axis=1)
-            y0, y1 = features(x_ref, source, cells, as_float(source) - 1.0, side - 1.0)
+            y0, y1 = features(x_ref, q, cells, as_float(source) - 1.0, as_float(at_side) - 1.0)
             for at in range(0, cells, 16):
                 halves = []
                 for a in (at, at + 8):
-                    p = e_ref[source, side, a : a + 8, :] * factor
+                    p = e_ref[q, side, a : a + 8, :] * factor
                     sums = [mom_s[n, a : a + 8, :] for n in range(6)]
                     sums = add_moments(p, y0, y1, sums)
                     for n in range(6):
                         mom_s[n, a : a + 8, :] = sums[n]
                     halves.append(p)
                 sh_s[side, at : at + 16, :] = jnp.concatenate(halves, axis=0).astype(bf16)
-            add_counts(gene_hot(x_ref, source, cells, cnt_s.shape[0]), sh_s.at[side], cnt_s)
-
-    sources(posterior)
+            add_counts(gene_hot(x_ref, q, cells, cnt_s.shape[0]), sh_s.at[side], cnt_s)
+
     profile, state, log_weight = new_cells(genes, mom_s, cnt_s, state_ref)
     profile_ref[...] = jnp.log(profile)
     mu_row, mu_col, rr, rc, cc = state
@@ -540,14 +537,12 @@
             )
         ],
     )
-    from_up = shifted(packed, "row", 1)
-    from_down = shifted(packed, "row", -1)
-    table_left = shifted(table_own, "col", 1)
-    table_right = shifted(table_own, "col", -1)
+    row_first, row_second = swapped(packed, packed, "row")
+    table_first, table_second = swapped(table_own, table_own, "col")
     ltp, par = call(
         tables_kernel, "tables",
         [((3, PARTS * cells, padded), bf16), ((3, 6, cells, LANES), f32)], [VMEM] * 3, [],
-        tokens * slots, (table_left, table_own, table_right),
+        tokens * slots, (table_first, table_own, table_second),
     )
     one = ((cells + FEATURES, tokens), f32)
     three = ((3, cells + FEATURES, tokens), f32)
@@ -556,12 +551,11 @@
         functools.partial(own_counts_kernel, cells), "own_counts", [one] * 3, [VMEM],
         count_scratch, pairs * 40, (packed,),
     )
-    to_left, mid, to_right = call(
+    to_first, mid, to_second = call(
         functools.partial(counts_kernel, cells), "counts", [three] * 3, [VMEM] * 5 + [ANY],
-        count_scratch, pairs * 80, (from_up, from_down, *own, ltp),
-    )
-    from_right = shifted(to_left, "col", -1)
-    from_left = shifted(to_right, "col", 1)
+        count_scratch, pairs * 80, (row_first, row_second, *own, ltp),
+    )
+    from_first, from_second = swapped(to_first, to_second, "col")
 
     chunk = (2 * tiles, LANES)
     parts, = call(
@@ -572,13 +566,13 @@
             vmem((3, cells, tokens), f32),
         ],
         pairs * 100,
-        (to_left, mid, to_right, ltp, par),
+        (to_first, mid, to_second, ltp, par),
     )
     back = lax.all_to_all(parts, "row", 0, 0)
     sums, = call(row_join_kernel, "row_join", [((3,) + chunk, f32)], [VMEM], [], tokens * 100, (back,))
     told_all = lax.all_gather(sums, "col", axis=0)
 
-    x = (from_left, mid, from_right)
+    x = (from_first, mid, from_second)
     sum_scratch = [
         vmem((3, cells, tokens), bf16),
         vmem((6, cells, LANES), f32),

time: 70.1 us -> 62.6 us (0.89)
  starting transfers between devices: 17.3 us -> 12.7 us
  blocking collectives: 32.5 us -> 29.4 us
    ppermute x6, starting transfers between devices: 17.3 us -> 12.7 us  [swapped(): out.append(lax.ppermute(x, axis, pairs))]
    all_gather x2, blocking collectives: 13.5 us -> 11.7 us  [body(): told_all = lax.all_gather(sums, 'col', axis=0)]
    all_to_all x2, blocking collectives: 18.9 us -> 17.7 us  [body(): back = lax.all_to_all(parts, 'row', 0, 0)]
  transfers between devices with their start and end apart: 6 -> 6, of which waited for: 0 -> 1; matrix products, arithmetic and copies ran while one was open for 0% -> 0% of each run, Pallas kernels for 7% -> 8%
where the time goes in v4:
time: 62.6 us; the launch traced here: 62.3 us
  blocking collectives  29.4 us (47%)
  Pallas kernels  19.3 us (31%)
  starting transfers between devices  12.7 us (20%)
  between operations  0.73 us (1%)
    pallas_call x9, Pallas kernels, call(): pl.pallas_call(kernel, name=name, out_shape=shapes, in_specs=in_specs, ou...  19.3 us
    all_to_all x2, blocking collectives, body(): back = lax.all_to_all(parts, 'row', 0, 0)  17.7 us
    ppermute x6, starting transfers between devices, swapped(): out.append(lax.ppermute(x, axis, pairs))  12.7 us
    all_gather x2, blocking collectives, body(): told_all = lax.all_gather(sums, 'col', axis=0)  11.7 us
  transfers between devices with their start and end apart: 6, of which 1 were waited for; matrix products, arithmetic and copies ran while one was open for 0% of the time, Pallas kernels for 8%

profile of v4, /device:TPU:0, one launch (start us, length us, event | category | flops | bytes accessed | tf_op | source)
XLA Modules:
  0.0 62.3 jit_solution(8773540614746415887)
XLA Ops:
  0.6 1.3 %pack.1 = (f32[136,512]{1,0:T(8,128)S(1)}, f32[488,128]{1,0:T(8,128)S(1)}, f32[8,128]{1,0:T(8,128)S(1)}) custom-call(s32[1,2]{1,0:T(1,128)} %bitcast.24, s32[512,128]{1,0:T(8,128)} %bitcast.18, f32[8,128]{1,0:T(8,128)} %bitcast.20, s32[4,128]{1,0:T(4,128)} %bitcast.21, f32[480,128]{1,0:T(8,128)} %bitcast.19, f32[2,128]{1,0:T(2,128)} %bitcast.22, ...), custom_call_target="tpu_custom_call" | custom-call | flops 65536 | bytes 1048576 | tf_op jit(solution)/shard_map/pack/pallas_call | solution.py:43
  2.0 0.7 %collective-permute-start.1 = (f32[136,512]{1,0:T(8,128)S(1)}, f32[136,512]{1,0:T(8,128)S(1)}, u32[]{:S(2)}, u32[]{:S(2)}) collective-permute-start(f32[136,512]{1,0:T(8,128)S(1)} %get-tuple-element.19.own_ref), channel_id=1, source_target_pairs={{4,8},{8,4},{5,9},{9,5},{6,10},{10,6},{7,11},{11,7},{20,24},{24,20... | collective-permute-start | bytes 835592 | tf_op jit(solution)/shard_map/ppermute | solution.py:29
  2.7 5.9 %collective-permute-start = (f32[136,512]{1,0:T(8,128)S(1)}, f32[136,512]{1,0:T(8,128)S(1)}, u32[]{:S(2)}, u32[]{:S(2)}) collective-permute-start(f32[136,512]{1,0:T(8,128)S(1)} %get-tuple-element.19.own_ref), channel_id=1, source_target_pairs={{0,4},{4,0},{8,12},{12,8},{1,5},{5,1},{9,13},{13,9},{2,6},{6,2},{1... | collective-permute-start | bytes 835592 | tf_op jit(solution)/shard_map/ppermute | solution.py:29
  8.6 0.7 %collective-permute-start.3 = (f32[488,128]{1,0:T(8,128)S(1)}, f32[488,128]{1,0:T(8,128)S(1)}, u32[]{:S(2)}, u32[]{:S(2)}) collective-permute-start(f32[488,128]{1,0:T(8,128)S(1)} %get-tuple-element.23.own_ref), channel_id=1, source_target_pairs={{1,2},{2,1},{5,6},{6,5},{9,10},{10,9},{13,14},{14,13},{17,18},{18,... | collective-permute-start | bytes 749576 | tf_op jit(solution)/shard_map/ppermute | solution.py:29
  9.2 2.9 %collective-permute-start.2 = (f32[488,128]{1,0:T(8,128)S(1)}, f32[488,128]{1,0:T(8,128)S(1)}, u32[]{:S(2)}, u32[]{:S(2)}) collective-permute-start(f32[488,128]{1,0:T(8,128)S(1)} %get-tuple-element.23.own_ref), channel_id=1, source_target_pairs={{0,1},{1,0},{2,3},{3,2},{4,5},{5,4},{6,7},{7,6},{8,9},{9,8},{10,11... | collective-permute-start | bytes 749576 | tf_op jit(solution)/shard_map/ppermute | solution.py:29
  12.2 1.8 %own_counts.1 = (f32[136,512]{1,0:T(8,128)S(1)}, f32[136,512]{1,0:T(8,128)S(1)}, f32[136,512]{1,0:T(8,128)S(1)}) custom-call(f32[136,512]{1,0:T(8,128)S(1)} %get-tuple-element.19.own_ref), custom_call_target="tpu_custom_call" | custom-call | flops 23592960 | bytes 1048576 | tf_op jit(solution)/shard_map/own_counts/pallas_call | solution.py:43
  14.0 0.0 collective-permute-done.3.second_ref
  14.0 0.0 collective-permute-done.2.first_ref
  14.0 0.7 %tables.1 = (bf16[3,256,512]{2,1,0:T(8,128)(2,1)S(1)}, f32[3,6,128,128]{3,2,1,0:T(8,128)S(1)}) custom-call(f32[488,128]{1,0:T(8,128)S(1)} %collective-permute-done.2.first_ref, f32[488,128]{1,0:T(8,128)S(1)} %get-tuple-element.23.own_ref, f32[488,128]{1,0:T(8,128)S(1)} %collective-permute-done.3.second_ref), custom_call_target="tpu_custom_call" | custom-call | flops 65536 | bytes 1048576 | tf_op jit(solution)/shard_map/tables/pallas_call | solution.py:43
  14.7 0.0 collective-permute-done.1.second_ref
  14.7 0.2 collective-permute-done.first_ref
  15.0 3.9 %counts.1 = (f32[3,136,512]{2,1,0:T(8,128)S(1)}, f32[3,136,512]{2,1,0:T(8,128)S(1)}, f32[3,136,512]{2,1,0:T(8,128)S(1)}) custom-call(f32[136,512]{1,0:T(8,128)S(1)} %collective-permute-done.first_ref, f32[136,512]{1,0:T(8,128)S(1)} %collective-permute-done.1.second_ref, f32[136,512]{1,0:T(8,128)S(1)} %get-tuple-element.20.own_first, ...), custom_call_target="tpu_custom_call" | custom-call | flops 47185920 | bytes 1048576 | tf_op jit(solution)/shard_map/counts/pallas_call | solution.py:43
  18.9 1.9 %collective-permute-start.4 = (f32[3,136,512]{2,1,0:T(8,128)S(1)}, f32[3,136,512]{2,1,0:T(8,128)S(1)}, u32[]{:S(2)}, u32[]{:S(2)}) collective-permute-start(f32[3,136,512]{2,1,0:T(8,128)S(1)} %get-tuple-element.25.first_ref), channel_id=1, source_target_pairs={{0,1},{1,0},{2,3},{3,2},{4,5},{5,4},{6,7},{7,6},{8,9},{9,8},{10,11... | collective-permute-start | bytes 2506760 | tf_op jit(solution)/shard_map/ppermute | solution.py:29
  20.7 0.7 %collective-permute-start.5 = (f32[3,136,512]{2,1,0:T(8,128)S(1)}, f32[3,136,512]{2,1,0:T(8,128)S(1)}, u32[]{:S(2)}, u32[]{:S(2)}) collective-permute-start(f32[3,136,512]{2,1,0:T(8,128)S(1)} %get-tuple-element.27.second_ref), channel_id=1, source_target_pairs={{1,2},{2,1},{5,6},{6,5},{9,10},{10,9},{13,14},{14,13},{17,18},{18,... | collective-permute-start | bytes 2506760 | tf_op jit(solution)/shard_map/ppermute | solution.py:29
  21.4 2.2 %row_parts.1 = f32[4,3,8,128]{3,2,1,0:T(8,128)S(1)} custom-call(f32[3,136,512]{2,1,0:T(8,128)S(1)} %get-tuple-element.25.first_ref, f32[3,136,512]{2,1,0:T(8,128)S(1)} %get-tuple-element.26.mid_ref, f32[3,136,512]{2,1,0:T(8,128)S(1)} %get-tuple-element.27.second_ref, bf16[3,256,512]{2,1,0:T(8,128)(2,1)S(1)} %get-tuple-element.24.ltp_hbm.ltp_s.ltp_ref, ...), custom_call_target="tpu_custom_call" | custom-call | flops 58982400 | bytes 1048576 | tf_op jit(solution)/shard_map/row_parts/pallas_call | solution.py:43
  23.7 8.1 %all_to_all.10.in_ref = f32[4,3,8,128]{3,2,1,0:T(8,128)S(1)} all-to-all(f32[4,3,8,128]{3,2,1,0:T(8,128)S(1)} %row_parts.1), channel_id=1, replica_groups=mesh['groups'=2,'row'=4,'col'=4] {'row'}, dimensions={0} | all-to-all | bytes 98304 | tf_op jit(solution)/shard_map/all_to_all | solution.py:571
  31.8 6.1 %all-gather = f32[12,8,128]{2,1,0:T(8,128)S(1)} all-gather(f32[3,8,128]{2,1,0:T(8,128)S(1)} %row_join.1), channel_id=2, replica_groups=mesh['groups'=2,'row'=4,'col'=4] {'col'}, dimensions={0}, use_global_device_ids=true | all-gather | bytes 61440 | tf_op jit(solution)/shard_map/all_gather | solution.py:573
  38.0 0.0 collective-permute-done.4.first_ref
  38.0 0.0 collective-permute-done.5.second_ref
  38.0 6.1 %middle.1 = (f32[3,3,128,512]{3,2,1,0:T(8,128)S(1)}, f32[3,3,8,128]{3,2,1,0:T(8,128)S(1)}, f32[4,3,3,8,128]{4,3,2,1,0:T(8,128)S(1)}, f32[8,128]{1,0:T(8,128)S(1)}) custom-call(f32[3,136,512]{2,1,0:T(8,128)S(1)} %collective-permute-done.4.first_ref, f32[3,136,512]{2,1,0:T(8,128)S(1)} %get-tuple-element.26.mid_ref, ...), custom_call_target="tpu_custom_call" | custom-call | flops 117964800 | bytes 1048576 | tf_op jit(solution)/shard_map/middle/pallas_call | solution.py:43
  44.1 9.6 %all_to_all.11.in_ref = f32[4,3,3,8,128]{4,3,2,1,0:T(8,128)S(1)} all-to-all(f32[4,3,3,8,128]{4,3,2,1,0:T(8,128)S(1)} %get-tuple-element.32), channel_id=1, replica_groups=mesh['groups'=2,'row'=4,'col'=4] {'row'}, dimensions={0} | all-to-all | bytes 294912 | tf_op jit(solution)/shard_map/all_to_all | solution.py:596
  53.7 0.1 part_join.1
  53.7 5.6 %all-gather.1 = f32[12,3,8,128]{3,2,1,0:T(8,128)S(1)} all-gather(f32[3,3,8,128]{3,2,1,0:T(8,128)S(1)} %part_join.1), channel_id=3, replica_groups=mesh['groups'=2,'row'=4,'col'=4] {'col'}, dimensions={0}, use_global_device_ids=true | all-gather | bytes 184320 | tf_op jit(solution)/shard_map/all_gather | solution.py:598
  59.3 3.0 %last.1 = (f32[480,128]{1,0:T(8,128)}, f32[6,1,128]{2,1,0:T(1,128)}) custom-call(f32[3,136,512]{2,1,0:T(8,128)S(1)} %collective-permute-done.4.first_ref, f32[3,136,512]{2,1,0:T(8,128)S(1)} %get-tuple-element.26.mid_ref, f32[3,136,512]{2,1,0:T(8,128)S(1)} %collective-permute-done.5.second_ref, f32[3,3,128,512]{3,2,1,0:T(8,128)S(1)} %get-tuple-element.30.e_ref, ...), custom_call_target="tpu_custom_call" | custom-call | flops 58982400 | bytes 1048576 | tf_op jit(solution)/shard_map/last/pallas_call | solution.py:43
  (1 shorter events, 0.0 us)
Async XLA Ops:
  2.0 12.8 %collective-permute-start.1 = (f32[136,512]{1,0:T(8,128)S(1)}, f32[136,512]{1,0:T(8,128)S(1)}, u32[]{:S(2)}, u32[]{:S(2)}) collective-permute-start(f32[136,512]{1,0:T(8,128)S(1)} %get-tuple-element.19.own_ref), channel_id=1, source_target_pairs={{4,8},{8,4},{5,9},{9,5},{6,10},{10,6},{7,11},{11,7},{20,24},{24,20... | collective-permute-start | bytes 835592 | tf_op jit(solution)/shard_map/ppermute | solution.py:29
  2.7 12.3 %collective-permute-start = (f32[136,512]{1,0:T(8,128)S(1)}, f32[136,512]{1,0:T(8,128)S(1)}, u32[]{:S(2)}, u32[]{:S(2)}) collective-permute-start(f32[136,512]{1,0:T(8,128)S(1)} %get-tuple-element.19.own_ref), channel_id=1, source_target_pairs={{0,4},{4,0},{8,12},{12,8},{1,5},{5,1},{9,13},{13,9},{2,6},{6,2},{1... | collective-permute-start | bytes 835592 | tf_op jit(solution)/shard_map/ppermute | solution.py:29
  8.6 5.4 %collective-permute-start.3 = (f32[488,128]{1,0:T(8,128)S(1)}, f32[488,128]{1,0:T(8,128)S(1)}, u32[]{:S(2)}, u32[]{:S(2)}) collective-permute-start(f32[488,128]{1,0:T(8,128)S(1)} %get-tuple-element.23.own_ref), channel_id=1, source_target_pairs={{1,2},{2,1},{5,6},{6,5},{9,10},{10,9},{13,14},{14,13},{17,18},{18,... | collective-permute-start | bytes 749576 | tf_op jit(solution)/shard_map/ppermute | solution.py:29
  9.2 4.8 %collective-permute-start.2 = (f32[488,128]{1,0:T(8,128)S(1)}, f32[488,128]{1,0:T(8,128)S(1)}, u32[]{:S(2)}, u32[]{:S(2)}) collective-permute-start(f32[488,128]{1,0:T(8,128)S(1)} %get-tuple-element.23.own_ref), channel_id=1, source_target_pairs={{0,1},{1,0},{2,3},{3,2},{4,5},{5,4},{6,7},{7,6},{8,9},{9,8},{10,11... | collective-permute-start | bytes 749576 | tf_op jit(solution)/shard_map/ppermute | solution.py:29
  18.9 19.1 %collective-permute-start.4 = (f32[3,136,512]{2,1,0:T(8,128)S(1)}, f32[3,136,512]{2,1,0:T(8,128)S(1)}, u32[]{:S(2)}, u32[]{:S(2)}) collective-permute-start(f32[3,136,512]{2,1,0:T(8,128)S(1)} %get-tuple-element.25.first_ref), channel_id=1, source_target_pairs={{0,1},{1,0},{2,3},{3,2},{4,5},{5,4},{6,7},{7,6},{8,9},{9,8},{10,11... | collective-permute-start | bytes 2506760 | tf_op jit(solution)/shard_map/ppermute | solution.py:29
  20.7 17.3 %collective-permute-start.5 = (f32[3,136,512]{2,1,0:T(8,128)S(1)}, f32[3,136,512]{2,1,0:T(8,128)S(1)}, u32[]{:S(2)}, u32[]{:S(2)}) collective-permute-start(f32[3,136,512]{2,1,0:T(8,128)S(1)} %get-tuple-element.27.second_ref), channel_id=1, source_target_pairs={{1,2},{2,1},{5,6},{6,5},{9,10},{10,9},{13,14},{14,13},{17,18},{18,... | collective-permute-start | bytes 2506760 | tf_op jit(solution)/shard_map/ppermute | solution.py:29

commit v5 on v4

--- a/solution.py
+++ b/solution.py
@@ -263,46 +263,84 @@
     return jnp.concatenate([row[:, k * LANES : (k + 1) * LANES] for k in range(row.shape[1] // LANES)], axis=0)
 
 
-def spread_rows(part_s, out_ref):
-    rows = out_ref.shape[0]
-    half = part_s.shape[-2] // 2
-    shape = out_ref.shape[2:]
-    level = lax.broadcasted_iota(i32, shape, len(shape) - 2)
-    nothing = jnp.where(level < half, NEVER, 0.0)
+def log_sum(top, total):
+    return jnp.where(total > 0.0, top + jnp.log(total), NEVER)
+
+
+def joined(parts):
+    top = functools.reduce(jnp.maximum, parts)
+    return top + jnp.log(sum(jnp.exp(p - top) for p in parts))
+
+
+def device_at(row_step, col_step):
+    rows, cols = lax.axis_size("row"), lax.axis_size("col")
+    row = lax.axis_index("row") + row_step
+    col = lax.axis_index("col") + col_step
+    inside = (row >= 0) & (row < rows) & (col >= 0) & (col < cols)
+    return inside, jnp.clip(row, 0, rows - 1) * cols + jnp.clip(col, 0, cols - 1)
+
+
+def send_first(part_s, out_ref):
+    cols = lax.axis_size("col")
     row = lax.axis_index("row")
-
-    @pl.loop(0, rows)
+    tiles = part_s.shape[1]
+
+    @pl.loop(0, out_ref.shape[0] // cols)
     def _(at):
-        for slot in range(3):
-            source = at - row + slot
+        for q in range(3):
+            source = at - row + q
             inside = (source >= 0) & (source < 3)
-            out_ref[at, slot] = jnp.where(inside, part_s[jnp.clip(source, 0, 2)], nothing)
-
-
-def joined(parts):
-    half = parts[0].shape[-2] // 2
-    tops = [p[..., 0:half, :] for p in parts]
-    top = functools.reduce(jnp.maximum, tops)
-    total = sum(p[..., half:, :] * jnp.exp(m - top) for p, m in zip(parts, tops))
-    return top, total
-
-
-def gather_rows(in_ref):
-    rows = in_ref.shape[0]
-    row = lax.axis_index("row")
-    shape = in_ref.shape[1:]
-    half = shape[-2] // 2
-    level = lax.broadcasted_iota(i32, shape, len(shape) - 2)
-    nothing = jnp.where(level < half, NEVER, 0.0)
-    parts = []
-    for step in range(-2, 3):
-        inside = (row + step >= 0) & (row + step < rows)
-        parts.append(jnp.where(inside, in_ref[jnp.clip(row + step, 0, rows - 1)], nothing))
-    return joined(parts)
-
-
-def told(top, total):
-    return jnp.concatenate([top, jnp.where(total > 0.0, 1.0 / total, 0.0)], axis=-2)
+            part = jnp.where(inside, part_s[jnp.clip(source, 0, 2)], NEVER)
+            for c in range(cols):
+                out_ref[at * cols + c, q * tiles : (q + 1) * tiles, :] = part
+
+
+def receive_first(in_ref, log_s):
+    tiles = log_s.shape[2]
+    for q in range(3):
+        for s in range(3):
+            parts = []
+            for row_step in range(q - 2, q + 1):
+                inside, at = device_at(row_step, s - 1)
+                parts.append(jnp.where(inside, in_ref[at, q * tiles : (q + 1) * tiles, :], NEVER))
+            log_s[q, s] = joined(parts)
+
+
+def place(q, s, row_step, col_step):
+    if row_step == 0:
+        return q * 2 + s - max(0, -col_step)
+    return (q - max(0, -row_step)) * 3 + s
+
+
+def send_second(part_s, out_ref):
+    tiles = part_s.shape[2]
+    for row_step in range(-2, 3):
+        for col_step in range(-2, 3):
+            if row_step == 0 and col_step == 0:
+                continue
+            inside, at = device_at(row_step, col_step)
+
+            @pl.when(inside)
+            def _(row_step=row_step, col_step=col_step, at=at):
+                for q in range(max(0, -row_step), min(3, 3 - row_step)):
+                    for s in range(max(0, -col_step), min(3, 3 - col_step)):
+                        slot = place(q, s, row_step, col_step) * tiles
+                        out_ref[at, slot : slot + tiles, :] = part_s[q + row_step, s + col_step]
+
+
+def receive_second(in_ref, own_ref, log_s):
+    tiles = log_s.shape[2]
+    for q in range(3):
+        for s in range(3):
+            parts = [own_ref[q, s]]
+            for row_step in range(q - 2, q + 1):
+                for col_step in range(s - 2, s + 1):
+                    if row_step == 0 and col_step == 0:
+                        continue
+                    inside, at = device_at(row_step, col_step)
+                    slot = place(q, s, -row_step, -col_step) * tiles
+                    parts.append(jnp.where(inside, in_ref[at, slot : slot + tiles, :], NEVER))
+            log_s[q, s] = joined(parts)
 
 
 def row_parts_kernel(
@@ -330,16 +368,8 @@
                 count = x_refs[side][q, at : at + 8, :]
                 total = total + count * jnp.exp(sc_s[side, at : at + 8, :] - top)
         total = jnp.sum(total, axis=0, keepdims=True)
-        part_s[source] = jnp.concatenate([to_tiles(top), to_tiles(total)], axis=0)
-    spread_rows(part_s, out_ref)
-
-
-def row_join_kernel(in_ref, out_ref):
-    out_ref[...] = told(*gather_rows(in_ref))
-
-
-def part_join_kernel(in_ref, out_ref):
-    out_ref[...] = jnp.concatenate(gather_rows(in_ref), axis=-2)
+        part_s[source] = to_tiles(log_sum(top, total))
+    send_first(part_s, out_ref)
 
 
 def add_moments(p, y0, y1, sums):
@@ -381,33 +411,30 @@
 def middle_kernel(
     genes,
     first_ref, mid_ref, second_ref, ltp_ref, par_ref, state_ref, told_ref,
-    e_ref, m_ref, out_ref, state_out,
-    hot_s, sh_s, mom_s, cnt_s, ltp_s, par_s, gl_s, sc_s, table_s, part_s,
+    e_ref, m_ref, part_ref, out_ref, state_out,
+    hot_s, sh_s, mom_s, cnt_s, ltp_s, par_s, gl_s, sc_s, table_s, log_s,
 ):
     x_refs = (first_ref, mid_ref, second_ref)
     cells, tokens = sc_s.shape[1:]
     tiles = tokens // LANES
     padded = cnt_s.shape[0]
-    cols = told_ref.shape[0]
-    col = lax.axis_index("col")
     mom_s[...] = jnp.zeros(mom_s.shape, f32)
     cnt_s[...] = jnp.zeros(cnt_s.shape, f32)
+    receive_first(told_ref, log_s)
 
     for q, source in enumerate(order("row")):
         for side, x_ref in enumerate(x_refs):
             hot_s[q, side] = gene_hot(x_ref, q, cells, padded)
             gl_s[side] = jnp.dot(ltp_ref[1], hot_s[q, side], preferred_element_type=f32)
         for side, (at_side, x_ref) in enumerate(zip(order("col"), x_refs)):
-            at_col = jnp.clip(col + at_side - 1, 0, cols - 1)
-            top = row_of(told_ref, (at_col, source), 0, tiles)
-            factor = row_of(told_ref, (at_col, source), tiles, tiles)
+            total = row_of(log_s, (source, at_side), 0, tiles)
             y0, y1 = features(x_ref, q, cells, as_float(source) - 1.0, as_float(at_side) - 1.0)
             for at in range(0, cells, 16):
                 halves = []
                 for a in (at, at + 8):
                     score = score_rows(a, y0, y1, gl_s.at[side], par_ref.at[1], cells)
                     count = x_ref[q, a : a + 8, :]
-                    p = count * jnp.exp(jnp.minimum(score - top, 0.0)) * factor
+                    p = count * jnp.exp(jnp.minimum(score - total, 0.0))
                     sums = [mom_s[n, a : a + 8, :] for n in range(6)]
                     sums = add_moments(p, y0, y1, sums)
                     for n in range(6):
@@ -439,39 +466,28 @@
                 e_ref[q, side, at : at + 8, :] = e
                 total = total + e
             total = jnp.sum(total, axis=0, keepdims=True)
-            part_s[source, at_side] = jnp.concatenate([to_tiles(top), to_tiles(total)], axis=0)
-
-    m_ref[...] = part_s[...]
-    spread_rows(part_s, out_ref)
+            m_ref[source, at_side] = to_tiles(top)
+            part_ref[source, at_side] = to_tiles(log_sum(top, total))
+
+    send_second(part_ref, out_ref)
 
 
 def last_kernel(
     genes,
-    first_ref, mid_ref, second_ref, e_ref, m_ref, told_ref, state_ref,
+    first_ref, mid_ref, second_ref, e_ref, m_ref, part_ref, told_ref, state_ref,
     profile_ref, cells_ref,
-    sh_s, mom_s, cnt_s,
+    sh_s, mom_s, cnt_s, log_s,
 ):
     x_refs = (first_ref, mid_ref, second_ref)
     cells, tokens = sh_s.shape[1:]
     tiles = tokens // LANES
-    cols = told_ref.shape[0]
-    col = lax.axis_index("col")
     mom_s[...] = jnp.zeros(mom_s.shape, f32)
     cnt_s[...] = jnp.zeros(cnt_s.shape, f32)
-    shape = m_ref.shape[2:]
-    nothing = jnp.where(lax.broadcasted_iota(i32, shape, 0) < shape[0] // 2, NEVER, 0.0)
+    receive_second(told_ref, part_ref, log_s)
 
     for q, source in enumerate(order("row")):
         for side, (at_side, x_ref) in enumerate(zip(order("col"), x_refs)):
-            parts = []
-            for step in range(-1, 2):
-                owner = col + at_side - 1 + step
-                inside = (owner >= 0) & (owner < cols)
-                part = told_ref[jnp.clip(owner, 0, cols - 1), source, 1 - step]
-                parts.append(jnp.where(inside, part, nothing))
-            top, total = joined(parts)
-            scale = jnp.exp(m_ref[source, at_side][0:tiles] - top)
-            scale = jnp.where(total > 0.0, scale / total, 0.0)
+            scale = jnp.exp(m_ref[source, at_side] - log_s[source, at_side])
             factor = jnp.concatenate([scale[k : k + 1, :] for k in range(tiles)], axis=1)
             y0, y1 = features(x_ref, q, cells, as_float(source) - 1.0, as_float(at_side) - 1.0)
             for at in range(0, cells, 16):
@@ -501,7 +517,7 @@
     cells = profile_weights.shape[3]
     tokens, slots = candidates.shape[2:]
     tiles = tokens // LANES
-    rows = lax.axis_size("row")
+    group = lax.axis_size("row") * lax.axis_size("col")
     padded = padded_to(gene_total, LANES)
     pairs = 9 * tokens * cells
     table = ((padded_to(gene_total, 8) + 8, cells), f32)
@@ -557,20 +573,18 @@
     )
     from_first, from_second = swapped(to_first, to_second, "col")
 
-    chunk = (2 * tiles, LANES)
+    logs = (tiles, LANES)
     parts, = call(
-        row_parts_kernel, "row_parts", [((rows, 3) + chunk, f32)], [VMEM] * 5,
+        row_parts_kernel, "row_parts", [((group, padded_to(3 * tiles, 8), LANES), f32)], [VMEM] * 5,
         [
-            vmem((3,) + chunk, f32),
+            vmem((3,) + logs, f32),
             vmem((3, PARTS * cells, tokens), f32),
             vmem((3, cells, tokens), f32),
         ],
         pairs * 100,
         (to_first, mid, to_second, ltp, par),
     )
-    back = lax.all_to_all(parts, "row", 0, 0)
-    sums, = call(row_join_kernel, "row_join", [((3,) + chunk, f32)], [VMEM], [], tokens * 100, (back,))
-    told_all = lax.all_gather(sums, "col", axis=0)
+    told = lax.all_to_all(parts, ("row", "col"), 0, 0)
 
     x = (from_first, mid, from_second)
     sum_scratch = [
@@ -578,9 +592,15 @@
         vmem((6, cells, LANES), f32),
         vmem((padded, cells), f32),
     ]
-    e, m, parts, state_own = call(
+    e, m, held, parts, state_own = call(
         functools.partial(middle_kernel, gene_total), "middle",
-        [((3, 3, cells, tokens), f32), ((3, 3) + chunk, f32), ((rows, 3, 3) + chunk, f32), state],
+        [
+            ((3, 3, cells, tokens), f32),
+            ((3, 3) + logs, f32),
+            ((3, 3) + logs, f32),
+            ((group, 6 * tiles, LANES), f32),
+            state,
+        ],
         [VMEM] * 7,
         [vmem((3, 3, padded, tokens), bf16)] + sum_scratch + [
             vmem((PARTS * cells, padded), bf16),
@@ -588,19 +608,17 @@
             vmem((3, PARTS * cells, tokens), f32),
             vmem((3, cells, tokens), f32),
             vmem(*table),
-            vmem((3, 3) + chunk, f32),
+            vmem((3, 3) + logs, f32),
         ],
         pairs * 200,
-        (*x, ltp, par, state_own, told_all),
-    )
-    back = lax.all_to_all(parts, "row", 0, 0)
-    sums, = call(part_join_kernel, "part_join", [((3, 3) + chunk, f32)], [VMEM], [], tokens * 100, (back,))
-    told_all = lax.all_gather(sums, "col", axis=0)
+        (*x, ltp, par, state_own, told),
+    )
+    told = lax.all_to_all(parts, ("row", "col"), 0, 0)
     final_profile, final_cells = call(
         functools.partial(last_kernel, gene_total), "last",
         [((gene_total, cells), f32), ((6, 1, cells), f32)],
-        [VMEM] * 7, sum_scratch, pairs * 100,
-        (*x, e, m, told_all, state_own),
+        [VMEM] * 8, sum_scratch + [vmem((3, 3) + logs, f32)], pairs * 100,
+        (*x, e, m, held, told, state_own),
     )
     return (final_profile.reshape(gene_total, 1, 1, cells), final_cells.reshape(6, 1, 1, cells))
 

time: 62.6 us -> 57.8 us (0.923)
  blocking collectives: 29.4 us -> 24.9 us
    all_gather x2 -> x0, blocking collectives: 11.7 us -> none  [body(): told_all = lax.all_gather(sums, 'col', axis=0)]
    all_to_all x2, blocking collectives: 17.7 us -> 24.9 us  [body(): told = lax.all_to_all(parts, ('row', 'col'), 0, 0)]
    pallas_call x9 -> x7, Pallas kernels: 19.3 us -> 19 us  [call(): pl.pallas_call(kernel, name=name, out_shape=shapes, in_specs=in_specs, ou...]
where the time goes in v5:
time: 57.8 us; the launch traced here: 57.5 us
  blocking collectives  24.9 us (43%)
  Pallas kernels  19 us (33%)
  starting transfers between devices  12.7 us (22%)
  between operations  0.72 us (1%)
    all_to_all x2, blocking collectives, body(): told = lax.all_to_all(parts, ('row', 'col'), 0, 0)  24.9 us
    pallas_call x7, Pallas kernels, call(): pl.pallas_call(kernel, name=name, out_shape=shapes, in_specs=in_specs, ou...  19 us
    ppermute x6, starting transfers between devices, swapped(): out.append(lax.ppermute(x, axis, pairs))  12.7 us
  transfers between devices with their start and end apart: 6, of which 1 were waited for; matrix products, arithmetic and copies ran while one was open for 0% of the time, Pallas kernels for 8%

profile of v5, /device:TPU:0, one launch (start us, length us, event | category | flops | bytes accessed | tf_op | source)
XLA Modules:
  0.0 57.5 jit_solution(1829330781446464821)
XLA Ops:
  0.6 1.3 %pack.1 = (f32[136,512]{1,0:T(8,128)S(1)}, f32[488,128]{1,0:T(8,128)S(1)}, f32[8,128]{1,0:T(8,128)S(1)}) custom-call(s32[1,2]{1,0:T(1,128)} %bitcast.20, s32[512,128]{1,0:T(8,128)} %bitcast.14, f32[8,128]{1,0:T(8,128)} %bitcast.16, s32[4,128]{1,0:T(4,128)} %bitcast.17, f32[480,128]{1,0:T(8,128)} %bitcast.15, f32[2,128]{1,0:T(2,128)} %bitcast.18, ...), custom_call_target="tpu_custom_call" | custom-call | flops 65536 | bytes 1048576 | tf_op jit(solution)/shard_map/pack/pallas_call | solution.py:43
  2.0 0.7 %collective-permute-start.1 = (f32[136,512]{1,0:T(8,128)S(1)}, f32[136,512]{1,0:T(8,128)S(1)}, u32[]{:S(2)}, u32[]{:S(2)}) collective-permute-start(f32[136,512]{1,0:T(8,128)S(1)} %get-tuple-element.20.own_ref), channel_id=1, source_target_pairs={{4,8},{8,4},{5,9},{9,5},{6,10},{10,6},{7,11},{11,7},{20,24},{24,20... | collective-permute-start | bytes 835592 | tf_op jit(solution)/shard_map/ppermute | solution.py:29
  2.7 5.9 %collective-permute-start = (f32[136,512]{1,0:T(8,128)S(1)}, f32[136,512]{1,0:T(8,128)S(1)}, u32[]{:S(2)}, u32[]{:S(2)}) collective-permute-start(f32[136,512]{1,0:T(8,128)S(1)} %get-tuple-element.20.own_ref), channel_id=1, source_target_pairs={{0,4},{4,0},{8,12},{12,8},{1,5},{5,1},{9,13},{13,9},{2,6},{6,2},{1... | collective-permute-start | bytes 835592 | tf_op jit(solution)/shard_map/ppermute | solution.py:29
  8.6 0.7 %collective-permute-start.3 = (f32[488,128]{1,0:T(8,128)S(1)}, f32[488,128]{1,0:T(8,128)S(1)}, u32[]{:S(2)}, u32[]{:S(2)}) collective-permute-start(f32[488,128]{1,0:T(8,128)S(1)} %get-tuple-element.24.own_ref), channel_id=1, source_target_pairs={{1,2},{2,1},{5,6},{6,5},{9,10},{10,9},{13,14},{14,13},{17,18},{18,... | collective-permute-start | bytes 749576 | tf_op jit(solution)/shard_map/ppermute | solution.py:29
  9.2 2.9 %collective-permute-start.2 = (f32[488,128]{1,0:T(8,128)S(1)}, f32[488,128]{1,0:T(8,128)S(1)}, u32[]{:S(2)}, u32[]{:S(2)}) collective-permute-start(f32[488,128]{1,0:T(8,128)S(1)} %get-tuple-element.24.own_ref), channel_id=1, source_target_pairs={{0,1},{1,0},{2,3},{3,2},{4,5},{5,4},{6,7},{7,6},{8,9},{9,8},{10,11... | collective-permute-start | bytes 749576 | tf_op jit(solution)/shard_map/ppermute | solution.py:29
  12.2 1.8 %own_counts.1 = (f32[136,512]{1,0:T(8,128)S(1)}, f32[136,512]{1,0:T(8,128)S(1)}, f32[136,512]{1,0:T(8,128)S(1)}) custom-call(f32[136,512]{1,0:T(8,128)S(1)} %get-tuple-element.20.own_ref), custom_call_target="tpu_custom_call" | custom-call | flops 23592960 | bytes 1048576 | tf_op jit(solution)/shard_map/own_counts/pallas_call | solution.py:43
  14.0 0.0 collective-permute-done.3.second_ref
  14.0 0.0 collective-permute-done.2.first_ref
  14.0 0.7 %tables.1 = (bf16[3,256,512]{2,1,0:T(8,128)(2,1)S(1)}, f32[3,6,128,128]{3,2,1,0:T(8,128)S(1)}) custom-call(f32[488,128]{1,0:T(8,128)S(1)} %collective-permute-done.2.first_ref, f32[488,128]{1,0:T(8,128)S(1)} %get-tuple-element.24.own_ref, f32[488,128]{1,0:T(8,128)S(1)} %collective-permute-done.3.second_ref), custom_call_target="tpu_custom_call" | custom-call | flops 65536 | bytes 1048576 | tf_op jit(solution)/shard_map/tables/pallas_call | solution.py:43
  14.7 0.0 collective-permute-done.1.second_ref
  14.7 0.2 collective-permute-done.first_ref
  15.0 3.9 %counts.1 = (f32[3,136,512]{2,1,0:T(8,128)S(1)}, f32[3,136,512]{2,1,0:T(8,128)S(1)}, f32[3,136,512]{2,1,0:T(8,128)S(1)}) custom-call(f32[136,512]{1,0:T(8,128)S(1)} %collective-permute-done.first_ref, f32[136,512]{1,0:T(8,128)S(1)} %collective-permute-done.1.second_ref, f32[136,512]{1,0:T(8,128)S(1)} %get-tuple-element.21.own_first, ...), custom_call_target="tpu_custom_call" | custom-call | flops 47185920 | bytes 1048576 | tf_op jit(solution)/shard_map/counts/pallas_call | solution.py:43
  18.9 1.9 %collective-permute-start.4 = (f32[3,136,512]{2,1,0:T(8,128)S(1)}, f32[3,136,512]{2,1,0:T(8,128)S(1)}, u32[]{:S(2)}, u32[]{:S(2)}) collective-permute-start(f32[3,136,512]{2,1,0:T(8,128)S(1)} %get-tuple-element.26.first_ref), channel_id=1, source_target_pairs={{0,1},{1,0},{2,3},{3,2},{4,5},{5,4},{6,7},{7,6},{8,9},{9,8},{10,11... | collective-permute-start | bytes 2506760 | tf_op jit(solution)/shard_map/ppermute | solution.py:29
  20.7 0.7 %collective-permute-start.5 = (f32[3,136,512]{2,1,0:T(8,128)S(1)}, f32[3,136,512]{2,1,0:T(8,128)S(1)}, u32[]{:S(2)}, u32[]{:S(2)}) collective-permute-start(f32[3,136,512]{2,1,0:T(8,128)S(1)} %get-tuple-element.28.second_ref), channel_id=1, source_target_pairs={{1,2},{2,1},{5,6},{6,5},{9,10},{10,9},{13,14},{14,13},{17,18},{18,... | collective-permute-start | bytes 2506760 | tf_op jit(solution)/shard_map/ppermute | solution.py:29
  21.4 2.1 %row_parts.1 = f32[16,16,128]{2,1,0:T(8,128)S(1)} custom-call(f32[3,136,512]{2,1,0:T(8,128)S(1)} %get-tuple-element.26.first_ref, f32[3,136,512]{2,1,0:T(8,128)S(1)} %get-tuple-element.27.mid_ref, f32[3,136,512]{2,1,0:T(8,128)S(1)} %get-tuple-element.28.second_ref, bf16[3,256,512]{2,1,0:T(8,128)(2,1)S(1)} %get-tuple-element.25.ltp_hbm.ltp_s.ltp_ref, ...), custom_call_target="tpu_custom_call" | custom-call | flops 58982400 | bytes 1048576 | tf_op jit(solution)/shard_map/row_parts/pallas_call | solution.py:43
  23.5 13.0 %all_to_all.10.told_ref = f32[16,16,128]{2,1,0:T(8,128)S(1)} all-to-all(f32[16,16,128]{2,1,0:T(8,128)S(1)} %row_parts.1), channel_id=1, replica_groups=mesh['groups'=2,'row'=4,'col'=4] {'row','col'}, dimensions={0} | all-to-all | bytes 262144 | tf_op jit(solution)/shard_map/all_to_all | solution.py:587
  36.5 0.0 collective-permute-done.4.first_ref
  36.5 0.0 collective-permute-done.5.second_ref
  36.5 5.9 %middle.1 = (f32[3,3,128,512]{3,2,1,0:T(8,128)S(1)}, f32[3,3,4,128]{3,2,1,0:T(4,128)S(1)}, f32[3,3,4,128]{3,2,1,0:T(4,128)S(1)}, f32[16,24,128]{2,1,0:T(8,128)S(1)}, f32[8,128]{1,0:T(8,128)S(1)}) custom-call(f32[3,136,512]{2,1,0:T(8,128)S(1)} %collective-permute-done.4.first_ref, f32[3,136,512]{2,1,0:T(8,128)S(1)} %get-tuple-element.27.mid_ref, ...), custom_call_target="tpu_custom_call" | custom-call | flops 117964800 | bytes 1048576 | tf_op jit(solution)/shard_map/middle/pallas_call | solution.py:43
  42.4 11.9 %all_to_all.11.told_ref = f32[16,24,128]{2,1,0:T(8,128)S(1)} all-to-all(f32[16,24,128]{2,1,0:T(8,128)S(1)} %get-tuple-element.34), channel_id=1, replica_groups=mesh['groups'=2,'row'=4,'col'=4] {'row','col'}, dimensions={0} | all-to-all | bytes 393216 | tf_op jit(solution)/shard_map/all_to_all | solution.py:616
  54.3 3.2 %last.1 = (f32[480,128]{1,0:T(8,128)}, f32[6,1,128]{2,1,0:T(1,128)}) custom-call(f32[3,136,512]{2,1,0:T(8,128)S(1)} %collective-permute-done.4.first_ref, f32[3,136,512]{2,1,0:T(8,128)S(1)} %get-tuple-element.27.mid_ref, f32[3,136,512]{2,1,0:T(8,128)S(1)} %collective-permute-done.5.second_ref, f32[3,3,128,512]{3,2,1,0:T(8,128)S(1)} %get-tuple-element.31.e_ref, ...), custom_call_target="tpu_custom_call" | custom-call | flops 58982400 | bytes 1048576 | tf_op jit(solution)/shard_map/last/pallas_call | solution.py:43
Async XLA Ops:
  2.0 12.8 %collective-permute-start.1 = (f32[136,512]{1,0:T(8,128)S(1)}, f32[136,512]{1,0:T(8,128)S(1)}, u32[]{:S(2)}, u32[]{:S(2)}) collective-permute-start(f32[136,512]{1,0:T(8,128)S(1)} %get-tuple-element.20.own_ref), channel_id=1, source_target_pairs={{4,8},{8,4},{5,9},{9,5},{6,10},{10,6},{7,11},{11,7},{20,24},{24,20... | collective-permute-start | bytes 835592 | tf_op jit(solution)/shard_map/ppermute | solution.py:29
  2.7 12.3 %collective-permute-start = (f32[136,512]{1,0:T(8,128)S(1)}, f32[136,512]{1,0:T(8,128)S(1)}, u32[]{:S(2)}, u32[]{:S(2)}) collective-permute-start(f32[136,512]{1,0:T(8,128)S(1)} %get-tuple-element.20.own_ref), channel_id=1, source_target_pairs={{0,4},{4,0},{8,12},{12,8},{1,5},{5,1},{9,13},{13,9},{2,6},{6,2},{1... | collective-permute-start | bytes 835592 | tf_op jit(solution)/shard_map/ppermute | solution.py:29
  8.6 5.4 %collective-permute-start.3 = (f32[488,128]{1,0:T(8,128)S(1)}, f32[488,128]{1,0:T(8,128)S(1)}, u32[]{:S(2)}, u32[]{:S(2)}) collective-permute-start(f32[488,128]{1,0:T(8,128)S(1)} %get-tuple-element.24.own_ref), channel_id=1, source_target_pairs={{1,2},{2,1},{5,6},{6,5},{9,10},{10,9},{13,14},{14,13},{17,18},{18,... | collective-permute-start | bytes 749576 | tf_op jit(solution)/shard_map/ppermute | solution.py:29
  9.2 4.8 %collective-permute-start.2 = (f32[488,128]{1,0:T(8,128)S(1)}, f32[488,128]{1,0:T(8,128)S(1)}, u32[]{:S(2)}, u32[]{:S(2)}) collective-permute-start(f32[488,128]{1,0:T(8,128)S(1)} %get-tuple-element.24.own_ref), channel_id=1, source_target_pairs={{0,1},{1,0},{2,3},{3,2},{4,5},{5,4},{6,7},{7,6},{8,9},{9,8},{10,11... | collective-permute-start | bytes 749576 | tf_op jit(solution)/shard_map/ppermute | solution.py:29
  18.9 17.6 %collective-permute-start.4 = (f32[3,136,512]{2,1,0:T(8,128)S(1)}, f32[3,136,512]{2,1,0:T(8,128)S(1)}, u32[]{:S(2)}, u32[]{:S(2)}) collective-permute-start(f32[3,136,512]{2,1,0:T(8,128)S(1)} %get-tuple-element.26.first_ref), channel_id=1, source_target_pairs={{0,1},{1,0},{2,3},{3,2},{4,5},{5,4},{6,7},{7,6},{8,9},{9,8},{10,11... | collective-permute-start | bytes 2506760 | tf_op jit(solution)/shard_map/ppermute | solution.py:29
  20.7 15.8 %collective-permute-start.5 = (f32[3,136,512]{2,1,0:T(8,128)S(1)}, f32[3,136,512]{2,1,0:T(8,128)S(1)}, u32[]{:S(2)}, u32[]{:S(2)}) collective-permute-start(f32[3,136,512]{2,1,0:T(8,128)S(1)} %get-tuple-element.28.second_ref), channel_id=1, source_target_pairs={{1,2},{2,1},{5,6},{6,5},{9,10},{10,9},{13,14},{14,13},{17,18},{18,... | collective-permute-start | bytes 2506760 | tf_op jit(solution)/shard_map/ppermute | solution.py:29

commit v6 on v5

--- a/solution.py
+++ b/solution.py
@@ -142,51 +142,69 @@
     table_ref[...] = table_rows(profile, state, jnp.zeros_like(spread_row))
 
 
+def full_add(a, b, c):
+    both = a ^ b
+    return both ^ c, (a & b) | (both & c)
+
+
 def count_source(source, z_ref, cells, outs, word_s, unit_s):
     rows, tokens = z_ref.shape
     slots = rows - FEATURES
-    words = cells // 8
     shift = cells.bit_length() - 1
-    word_shift = words.bit_length() - 1
-    held = 3 * words // 8
-    per_tile = words // 8
+    held = cells // 64
+    planes = slots.bit_length()
     sub = lax.broadcasted_iota(i32, (8, LANES), 0)
-    nibbles = jnp.full((8, LANES), 0x0F0F0F0F, i32)
     first = order("col")[0]
     for k in range(tokens // LANES):
         local = z_ref[0:slots, lane_tile(k)].astype(i32) - (2 - source) * 3 * cells
-        place = first + (local >> shift) * (1 - first)
-        word_s[k, 0:slots, :] = place * words + (local & (words - 1))
-        unit_s[k, 0:slots, :] = 1 << (((local & (cells - 1)) >> word_shift) * 4)
-
-    def some(k, start, amount, carry):
-        low, high = carry
-        word = [jnp.zeros((8, LANES), i32) for _ in range(held)]
-        for j in range(amount):
-            which = word_s[k, pl.ds(start + j, 8, stride=0), :]
-            unit = unit_s[k, pl.ds(start + j, 8, stride=0), :]
+        tile = first + (local >> shift) * (1 - first)
+        cell = local & (cells - 1)
+        live = z_ref[slots + 3 : slots + 4, lane_tile(k)] > 0.0
+        named = (tile >= 0) & (tile < 3) & live
+        word_s[k, 0:slots, :] = ((cell >> 6) << 3) | (cell & 7)
+        unit_s[k, 0:slots, :] = jnp.where(named, 1 << (((tile & 3) << 3) | ((cell >> 3) & 7)), 0)
+
+    for k in range(tokens // LANES):
+
+        def group(g, carry):
+            bits = [[] for _ in range(held)]
+            for j in range(16):
+                which = word_s[k, pl.ds(g * 16 + j, 8, stride=0), :]
+                unit = unit_s[k, pl.ds(g * 16 + j, 8, stride=0), :]
+                for n in range(held):
+                    bits[n].append(jnp.where(which == sub + 8 * n, unit, 0))
+            out = []
             for n in range(held):
-                word[n] = word[n] + jnp.where(which == sub + 8 * n, unit, 0)
-        low = [a + (w & nibbles) for a, w in zip(low, word)]
-        high = [a + ((w >> 4) & nibbles) for a, w in zip(high, word)]
-        return low, high
-
-    for k in range(tokens // LANES):
-        zero = [jnp.zeros((8, LANES), i32) for _ in range(held)]
-        whole = slots // 15
-        carry = lax.fori_loop(
-            0, whole, lambda g, carry: some(k, g * 15, 15, carry), (zero, list(zero))
-        )
-        if slots % 15:
-            carry = some(k, whole * 15, slots % 15, carry)
-        low, high = carry
-        live = z_ref[slots + 3 : slots + 4, lane_tile(k)]
+                plane = list(carry[n])
+                level = bits[n]
+                for p in range(4):
+                    following = []
+                    for a in range(0, len(level), 2):
+                        plane[p], over = full_add(plane[p], level[a], level[a + 1])
+                        following.append(over)
+                    level = following
+                over = level[0]
+                for p in range(4, planes):
+                    plane[p], over = plane[p] ^ over, plane[p] & over
+                out.append(plane)
+            return out
+
+        zero = jnp.zeros((8, LANES), i32)
+        total = lax.fori_loop(0, slots // 16, group, [[zero] * planes for _ in range(held)], unroll=True)
         for n in range(held):
-            for field in range(8):
-                part = low[n] if field % 2 == 0 else high[n]
-                value = ((part >> (8 * (field // 2))) & 255).astype(f32) * live
-                row = field * words + (n % per_tile) * 8
-                outs[n // per_tile][row : row + 8, lane_tile(k)] = value
+            for r in range(8):
+                value = zero
+                for p in range(planes):
+                    moved = total[n][p]
+                    if r > p:
+                        moved = moved >> (r - p)
+                    elif r < p:
+                        moved = moved << (p - r)
+                    value = value | (moved & (0x00010101 << p))
+                row = n * 64 + r * 8
+                for tile, out in enumerate(outs):
+                    part = value & 255 if tile == 0 else (value >> (8 * tile)) & 255
+                    out[row : row + 8, lane_tile(k)] = part.astype(f32)
     for out in outs:
         out[cells : cells + FEATURES, :] = z_ref[slots : slots + FEATURES, :]
 

time: 57.8 us -> 56.8 us (0.983)
  Pallas kernels: 19 us -> 17.5 us
    pallas_call x7, Pallas kernels: 19 us -> 17.5 us  [call(): pl.pallas_call(kernel, name=name, out_shape=shapes, in_specs=in_specs, ou...]
  transfers between devices with their start and end apart: 6 -> 6, of which waited for: 1 -> 1; matrix products, arithmetic and copies ran while one was open for 0% -> 0% of each run, Pallas kernels for 8% -> 7%
where the time goes in v6:
time: 56.8 us; the launch traced here: 56.5 us
  blocking collectives  24.9 us (44%)
  Pallas kernels  17.5 us (31%)
  starting transfers between devices  12.7 us (22%)
  between operations  0.71 us (1%)
  waiting for transfers between devices  0.68 us (1%)
    all_to_all x2, blocking collectives, body(): told = lax.all_to_all(parts, ('row', 'col'), 0, 0)  24.9 us
    pallas_call x7, Pallas kernels, call(): pl.pallas_call(kernel, name=name, out_shape=shapes, in_specs=in_specs, ou...  17.5 us
    ppermute x6, starting transfers between devices, swapped(): out.append(lax.ppermute(x, axis, pairs))  12.7 us
  transfers between devices with their start and end apart: 6, of which 1 were waited for; matrix products, arithmetic and copies ran while one was open for 0% of the time, Pallas kernels for 7%

profile of v6, /device:TPU:0, one launch (start us, length us, event | category | flops | bytes accessed | tf_op | source)
XLA Modules:
  0.0 56.5 jit_solution(16182681180341377991)
XLA Ops:
  0.6 1.3 %pack.1 = (f32[136,512]{1,0:T(8,128)S(1)}, f32[488,128]{1,0:T(8,128)S(1)}, f32[8,128]{1,0:T(8,128)S(1)}) custom-call(s32[1,2]{1,0:T(1,128)} %bitcast.20, s32[512,128]{1,0:T(8,128)} %bitcast.14, f32[8,128]{1,0:T(8,128)} %bitcast.16, s32[4,128]{1,0:T(4,128)} %bitcast.17, f32[480,128]{1,0:T(8,128)} %bitcast.15, f32[2,128]{1,0:T(2,128)} %bitcast.18, ...), custom_call_target="tpu_custom_call" | custom-call | flops 65536 | bytes 1048576 | tf_op jit(solution)/shard_map/pack/pallas_call | solution.py:43
  2.0 0.7 %collective-permute-start.1 = (f32[136,512]{1,0:T(8,128)S(1)}, f32[136,512]{1,0:T(8,128)S(1)}, u32[]{:S(2)}, u32[]{:S(2)}) collective-permute-start(f32[136,512]{1,0:T(8,128)S(1)} %get-tuple-element.20.own_ref), channel_id=1, source_target_pairs={{4,8},{8,4},{5,9},{9,5},{6,10},{10,6},{7,11},{11,7},{20,24},{24,20... | collective-permute-start | bytes 835592 | tf_op jit(solution)/shard_map/ppermute | solution.py:29
  2.7 5.9 %collective-permute-start = (f32[136,512]{1,0:T(8,128)S(1)}, f32[136,512]{1,0:T(8,128)S(1)}, u32[]{:S(2)}, u32[]{:S(2)}) collective-permute-start(f32[136,512]{1,0:T(8,128)S(1)} %get-tuple-element.20.own_ref), channel_id=1, source_target_pairs={{0,4},{4,0},{8,12},{12,8},{1,5},{5,1},{9,13},{13,9},{2,6},{6,2},{1... | collective-permute-start | bytes 835592 | tf_op jit(solution)/shard_map/ppermute | solution.py:29
  8.6 0.7 %collective-permute-start.3 = (f32[488,128]{1,0:T(8,128)S(1)}, f32[488,128]{1,0:T(8,128)S(1)}, u32[]{:S(2)}, u32[]{:S(2)}) collective-permute-start(f32[488,128]{1,0:T(8,128)S(1)} %get-tuple-element.24.own_ref), channel_id=1, source_target_pairs={{1,2},{2,1},{5,6},{6,5},{9,10},{10,9},{13,14},{14,13},{17,18},{18,... | collective-permute-start | bytes 749576 | tf_op jit(solution)/shard_map/ppermute | solution.py:29
  9.2 2.9 %collective-permute-start.2 = (f32[488,128]{1,0:T(8,128)S(1)}, f32[488,128]{1,0:T(8,128)S(1)}, u32[]{:S(2)}, u32[]{:S(2)}) collective-permute-start(f32[488,128]{1,0:T(8,128)S(1)} %get-tuple-element.24.own_ref), channel_id=1, source_target_pairs={{0,1},{1,0},{2,3},{3,2},{4,5},{5,4},{6,7},{7,6},{8,9},{9,8},{10,11... | collective-permute-start | bytes 749576 | tf_op jit(solution)/shard_map/ppermute | solution.py:29
  12.2 1.4 %own_counts.1 = (f32[136,512]{1,0:T(8,128)S(1)}, f32[136,512]{1,0:T(8,128)S(1)}, f32[136,512]{1,0:T(8,128)S(1)}) custom-call(f32[136,512]{1,0:T(8,128)S(1)} %get-tuple-element.20.own_ref), custom_call_target="tpu_custom_call" | custom-call | flops 23592960 | bytes 1048576 | tf_op jit(solution)/shard_map/own_counts/pallas_call | solution.py:43
  13.5 0.0 collective-permute-done.3.second_ref
  13.5 0.0 collective-permute-done.2.first_ref
  13.6 0.7 %tables.1 = (bf16[3,256,512]{2,1,0:T(8,128)(2,1)S(1)}, f32[3,6,128,128]{3,2,1,0:T(8,128)S(1)}) custom-call(f32[488,128]{1,0:T(8,128)S(1)} %collective-permute-done.2.first_ref, f32[488,128]{1,0:T(8,128)S(1)} %get-tuple-element.24.own_ref, f32[488,128]{1,0:T(8,128)S(1)} %collective-permute-done.3.second_ref), custom_call_target="tpu_custom_call" | custom-call | flops 65536 | bytes 1048576 | tf_op jit(solution)/shard_map/tables/pallas_call | solution.py:43
  14.3 0.0 collective-permute-done.1.second_ref
  14.3 0.7 %collective-permute-done.first_ref = f32[136,512]{1,0:T(8,128)S(1)} collective-permute-done((f32[136,512]{1,0:T(8,128)S(1)}, f32[136,512]{1,0:T(8,128)S(1)}, u32[]{:S(2)}, u32[]{:S(2)}) %collective-permute-start) | collective-permute-done | bytes 278560 | tf_op jit(solution)/shard_map/ppermute | solution.py:29
  15.0 2.9 %counts.1 = (f32[3,136,512]{2,1,0:T(8,128)S(1)}, f32[3,136,512]{2,1,0:T(8,128)S(1)}, f32[3,136,512]{2,1,0:T(8,128)S(1)}) custom-call(f32[136,512]{1,0:T(8,128)S(1)} %collective-permute-done.first_ref, f32[136,512]{1,0:T(8,128)S(1)} %collective-permute-done.1.second_ref, f32[136,512]{1,0:T(8,128)S(1)} %get-tuple-element.21.own_first, ...), custom_call_target="tpu_custom_call" | custom-call | flops 47185920 | bytes 1048576 | tf_op jit(solution)/shard_map/counts/pallas_call | solution.py:43
  17.8 1.9 %collective-permute-start.4 = (f32[3,136,512]{2,1,0:T(8,128)S(1)}, f32[3,136,512]{2,1,0:T(8,128)S(1)}, u32[]{:S(2)}, u32[]{:S(2)}) collective-permute-start(f32[3,136,512]{2,1,0:T(8,128)S(1)} %get-tuple-element.26.first_ref), channel_id=1, source_target_pairs={{0,1},{1,0},{2,3},{3,2},{4,5},{5,4},{6,7},{7,6},{8,9},{9,8},{10,11... | collective-permute-start | bytes 2506760 | tf_op jit(solution)/shard_map/ppermute | solution.py:29
  19.7 0.7 %collective-permute-start.5 = (f32[3,136,512]{2,1,0:T(8,128)S(1)}, f32[3,136,512]{2,1,0:T(8,128)S(1)}, u32[]{:S(2)}, u32[]{:S(2)}) collective-permute-start(f32[3,136,512]{2,1,0:T(8,128)S(1)} %get-tuple-element.28.second_ref), channel_id=1, source_target_pairs={{1,2},{2,1},{5,6},{6,5},{9,10},{10,9},{13,14},{14,13},{17,18},{18,... | collective-permute-start | bytes 2506760 | tf_op jit(solution)/shard_map/ppermute | solution.py:29
  20.4 2.1 %row_parts.1 = f32[16,16,128]{2,1,0:T(8,128)S(1)} custom-call(f32[3,136,512]{2,1,0:T(8,128)S(1)} %get-tuple-element.26.first_ref, f32[3,136,512]{2,1,0:T(8,128)S(1)} %get-tuple-element.27.mid_ref, f32[3,136,512]{2,1,0:T(8,128)S(1)} %get-tuple-element.28.second_ref, bf16[3,256,512]{2,1,0:T(8,128)(2,1)S(1)} %get-tuple-element.25.ltp_hbm.ltp_s.ltp_ref, ...), custom_call_target="tpu_custom_call" | custom-call | flops 58982400 | bytes 1048576 | tf_op jit(solution)/shard_map/row_parts/pallas_call | solution.py:43
  22.5 13.0 %all_to_all.10.told_ref = f32[16,16,128]{2,1,0:T(8,128)S(1)} all-to-all(f32[16,16,128]{2,1,0:T(8,128)S(1)} %row_parts.1), channel_id=1, replica_groups=mesh['groups'=2,'row'=4,'col'=4] {'row','col'}, dimensions={0} | all-to-all | bytes 262144 | tf_op jit(solution)/shard_map/all_to_all | solution.py:605
  35.5 0.0 collective-permute-done.4.first_ref
  35.5 0.0 collective-permute-done.5.second_ref
  35.5 5.9 %middle.1 = (f32[3,3,128,512]{3,2,1,0:T(8,128)S(1)}, f32[3,3,4,128]{3,2,1,0:T(4,128)S(1)}, f32[3,3,4,128]{3,2,1,0:T(4,128)S(1)}, f32[16,24,128]{2,1,0:T(8,128)S(1)}, f32[8,128]{1,0:T(8,128)S(1)}) custom-call(f32[3,136,512]{2,1,0:T(8,128)S(1)} %collective-permute-done.4.first_ref, f32[3,136,512]{2,1,0:T(8,128)S(1)} %get-tuple-element.27.mid_ref, ...), custom_call_target="tpu_custom_call" | custom-call | flops 117964800 | bytes 1048576 | tf_op jit(solution)/shard_map/middle/pallas_call | solution.py:43
  41.4 11.9 %all_to_all.11.told_ref = f32[16,24,128]{2,1,0:T(8,128)S(1)} all-to-all(f32[16,24,128]{2,1,0:T(8,128)S(1)} %get-tuple-element.34), channel_id=1, replica_groups=mesh['groups'=2,'row'=4,'col'=4] {'row','col'}, dimensions={0} | all-to-all | bytes 393216 | tf_op jit(solution)/shard_map/all_to_all | solution.py:634
  53.3 3.2 %last.1 = (f32[480,128]{1,0:T(8,128)}, f32[6,1,128]{2,1,0:T(1,128)}) custom-call(f32[3,136,512]{2,1,0:T(8,128)S(1)} %collective-permute-done.4.first_ref, f32[3,136,512]{2,1,0:T(8,128)S(1)} %get-tuple-element.27.mid_ref, f32[3,136,512]{2,1,0:T(8,128)S(1)} %collective-permute-done.5.second_ref, f32[3,3,128,512]{3,2,1,0:T(8,128)S(1)} %get-tuple-element.31.e_ref, ...), custom_call_target="tpu_custom_call" | custom-call | flops 58982400 | bytes 1048576 | tf_op jit(solution)/shard_map/last/pallas_call | solution.py:43
Async XLA Ops:
  2.0 12.3 %collective-permute-start.1 = (f32[136,512]{1,0:T(8,128)S(1)}, f32[136,512]{1,0:T(8,128)S(1)}, u32[]{:S(2)}, u32[]{:S(2)}) collective-permute-start(f32[136,512]{1,0:T(8,128)S(1)} %get-tuple-element.20.own_ref), channel_id=1, source_target_pairs={{4,8},{8,4},{5,9},{9,5},{6,10},{10,6},{7,11},{11,7},{20,24},{24,20... | collective-permute-start | bytes 835592 | tf_op jit(solution)/shard_map/ppermute | solution.py:29
  2.7 12.3 %collective-permute-start = (f32[136,512]{1,0:T(8,128)S(1)}, f32[136,512]{1,0:T(8,128)S(1)}, u32[]{:S(2)}, u32[]{:S(2)}) collective-permute-start(f32[136,512]{1,0:T(8,128)S(1)} %get-tuple-element.20.own_ref), channel_id=1, source_target_pairs={{0,4},{4,0},{8,12},{12,8},{1,5},{5,1},{9,13},{13,9},{2,6},{6,2},{1... | collective-permute-start | bytes 835592 | tf_op jit(solution)/shard_map/ppermute | solution.py:29
  8.6 5.0 %collective-permute-start.3 = (f32[488,128]{1,0:T(8,128)S(1)}, f32[488,128]{1,0:T(8,128)S(1)}, u32[]{:S(2)}, u32[]{:S(2)}) collective-permute-start(f32[488,128]{1,0:T(8,128)S(1)} %get-tuple-element.24.own_ref), channel_id=1, source_target_pairs={{1,2},{2,1},{5,6},{6,5},{9,10},{10,9},{13,14},{14,13},{17,18},{18,... | collective-permute-start | bytes 749576 | tf_op jit(solution)/shard_map/ppermute | solution.py:29
  9.2 4.3 %collective-permute-start.2 = (f32[488,128]{1,0:T(8,128)S(1)}, f32[488,128]{1,0:T(8,128)S(1)}, u32[]{:S(2)}, u32[]{:S(2)}) collective-permute-start(f32[488,128]{1,0:T(8,128)S(1)} %get-tuple-element.24.own_ref), channel_id=1, source_target_pairs={{0,1},{1,0},{2,3},{3,2},{4,5},{5,4},{6,7},{7,6},{8,9},{9,8},{10,11... | collective-permute-start | bytes 749576 | tf_op jit(solution)/shard_map/ppermute | solution.py:29
  17.8 17.6 %collective-permute-start.4 = (f32[3,136,512]{2,1,0:T(8,128)S(1)}, f32[3,136,512]{2,1,0:T(8,128)S(1)}, u32[]{:S(2)}, u32[]{:S(2)}) collective-permute-start(f32[3,136,512]{2,1,0:T(8,128)S(1)} %get-tuple-element.26.first_ref), channel_id=1, source_target_pairs={{0,1},{1,0},{2,3},{3,2},{4,5},{5,4},{6,7},{7,6},{8,9},{9,8},{10,11... | collective-permute-start | bytes 2506760 | tf_op jit(solution)/shard_map/ppermute | solution.py:29
  19.7 15.8 %collective-permute-start.5 = (f32[3,136,512]{2,1,0:T(8,128)S(1)}, f32[3,136,512]{2,1,0:T(8,128)S(1)}, u32[]{:S(2)}, u32[]{:S(2)}) collective-permute-start(f32[3,136,512]{2,1,0:T(8,128)S(1)} %get-tuple-element.28.second_ref), channel_id=1, source_target_pairs={{1,2},{2,1},{5,6},{6,5},{9,10},{10,9},{13,14},{14,13},{17,18},{18,... | collective-permute-start | bytes 2506760 | tf_op jit(solution)/shard_map/ppermute | solution.py:29

commit v7 on v6

--- a/solution.py
+++ b/solution.py
@@ -6,6 +6,7 @@
 from jax.experimental import pallas as pl
 from jax.experimental.pallas import tpu as pltpu
 from jax.sharding import PartitionSpec as P
+
 
 BLOCK = 256
 LANES = 128
@@ -38,11 +39,10 @@
     return pl.CostEstimate(flops=flops, bytes_accessed=size, transcendentals=0)
 
 
-def call(kernel, name, outs, in_specs, scratch, flops, args):
+def call(kernel, outs, in_specs, scratch, flops, args):
     shapes = [jax.ShapeDtypeStruct(s, d) for s, d in outs]
     return pl.pallas_call(
         kernel,
-        name=name,
         out_shape=shapes,
         in_specs=in_specs,
         out_specs=[pl.BlockSpec(memory_space=pltpu.VMEM)] * len(shapes),
@@ -214,7 +214,7 @@
 
 
 def counts_kernel(
-    cells, first_ref, second_ref, own_first, own_mid, own_second, ltp_hbm,
+    cells, first_ref, second_ref, own_first, own_mid, own_second,
     to_first, mid_ref, to_second, word_s, unit_s,
 ):
     outs = (to_first, mid_ref, to_second)
@@ -543,7 +543,7 @@
     vmem = pltpu.VMEM
 
     packed, table_own, state_own = call(
-        pack_kernel, "pack", [((slots + FEATURES, tokens), f32), table, state],
+        pack_kernel, [((slots + FEATURES, tokens), f32), table, state],
         [ANY] * 8,
         [
             vmem((1, block_counts.shape[2]), i32),
@@ -574,7 +574,7 @@
     row_first, row_second = swapped(packed, packed, "row")
     table_first, table_second = swapped(table_own, table_own, "col")
     ltp, par = call(
-        tables_kernel, "tables",
+        tables_kernel,
         [((3, PARTS * cells, padded), bf16), ((3, 6, cells, LANES), f32)], [VMEM] * 3, [],
         tokens * slots, (table_first, table_own, table_second),
     )
@@ -582,18 +582,18 @@
     three = ((3, cells + FEATURES, tokens), f32)
     count_scratch = [vmem((tiles, slots + 8, LANES), i32)] * 2
     own = call(
-        functools.partial(own_counts_kernel, cells), "own_counts", [one] * 3, [VMEM],
+        functools.partial(own_counts_kernel, cells), [one] * 3, [VMEM],
         count_scratch, pairs * 40, (packed,),
     )
     to_first, mid, to_second = call(
-        functools.partial(counts_kernel, cells), "counts", [three] * 3, [VMEM] * 5 + [ANY],
-        count_scratch, pairs * 80, (row_first, row_second, *own, ltp),
+        functools.partial(counts_kernel, cells), [three] * 3, [VMEM] * 5,
+        count_scratch, pairs * 80, (row_first, row_second, *own),
     )
     from_first, from_second = swapped(to_first, to_second, "col")
 
     logs = (tiles, LANES)
     parts, = call(
-        row_parts_kernel, "row_parts", [((group, padded_to(3 * tiles, 8), LANES), f32)], [VMEM] * 5,
+        row_parts_kernel, [((group, padded_to(3 * tiles, 8), LANES), f32)], [VMEM] * 5,
         [
             vmem((3,) + logs, f32),
             vmem((3, PARTS * cells, tokens), f32),
@@ -611,7 +611,7 @@
         vmem((padded, cells), f32),
     ]
     e, m, held, parts, state_own = call(
-        functools.partial(middle_kernel, gene_total), "middle",
+        functools.partial(middle_kernel, gene_total),
         [
             ((3, 3, cells, tokens), f32),
             ((3, 3) + logs, f32),
@@ -633,7 +633,7 @@
     )
     told = lax.all_to_all(parts, ("row", "col"), 0, 0)
     final_profile, final_cells = call(
-        functools.partial(last_kernel, gene_total), "last",
+        functools.partial(last_kernel, gene_total),
         [((gene_total, cells), f32), ((6, 1, cells), f32)],
         [VMEM] * 8, sum_scratch + [vmem((3, 3) + logs, f32)], pairs * 100,
         (*x, e, m, held, told, state_own),
@@ -642,8 +642,8 @@
 
 
 def solution(mesh):
-    tiles = P(("groups", "row"), "col")
     stacked = P(None, ("groups", "row"), "col", None)
+
     return jax.shard_map(
         body,
         mesh=mesh,

time: 56.8 us -> 69.8 us (1.23)
  blocking collectives: 24.9 us -> 32.5 us
  waiting for transfers between devices: 0.68 us -> 6.13 us
    all_to_all x2, blocking collectives: 24.9 us -> 32.5 us  [body(): told = lax.all_to_all(parts, ('row', 'col'), 0, 0)]
    ppermute x6, waiting for transfers between devices: 0.68 us -> 6.13 us  [swapped(): out.append(lax.ppermute(x, axis, pairs))]
  transfers between devices with their start and end apart: 6 -> 6, of which waited for: 1 -> 2; matrix products, arithmetic and copies ran while one was open for 0% -> 0% of each run, Pallas kernels for 7% -> 6%
where the time goes in v7:
time: 69.8 us; the launch traced here: 69.6 us
  blocking collectives  32.5 us (47%)
  Pallas kernels  17.4 us (25%)
  starting transfers between devices  12.8 us (18%)
  waiting for transfers between devices  6.13 us (9%)
  between operations  0.71 us (1%)
    all_to_all x2, blocking collectives, body(): told = lax.all_to_all(parts, ('row', 'col'), 0, 0)  32.5 us
    pallas_call x7, Pallas kernels, call(): pl.pallas_call(kernel, out_shape=shapes, in_specs=in_specs, out_specs=[pl...  17.4 us
    ppermute x6, starting transfers between devices, swapped(): out.append(lax.ppermute(x, axis, pairs))  12.8 us
    ppermute x6, waiting for transfers between devices, swapped(): out.append(lax.ppermute(x, axis, pairs))  6.13 us
  transfers between devices with their start and end apart: 6, of which 2 were waited for; matrix products, arithmetic and copies ran while one was open for 0% of the time, Pallas kernels for 6%

profile of v7, /device:TPU:0, one launch (start us, length us, event | category | flops | bytes accessed | tf_op | source)
XLA Modules:
  0.0 69.6 jit_solution(12340963344988744624)
XLA Ops:
  0.6 1.3 %shard_map.95 = (f32[136,512]{1,0:T(8,128)S(1)}, f32[488,128]{1,0:T(8,128)S(1)}, f32[8,128]{1,0:T(8,128)S(1)}) custom-call(s32[1,2]{1,0:T(1,128)} %bitcast.20, s32[512,128]{1,0:T(8,128)} %bitcast.14, f32[8,128]{1,0:T(8,128)} %bitcast.16, s32[4,128]{1,0:T(4,128)} %bitcast.17, f32[480,128]{1,0:T(8,128)} %bitcast.15, f32[2,128]{1,0:T(2,128)} %bitcast.18, ...), custom_call_target="tpu_custom_call" | custom-call | flops 65536 | bytes 1048576 | tf_op jit(solution)/shard_map/pallas_call | solution.py:44
  2.0 0.7 collective-permute-start.1
  2.7 5.9 %collective-permute-start = (f32[136,512]{1,0:T(8,128)S(1)}, f32[136,512]{1,0:T(8,128)S(1)}, u32[]{:S(2)}, u32[]{:S(2)}) collective-permute-start(f32[136,512]{1,0:T(8,128)S(1)} %get-tuple-element.20.own_ref), channel_id=1, source_target_pairs={{0,4},{4,0},{8,12},{12,8},{1,5},{5,1},{9,13},{13,9},{2,6},{6,2},{1... | collective-permute-start | bytes 835592 | tf_op jit(solution)/shard_map/ppermute | solution.py:30
  8.6 1.4 %shard_map.96 = (f32[136,512]{1,0:T(8,128)S(1)}, f32[136,512]{1,0:T(8,128)S(1)}, f32[136,512]{1,0:T(8,128)S(1)}) custom-call(f32[136,512]{1,0:T(8,128)S(1)} %get-tuple-element.20.own_ref), custom_call_target="tpu_custom_call" | custom-call | flops 23592960 | bytes 1048576 | tf_op jit(solution)/shard_map/pallas_call | solution.py:44
  10.0 0.0 collective-permute-done.1.second_ref
  10.0 5.0 %collective-permute-done.first_ref = f32[136,512]{1,0:T(8,128)S(1)} collective-permute-done((f32[136,512]{1,0:T(8,128)S(1)}, f32[136,512]{1,0:T(8,128)S(1)}, u32[]{:S(2)}, u32[]{:S(2)}) %collective-permute-start) | collective-permute-done | bytes 278560 | tf_op jit(solution)/shard_map/ppermute | solution.py:30
  15.0 2.9 %shard_map.97 = (f32[3,136,512]{2,1,0:T(8,128)S(1)}, f32[3,136,512]{2,1,0:T(8,128)S(1)}, f32[3,136,512]{2,1,0:T(8,128)S(1)}) custom-call(f32[136,512]{1,0:T(8,128)S(1)} %collective-permute-done.first_ref, f32[136,512]{1,0:T(8,128)S(1)} %collective-permute-done.1.second_ref, f32[136,512]{1,0:T(8,128)S(1)} %get-tuple-element.21.own_first, ...), custom_call_target="tpu_custom_call" | custom-call | flops 47185920 | bytes 1048576 | tf_op jit(solution)/shard_map/pallas_call | solution.py:44
  17.8 0.1 collective-permute-start.2
  17.9 0.7 %collective-permute-start.3 = (f32[3,136,512]{2,1,0:T(8,128)S(1)}, f32[3,136,512]{2,1,0:T(8,128)S(1)}, u32[]{:S(2)}, u32[]{:S(2)}) collective-permute-start(f32[3,136,512]{2,1,0:T(8,128)S(1)} %get-tuple-element.26.second_ref), channel_id=1, source_target_pairs={{1,2},{2,1},{5,6},{6,5},{9,10},{10,9},{13,14},{14,13},{17,18},{18,... | collective-permute-start | bytes 2506760 | tf_op jit(solution)/shard_map/ppermute | solution.py:30
  18.6 0.7 collective-permute-start.5
  19.3 4.7 %collective-permute-start.4 = (f32[488,128]{1,0:T(8,128)S(1)}, f32[488,128]{1,0:T(8,128)S(1)}, u32[]{:S(2)}, u32[]{:S(2)}) collective-permute-start(f32[488,128]{1,0:T(8,128)S(1)} %get-tuple-element.27.own_ref), channel_id=1, source_target_pairs={{0,1},{1,0},{2,3},{3,2},{4,5},{5,4},{6,7},{7,6},{8,9},{9,8},{10,11... | collective-permute-start | bytes 749576 | tf_op jit(solution)/shard_map/ppermute | solution.py:30
  24.0 0.0 collective-permute-done.5.second_ref
  24.0 1.1 %collective-permute-done.4.first_ref = f32[488,128]{1,0:T(8,128)S(1)} collective-permute-done((f32[488,128]{1,0:T(8,128)S(1)}, f32[488,128]{1,0:T(8,128)S(1)}, u32[]{:S(2)}, u32[]{:S(2)}) %collective-permute-start.4) | collective-permute-done | bytes 249888 | tf_op jit(solution)/shard_map/ppermute | solution.py:30
  25.2 0.7 %shard_map.98 = (bf16[3,256,512]{2,1,0:T(8,128)(2,1)S(1)}, f32[3,6,128,128]{3,2,1,0:T(8,128)S(1)}) custom-call(f32[488,128]{1,0:T(8,128)S(1)} %collective-permute-done.4.first_ref, f32[488,128]{1,0:T(8,128)S(1)} %get-tuple-element.27.own_ref, f32[488,128]{1,0:T(8,128)S(1)} %collective-permute-done.5.second_ref), custom_call_target="tpu_custom_call" | custom-call | flops 65536 | bytes 1048576 | tf_op jit(solution)/shard_map/pallas_call | solution.py:44
  25.9 2.1 %shard_map.99 = f32[16,16,128]{2,1,0:T(8,128)S(1)} custom-call(f32[3,136,512]{2,1,0:T(8,128)S(1)} %get-tuple-element.24.first_ref, f32[3,136,512]{2,1,0:T(8,128)S(1)} %get-tuple-element.25.mid_ref, f32[3,136,512]{2,1,0:T(8,128)S(1)} %get-tuple-element.26.second_ref, bf16[3,256,512]{2,1,0:T(8,128)(2,1)S(1)} %get-tuple-element.28.ltp_s.ltp_ref, ...), custom_call_target="tpu_custom_call" | custom-call | flops 58982400 | bytes 1048576 | tf_op jit(solution)/shard_map/pallas_call | solution.py:44
  28.0 21.0 %all_to_all.10.told_ref = f32[16,16,128]{2,1,0:T(8,128)S(1)} all-to-all(f32[16,16,128]{2,1,0:T(8,128)S(1)} %shard_map.99), channel_id=1, replica_groups=mesh['groups'=2,'row'=4,'col'=4] {'row','col'}, dimensions={0} | all-to-all | bytes 262144 | tf_op jit(solution)/shard_map/all_to_all | solution.py:605
  49.0 0.0 collective-permute-done.2.first_ref
  49.0 0.0 collective-permute-done.3.second_ref
  49.0 5.8 %shard_map.100 = (f32[3,3,128,512]{3,2,1,0:T(8,128)S(1)}, f32[3,3,4,128]{3,2,1,0:T(4,128)S(1)}, f32[3,3,4,128]{3,2,1,0:T(4,128)S(1)}, f32[16,24,128]{2,1,0:T(8,128)S(1)}, f32[8,128]{1,0:T(8,128)S(1)}) custom-call(f32[3,136,512]{2,1,0:T(8,128)S(1)} %collective-permute-done.2.first_ref, f32[3,136,512]{2,1,0:T(8,128)S(1)} %get-tuple-element.25.mid_ref, ...), custom_call_target="tpu_custom_call" | custom-call | flops 117964800 | bytes 1048576 | tf_op jit(solution)/shard_map/pallas_call | solution.py:44
  54.8 11.6 %all_to_all.11.told_ref = f32[16,24,128]{2,1,0:T(8,128)S(1)} all-to-all(f32[16,24,128]{2,1,0:T(8,128)S(1)} %get-tuple-element.34), channel_id=1, replica_groups=mesh['groups'=2,'row'=4,'col'=4] {'row','col'}, dimensions={0} | all-to-all | bytes 393216 | tf_op jit(solution)/shard_map/all_to_all | solution.py:634
  66.4 3.2 %shard_map.101 = (f32[480,128]{1,0:T(8,128)}, f32[6,1,128]{2,1,0:T(1,128)}) custom-call(f32[3,136,512]{2,1,0:T(8,128)S(1)} %collective-permute-done.2.first_ref, f32[3,136,512]{2,1,0:T(8,128)S(1)} %get-tuple-element.25.mid_ref, f32[3,136,512]{2,1,0:T(8,128)S(1)} %collective-permute-done.3.second_ref, f32[3,3,128,512]{3,2,1,0:T(8,128)S(1)} %get-tuple-element.31.e_ref, ...), custom_call_target="tpu_custom_call" | custom-call | flops 58982400 | bytes 1048576 | tf_op jit(solution)/shard_map/pallas_call | solution.py:44
Async XLA Ops:
  2.0 8.0 %collective-permute-start.1 = (f32[136,512]{1,0:T(8,128)S(1)}, f32[136,512]{1,0:T(8,128)S(1)}, u32[]{:S(2)}, u32[]{:S(2)}) collective-permute-start(f32[136,512]{1,0:T(8,128)S(1)} %get-tuple-element.20.own_ref), channel_id=1, source_target_pairs={{4,8},{8,4},{5,9},{9,5},{6,10},{10,6},{7,11},{11,7},{20,24},{24,20... | collective-permute-start | bytes 835592 | tf_op jit(solution)/shard_map/ppermute | solution.py:30
  2.7 12.3 %collective-permute-start = (f32[136,512]{1,0:T(8,128)S(1)}, f32[136,512]{1,0:T(8,128)S(1)}, u32[]{:S(2)}, u32[]{:S(2)}) collective-permute-start(f32[136,512]{1,0:T(8,128)S(1)} %get-tuple-element.20.own_ref), channel_id=1, source_target_pairs={{0,4},{4,0},{8,12},{12,8},{1,5},{5,1},{9,13},{13,9},{2,6},{6,2},{1... | collective-permute-start | bytes 835592 | tf_op jit(solution)/shard_map/ppermute | solution.py:30
  17.8 31.2 %collective-permute-start.2 = (f32[3,136,512]{2,1,0:T(8,128)S(1)}, f32[3,136,512]{2,1,0:T(8,128)S(1)}, u32[]{:S(2)}, u32[]{:S(2)}) collective-permute-start(f32[3,136,512]{2,1,0:T(8,128)S(1)} %get-tuple-element.24.first_ref), channel_id=1, source_target_pairs={{0,1},{1,0},{2,3},{3,2},{4,5},{5,4},{6,7},{7,6},{8,9},{9,8},{10,11... | collective-permute-start | bytes 2506760 | tf_op jit(solution)/shard_map/ppermute | solution.py:30
  17.9 31.1 %collective-permute-start.3 = (f32[3,136,512]{2,1,0:T(8,128)S(1)}, f32[3,136,512]{2,1,0:T(8,128)S(1)}, u32[]{:S(2)}, u32[]{:S(2)}) collective-permute-start(f32[3,136,512]{2,1,0:T(8,128)S(1)} %get-tuple-element.26.second_ref), channel_id=1, source_target_pairs={{1,2},{2,1},{5,6},{6,5},{9,10},{10,9},{13,14},{14,13},{17,18},{18,... | collective-permute-start | bytes 2506760 | tf_op jit(solution)/shard_map/ppermute | solution.py:30
  18.6 5.4 %collective-permute-start.5 = (f32[488,128]{1,0:T(8,128)S(1)}, f32[488,128]{1,0:T(8,128)S(1)}, u32[]{:S(2)}, u32[]{:S(2)}) collective-permute-start(f32[488,128]{1,0:T(8,128)S(1)} %get-tuple-element.27.own_ref), channel_id=1, source_target_pairs={{1,2},{2,1},{5,6},{6,5},{9,10},{10,9},{13,14},{14,13},{17,18},{18,... | collective-permute-start | bytes 749576 | tf_op jit(solution)/shard_map/ppermute | solution.py:30
  19.3 5.9 %collective-permute-start.4 = (f32[488,128]{1,0:T(8,128)S(1)}, f32[488,128]{1,0:T(8,128)S(1)}, u32[]{:S(2)}, u32[]{:S(2)}) collective-permute-start(f32[488,128]{1,0:T(8,128)S(1)} %get-tuple-element.27.own_ref), channel_id=1, source_target_pairs={{0,1},{1,0},{2,3},{3,2},{4,5},{5,4},{6,7},{7,6},{8,9},{9,8},{10,11... | collective-permute-start | bytes 749576 | tf_op jit(solution)/shard_map/ppermute | solution.py:30
